TPU v7x, 32 devices: a whole 2x2x4 slice. The times are simulated.
32 devices in a mesh: mer: 8 (over z, x), box: 4 (over y, core).
Axes of the slice: x: 2, y: 2, z: 4, core: 2. Of those that a mesh axis runs over, the one named last changes fastest.
Arguments:
- annulus: float32 [25, 512, 1024], P(None, 'box', 'mer'), may hold values from -6 to 6
- annulus_prev: float32 [25, 512, 1024], P(None, 'box', 'mer'), may hold values from -6 to 6
- derivative: float32 [25, 25], replicated, may hold values from -1.25 to 1.25
- radial_modulus: float32 [25, 1024], P(None, 'mer'), may hold values from 0.5 to 2
- shear_modulus: float32 [25, 1024], P(None, 'mer'), may hold values from 0.5 to 2
- node_mass: float32 [25, 1024], P(None, 'mer'), may hold values from 1 to 4
- element_modes: int32 [1024], P('mer'), may hold values from 1 to 256
- upper_rows: int32 [2048], P('mer'), may hold values from 0 to 3199
- lower_rows: int32 [2048], P('mer'), may hold values from 0 to 3199
- coupling_rows: int32 [16384], P('mer'), may hold values from 0 to 3199
- coupling_target: int32 [16384, 1], P('mer'), may hold values from 0 to 31; in each aligned block of 2048 rows (0 to 2047, 2048 to 4095, ...) at most 128 rows name the same one
- box_field: float32 [32768], P(('mer', 'box')), may hold values from -6 to 6
- box_prev: float32 [32768], P(('mer', 'box')), may hold values from -6 to 6
- box_angle: float32 [32768], P(('mer', 'box')), may hold values from -3.140625 to 3.140625
- box_spring: float32 [32768], P(('mer', 'box')), may hold values from 0.5 to 2
- box_mass: float32 [32768], P(('mer', 'box')), may hold values from 1 to 4
- box_weight: float32 [32768], P(('mer', 'box')), may hold values from 0.05 to 0.5
- box_slot: int32 [32768], P(('mer', 'box')), may hold values from 0 to 1023, as said below
Outputs:
- annulus_out: float32 [25, 512, 1024], P(None, 'box', 'mer')
- box_out: float32 [32768], P(('mer', 'box'))
Inputs may be any that keep to these rules, and one draw needn't show every extreme that they name: `lower_rows`: part rows, paired with the previous part's upper rows. `coupling_target`: among the 2048 rows of one part no box part is named more than 128 times, and some box part exactly 128 times. `box_slot`: slot p * 8 + i of the node's box part: the p-th coupling row that part i sends there; slots that no row fills hold zeros. Among the 1024 nodes of one box part, exactly 128 read slots of each meridional part i.
All inputs are finite; a program needn't handle non-finite values.
Results may differ from a plain program's by a relative error of at most 0.0003.
Values sent between devices are 32-bit elements; how exact they have to be, the bound alone decides.
No kernel may reach another device: no remote copies, remote signals or barrier semaphores. Data moves between devices by JAX's collectives and lax.ppermute only.
A program may use at most 128 MiB of HBM per device.

v0:
```python
import jax
import jax.numpy as jnp
from jax import lax
from jax.sharding import PartitionSpec as P

MODES = 256
STEPS = 2


step_scale = 0.25


def padded(value, sides, width):
    for axis, dim in sides:
        size, length = (lax.axis_size(axis), value.shape[dim])
        up = [(i, (i + 1) % size) for i in range(size - 1)]
        down = [(j, i) for i, j in up]
        last = lax.slice_in_dim(value, length - width, length, axis=dim)
        first = lax.slice_in_dim(value, 0, width, axis=dim)
        before = lax.ppermute(last, axis, up)
        after = lax.ppermute(first, axis, down)
        value = jnp.concatenate([before, value, after], axis=dim)
    return value


def column_basis(angles, column, modes):
    order = (column % modes).astype(jnp.float32)
    phase = angles[:, None] * order[None, :]
    return jnp.where(column[None, :] < modes, jnp.cos(phase), jnp.sin(phase))


def annulus_force(values, derivative, radial_modulus, shear_modulus, wavenum):
    node_count, column_count, element_count = values.shape
    flat = values.reshape(node_count, column_count * element_count)
    gradient = jnp.dot(derivative, flat, precision=lax.Precision.HIGHEST)
    gradient = gradient.reshape(node_count, column_count, element_count)
    flux = (radial_modulus[:, None, :] * gradient).reshape(node_count, column_count * element_count)
    backward = jnp.dot(derivative.T, flux, precision=lax.Precision.HIGHEST)
    backward = backward.reshape(node_count, column_count, element_count)
    return -backward - shear_modulus[:, None, :] * wavenum[None, :, None] * values


def per_device(
    annulus,
    annulus_prev,
    derivative,
    radial_modulus,
    shear_modulus,
    node_mass,
    element_modes,
    upper_rows,
    lower_rows,
    coupling_rows,
    coupling_target,
    box_field,
    box_prev,
    box_angle,
    box_spring,
    box_mass,
    box_weight,
    box_slot,
):
    mer_count = lax.axis_size("mer")
    box_count = lax.axis_size("box")
    devices = mer_count * box_count
    node_count, block_columns, element_count = annulus.shape
    coupling_count = coupling_rows.shape[0]
    capacity = max(2, 2 * coupling_count // devices)
    slot_count = capacity * mer_count
    column = lax.axis_index("box") * block_columns + jnp.arange(block_columns, dtype=jnp.int32)
    order = (column % MODES).astype(jnp.float32)
    wavenum = (2.0 * order / MODES) ** 2
    live_mask = ((column % MODES)[:, None] < element_modes[None, :]).astype(jnp.float32)
    upper_node = upper_rows // element_count
    upper_element = upper_rows % element_count
    lower_node = lower_rows // element_count
    lower_element = lower_rows % element_count
    coupled_node = coupling_rows // element_count
    coupled_element = coupling_rows % element_count
    target = coupling_target[:, 0]
    target_hot = (target[:, None] == jnp.arange(devices, dtype=jnp.int32)[None, :]).astype(
        jnp.int32
    )
    position = jnp.sum((jnp.cumsum(target_hot, axis=0) - target_hot) * target_hot, axis=1)
    harmonic = column_basis(box_angle, jnp.arange(2 * MODES, dtype=jnp.int32), MODES)
    slot_hot = (box_slot[:, None] == jnp.arange(slot_count, dtype=jnp.int32)[None, :]).astype(
        jnp.float32
    )
    current = annulus
    previous = annulus_prev
    box_now = box_field
    box_before = box_prev
    for step_index in range(STEPS):
        force = annulus_force(current, derivative, radial_modulus, shear_modulus, wavenum)
        lower_values = force[lower_node, :, lower_element]
        upper_values = force[upper_node, :, upper_element]
        boundary = jnp.stack([lower_values, upper_values], axis=0)
        extended = padded(boundary, (("mer", 0),), 1)
        force = force.at[lower_node, :, lower_element].add(extended[0])
        force = force.at[upper_node, :, upper_element].add(extended[3])
        sent_rows = current[coupled_node, :, coupled_element]
        outgoing = (
            jnp.zeros((capacity, devices, block_columns), jnp.float32)
            .at[position, target]
            .set(sent_rows)
        )
        received = lax.all_to_all(outgoing, ("mer", "box"), split_axis=1, concat_axis=1, tiled=True)
        coefficients = received.reshape(slot_count, box_count * block_columns)
        node_rows = jnp.dot(slot_hot, coefficients, precision=lax.Precision.HIGHEST)
        sample = jnp.sum(node_rows * harmonic, axis=1)
        pull = box_spring * (sample - box_now)
        weighted = (-box_weight * pull)[:, None] * harmonic
        reaction = lax.dot_general(
            slot_hot, weighted, (((0,), (0,)), ((), ())), precision=lax.Precision.HIGHEST
        )
        replies = reaction.reshape(capacity, devices, block_columns)
        returned = lax.all_to_all(replies, ("mer", "box"), split_axis=1, concat_axis=1, tiled=True)
        force = force.at[coupled_node, :, coupled_element].add(returned[position, target])
        annulus_next = (
            2.0 * current
            - previous
            + step_scale * live_mask[None, :, :] * force / node_mass[:, None, :]
        )
        box_next = 2.0 * box_now - box_before + step_scale * pull / box_mass
        previous = current
        current = annulus_next
        box_before = box_now
        box_now = box_next
    return (current, box_now)


def solution(mesh):
    in_specs = (
        P(None, "box", "mer"),
        P(None, "box", "mer"),
        P(),
        P(None, "mer"),
        P(None, "mer"),
        P(None, "mer"),
        P("mer"),
        P("mer"),
        P("mer"),
        P("mer"),
        P("mer", None),
        P(("mer", "box")),
        P(("mer", "box")),
        P(("mer", "box")),
        P(("mer", "box")),
        P(("mer", "box")),
        P(("mer", "box")),
        P(("mer", "box")),
    )
    out_specs = (P(None, "box", "mer"), P(("mer", "box")))
    return jax.shard_map(
        per_device, mesh=mesh, in_specs=in_specs, out_specs=out_specs, check_vma=False
    )
```

profile of v0, /device:TPU:21, one launch (start us, length us, event | category | flops | bytes accessed | tf_op | source)
XLA Modules:
  0.0 478.1 jit_solution(13795776355500408303)
XLA Ops:
  0.7 2.0 copy.60
  2.8 9.1 %reduce-window.6 = s32[32,16,128]{2,1,0:T(8,128)S(1)} reduce-window(s32[32,16,128]{2,1,0:T(8,128)S(1)} %fusion.49, s32[]{:T(128)} %constant.107.clone.1), window={size=1x1x128 pad=0_0x0_0x127_0}, to_apply=%region_2.3 | reduce-window | flops 8323072 | bytes 524292 | tf_op jit(solution)/shard_map/reduce-window
  13.6 18.9 %scatter_custom_fusion.4 = f32[4096,128]{1,0:T(8,128)} fusion(s32[2048]{0:T(1024)S(1)} %broadcast_select_fusion, f32[25,128,128]{1,2,0:T(8,128)S(1)} %copy.60, s32[2048]{0:T(1024)S(1)} %bitcast.144, f32[]{:T(128)} %constant.111.clone.1), kind=kCustom, calls=%fused_computation.55 | custom fusion | bytes 2097156
  32.5 4.1 copy.69
  36.7 6.2 %all-to-all-start = ((f32[128,32,128]{2,0,1:T(8,128)}), f32[128,32,128]{2,0,1:T(8,128)}, u32[]{:S(2)}, u32[]{:S(2)}) async-start(f32[128,32,128]{2,0,1:T(8,128)} %copy.69), calls=%async_computation | async-start | bytes 4194304 | tf_op jit(solution)/shard_map/all_to_all | solution.py:107
  42.9 45.0 %all-to-all-done = f32[128,32,128]{2,0,1:T(8,128)} async-done(((f32[128,32,128]{2,0,1:T(8,128)}), f32[128,32,128]{2,0,1:T(8,128)}, u32[]{:S(2)}, u32[]{:S(2)}) %all-to-all-start) | async-done | bytes 2097184 | tf_op jit(solution)/shard_map/all_to_all | solution.py:107
  87.9 4.1 copy.70
  92.0 3.0 reshape.151
  95.1 12.8 %fusion.13 = f32[1024]{0:T(1024)S(1)} fusion(f32[1024,512]{1,0:T(8,128)} %reshape.151, s32[1024]{0:T(1024)S(1)} %copy-done.32, f32[512]{0:T(512)S(1)} %fusion.53, f32[1024]{0:T(1024)S(1)} %copy-done.34, pred[512]{0:T(512)(128)(4,1)S(1)} %iota_compare_fusion.9), kind=kOutput, calls=%fused_computation.35 | convolution fusion | flops 6445595648 | bytes 2112000 | tf_op jit(solution)/shard_map/dot_general | solution.py:109
  108.5 13.5 %fusion.6 = f32[1024,512]{1,0:T(8,128)} fusion(s32[1024]{0:T(1024)S(1)} %copy-done.32, f32[1024]{0:T(1024)S(1)} %negate_multiply_fusion.1, f32[512]{0:T(512)S(1)} %fusion.53, f32[1024]{0:T(1024)S(1)} %copy-done.34, pred[512]{0:T(512)(128)(4,1)S(1)} %iota_compare_fusion.9), kind=kOutput, calls=%fused_computation.27 | convolution fusion | flops 6446120960 | bytes 2112000 | tf_op jit(solution)/shard_map/dot_general | solution.py:113
  122.0 2.8 reshape.152
  124.8 4.1 copy.71
  128.9 7.8 %all-to-all-start.1 = ((f32[128,32,128]{2,0,1:T(8,128)}), f32[128,32,128]{2,0,1:T(8,128)}, u32[]{:S(2)}, u32[]{:S(2)}) async-start(f32[128,32,128]{2,0,1:T(8,128)} %copy.71), calls=%async_computation.1 | async-start | bytes 4194304 | tf_op jit(solution)/shard_map/all_to_all | solution.py:117
  137.5 2.8 fusion.25
  149.0 2.5 gather_fusion
  151.6 3.5 collective-permute-start
  155.1 2.6 gather_fusion.1
  157.7 3.1 collective-permute-start.1
  160.8 2.7 copy.61
  164.4 23.0 %collective-permute-done = f32[1,256,128]{2,1,0:T(8,128)S(1)} collective-permute-done((f32[1,256,128]{2,1,0:T(8,128)}, f32[1,256,128]{2,1,0:T(8,128)S(1)}, u32[]{:S(2)}, u32[]{:S(2)}) %collective-permute-start) | collective-permute-done | bytes 131104 | tf_op jit(solution)/shard_map/ppermute | solution.py:20
  187.3 12.1 %scatter_fusion = f32[25,128,128]{1,2,0:T(8,128)S(1)} fusion(f32[25,128,128]{1,2,0:T(8,128)S(1)} %fusion.23, s32[256]{0:T(256)S(1)} %bitcast.105, f32[256,128]{1,0:T(8,128)S(1)} %bitcast.126), kind=kCustom, calls=%fused_computation.8 | custom fusion | flops 32768 | bytes 395264 | tf_op jit(solution)/shard_map/scatter-add | solution.py:99
  199.4 16.5 %scatter_fusion.1 = f32[25,128,128]{1,2,0:T(8,128)S(1)} fusion(f32[25,128,128]{1,2,0:T(8,128)S(1)} %scatter_fusion, s32[256]{0:T(256)S(1)} %bitcast.101, f32[256,128]{1,0:T(8,128)} %bitcast.14), kind=kCustom, calls=%fused_computation.9 | custom fusion | flops 32768 | bytes 395264 | tf_op jit(solution)/shard_map/scatter-add | solution.py:100
  216.0 4.1 copy.72
  220.1 23.7 %scatter_custom_fusion.5 = f32[3200,128]{1,0:T(8,128)S(1)} fusion(f32[3200,128]{1,0:T(8,128)S(1)} %bitcast.109, s32[2048]{0:T(1024)} %broadcast_select_fusion.1, f32[128,32,128]{2,1,0:T(8,128)} %copy.72, s32[2048]{0:T(1024)} %bitcast.142), kind=kCustom, calls=%fused_computation.53 | custom fusion | flops 262144 | bytes 1638400
  243.9 3.3 divide_add_fusion.1
  247.1 19.1 %scatter_custom_fusion.6 = f32[4096,128]{1,0:T(8,128)} fusion(s32[2048]{0:T(1024)} %copy-done.18, f32[25,128,128]{1,2,0:T(8,128)} %divide_add_fusion.1, s32[2048]{0:T(1024)} %bitcast.145, f32[]{:T(128)} %constant.111.clone.1), kind=kCustom, calls=%fused_computation.51 | custom fusion | bytes 2097664
  266.2 2.8 copy.77
  269.1 49.2 %all_to_all.20 = f32[128,32,128]{2,0,1:T(8,128)S(1)} all-to-all(f32[128,32,128]{2,0,1:T(8,128)S(1)} %copy.77), channel_id=1, replica_groups=mesh['mer'=8,'box'=4] {'mer','box'}, dimensions={1} | all-to-all | bytes 4194304 | tf_op jit(solution)/shard_map/all_to_all | solution.py:107
  318.3 2.5 copy.78
  320.8 2.9 reshape.154
  323.9 12.8 %fusion.15 = f32[1024]{0:T(1024)S(1)} fusion(f32[1024,512]{1,0:T(8,128)} %reshape.154, s32[1024]{0:T(1024)S(1)} %copy-done.33, f32[512]{0:T(512)S(1)} %copy-done.24, f32[1024]{0:T(1024)S(1)} %copy-done.35, pred[512]{0:T(512)(128)(4,1)S(1)} %copy-done.37), kind=kOutput, calls=%fused_computation.36 | convolution fusion | flops 6445595648 | bytes 2112000 | tf_op jit(solution)/shard_map/dot_general | solution.py:109
  337.3 13.3 %fusion.4 = f32[1024,512]{1,0:T(8,128)} fusion(s32[1024]{0:T(1024)S(1)} %copy-done.33, f32[1024]{0:T(1024)S(1)} %get-tuple-element.11, f32[512]{0:T(512)S(1)} %copy-done.24, f32[1024]{0:T(1024)S(1)} %copy-done.35, pred[512]{0:T(512)(128)(4,1)S(1)} %copy-done.37), kind=kOutput, calls=%fused_computation.26 | convolution fusion | flops 6446120960 | bytes 2112000 | tf_op jit(solution)/shard_map/dot_general | solution.py:113
  350.6 3.0 reshape.155
  353.7 4.1 copy.79
  357.8 7.0 %all-to-all-start.3 = ((f32[128,32,128]{2,0,1:T(8,128)}), f32[128,32,128]{2,0,1:T(8,128)}, u32[]{:S(2)}, u32[]{:S(2)}) async-start(f32[128,32,128]{2,0,1:T(8,128)} %copy.79), calls=%async_computation.3 | async-start | bytes 4194304 | tf_op jit(solution)/shard_map/all_to_all | solution.py:117
  365.1 2.5 copy.89
  378.9 2.5 fusion.24
  381.4 2.5 gather_fusion.2
  384.0 3.3 collective-permute-start.2
  387.2 2.6 gather_fusion.3
  389.8 3.1 collective-permute-start.3
  392.9 22.6 %collective-permute-done.2 = f32[1,256,128]{2,1,0:T(8,128)} collective-permute-done((f32[1,256,128]{2,1,0:T(8,128)}, f32[1,256,128]{2,1,0:T(8,128)}, u32[]{:S(2)}, u32[]{:S(2)}) %collective-permute-start.2) | collective-permute-done | bytes 131104 | tf_op jit(solution)/shard_map/ppermute | solution.py:20
  415.5 16.5 %scatter_fusion.2 = f32[25,128,128]{1,2,0:T(8,128)S(1)} fusion(f32[25,128,128]{1,2,0:T(8,128)S(1)} %fusion.24, s32[256]{0:T(256)S(1)} %bitcast.106, f32[256,128]{1,0:T(8,128)} %bitcast.33), kind=kCustom, calls=%fused_computation.10 | custom fusion | flops 32768 | bytes 395264 | tf_op jit(solution)/shard_map/scatter-add | solution.py:99
  432.0 12.1 %scatter_fusion.3 = f32[25,128,128]{1,2,0:T(8,128)S(1)} fusion(f32[25,128,128]{1,2,0:T(8,128)S(1)} %scatter_fusion.2, s32[256]{0:T(256)S(1)} %bitcast.102, f32[256,128]{1,0:T(8,128)S(1)} %bitcast.129), kind=kCustom, calls=%fused_computation.11 | custom fusion | flops 32768 | bytes 395264 | tf_op jit(solution)/shard_map/scatter-add | solution.py:100
  444.1 4.1 copy.80
  448.3 23.7 %scatter_custom_fusion.7 = f32[3200,128]{1,0:T(8,128)S(1)} fusion(f32[3200,128]{1,0:T(8,128)S(1)} %bitcast.111, s32[2048]{0:T(1024)} %broadcast_select_fusion.1, f32[128,32,128]{2,1,0:T(8,128)} %copy.80, s32[2048]{0:T(1024)} %bitcast.143), kind=kCustom, calls=%fused_computation.49 | custom fusion | flops 262144 | bytes 1638400
  472.0 3.3 divide_add_fusion
  475.3 2.7 copy.81
  (125 shorter events, 24.8 us)
Async XLA Ops:
  0.6 136.3 %copy-start = (f32[25,25]{1,0:T(8,128)S(1)}, f32[25,25]{1,0:T(8,128)}, u32[]{:S(2)}) copy-start(f32[25,25]{1,0:T(8,128)} %param.20) | copy-start | bytes 7504
  0.6 12.7 %copy-start.31 = (s32[2]{0:T(128)S(1)}, s32[2]{0:T(128)}, u32[]{:S(2)}) copy-start(s32[2]{0:T(128)} %constant.122) | copy-start | bytes 28
  0.7 12.8 %copy-start.30 = (s32[2]{0:T(128)S(1)}, s32[2]{0:T(128)}, u32[]{:S(2)}) copy-start(s32[2]{0:T(128)} %constant.119) | copy-start | bytes 28
  0.7 2.0 copy-start.16
  0.7 2.1 copy-start.4
  13.5 23.1 %copy-start.18 = (s32[2048]{0:T(1024)}, s32[2048]{0:T(1024)S(1)}, u32[]{:S(2)}) copy-start(s32[2048]{0:T(1024)S(1)} %broadcast_select_fusion) | copy-start | bytes 24580
  13.6 23.1 %copy-start.17 = (s32[2048,1]{0,1:T(1,128)}, s32[2048,1]{0,1:T(1,128)S(1)}, u32[]{:S(2)}) copy-start(s32[2048,1]{0,1:T(1,128)S(1)} %shift-left_or_fusion.1) | copy-start | bytes 24580
  36.7 51.3 %all-to-all-start = ((f32[128,32,128]{2,0,1:T(8,128)}), f32[128,32,128]{2,0,1:T(8,128)}, u32[]{:S(2)}, u32[]{:S(2)}) async-start(f32[128,32,128]{2,0,1:T(8,128)} %copy.69), calls=%async_computation | async-start | bytes 4194304 | tf_op jit(solution)/shard_map/all_to_all | solution.py:107
  42.9 65.0 %copy-start.36 = (pred[512]{0:T(512)(128)(4,1)}, pred[512]{0:T(512)(128)(4,1)S(1)}, u32[]{:S(2)}) copy-start(pred[512]{0:T(512)(128)(4,1)S(1)} %iota_compare_fusion.9) | copy-start | bytes 1540
  42.9 65.0 %copy-start.23 = (f32[512]{0:T(512)}, f32[512]{0:T(512)S(1)}, u32[]{:S(2)}) copy-start(f32[512]{0:T(512)S(1)} %fusion.53) | copy-start | bytes 6148
  92.0 3.0 copy-start.32
  92.0 3.0 copy-start.34
  95.0 12.8 %copy-start.8 = (f32[1024]{0:T(1024)S(1)}, f32[1024]{0:T(1024)}, u32[]{:S(2)}) copy-start(f32[1024]{0:T(1024)} %param.34) | copy-start | bytes 12292
  95.1 12.8 %copy-start.10 = (f32[1024]{0:T(1024)S(1)}, f32[1024]{0:T(1024)}, u32[]{:S(2)}) copy-start(f32[1024]{0:T(1024)} %param.32) | copy-start | bytes 12292
  95.1 12.8 %copy-start.12 = (f32[1024]{0:T(1024)S(1)}, f32[1024]{0:T(1024)}, u32[]{:S(2)}) copy-start(f32[1024]{0:T(1024)} %param.29) | copy-start | bytes 12292
  107.9 0.6 copy-start.14
  128.9 7.8 %copy-start.3 = (f32[25,128,128]{2,1,0:T(8,128)S(1)}, f32[25,128,128]{2,1,0:T(8,128)}, u32[]{:S(2)}) copy-start(f32[25,128,128]{2,1,0:T(8,128)} %param.18) | copy-start | bytes 4915204
  128.9 87.1 %all-to-all-start.1 = ((f32[128,32,128]{2,0,1:T(8,128)}), f32[128,32,128]{2,0,1:T(8,128)}, u32[]{:S(2)}, u32[]{:S(2)}) async-start(f32[128,32,128]{2,0,1:T(8,128)} %copy.71), calls=%async_computation.1 | async-start | bytes 4194304 | tf_op jit(solution)/shard_map/all_to_all | solution.py:117
  136.8 0.7 copy-start.5
  145.2 1.8 copy-start.25
  145.2 1.8 copy-start.6
  147.0 2.1 copy-start.21
  147.0 8.1 %copy-start.26 = (s32[256]{0:T(256)S(1)}, s32[256]{0:T(256)}, u32[]{:S(2)}) copy-start(s32[256]{0:T(256)} %param.26) | copy-start | bytes 3076
  151.6 35.8 %collective-permute-start = (f32[1,256,128]{2,1,0:T(8,128)}, f32[1,256,128]{2,1,0:T(8,128)S(1)}, u32[]{:S(2)}, u32[]{:S(2)}) collective-permute-start(f32[1,256,128]{2,1,0:T(8,128)} %bitcast.127), channel_id=1, source_target_pairs={{0,4},{4,8},{8,12},{12,16},{16,20},{20,24},{24,28},{1,5},{5,9},{9,... | collective-permute-start | bytes 393224 | tf_op jit(solution)/shard_map/ppermute | solution.py:20
  155.1 8.3 %copy-start.29 = (s32[2]{0:T(128)S(1)}, s32[2]{0:T(128)}, u32[]{:S(2)}) copy-start(s32[2]{0:T(128)} %constant.125) | copy-start | bytes 28
  155.1 8.4 %copy-start.28 = (s32[2]{0:T(128)S(1)}, s32[2]{0:T(128)}, u32[]{:S(2)}) copy-start(s32[2]{0:T(128)} %constant.128) | copy-start | bytes 28
  155.1 8.5 %copy-start.27 = (s32[128]{0:T(128)S(1)}, s32[128]{0:T(128)}, u32[]{:S(2)}) copy-start(s32[128]{0:T(128)} %param.24) | copy-start | bytes 1540
  157.7 41.7 %collective-permute-start.1 = (f32[1,256,128]{2,1,0:T(8,128)}, f32[1,256,128]{2,1,0:T(8,128)}, u32[]{:S(2)}, u32[]{:S(2)}) collective-permute-start(f32[1,256,128]{2,1,0:T(8,128)} %bitcast.128), channel_id=1, source_target_pairs={{4,0},{8,4},{12,8},{16,12},{20,16},{24,20},{28,24},{5,1},{9,5},{13... | collective-permute-start | bytes 393224 | tf_op jit(solution)/shard_map/ppermute | solution.py:21
  216.0 27.9 %copy-start.7 = (f32[25,128]{1,0:T(8,128)S(1)}, f32[25,128]{1,0:T(8,128)}, u32[]{:S(2)}) copy-start(f32[25,128]{1,0:T(8,128)} %param.23) | copy-start | bytes 38404
  320.8 3.0 copy-start.24
  320.8 3.0 copy-start.33
  320.8 3.0 copy-start.35
  320.8 3.0 copy-start.37
  323.8 12.9 %copy-start.9 = (f32[1024]{0:T(1024)S(1)}, f32[1024]{0:T(1024)}, u32[]{:S(2)}) copy-start(f32[1024]{0:T(1024)} %param.34) | copy-start | bytes 12292
  323.8 12.9 %copy-start.11 = (f32[1024]{0:T(1024)S(1)}, f32[1024]{0:T(1024)}, u32[]{:S(2)}) copy-start(f32[1024]{0:T(1024)} %param.32) | copy-start | bytes 12292
  323.8 12.9 %copy-start.13 = (f32[1024]{0:T(1024)S(1)}, f32[1024]{0:T(1024)}, u32[]{:S(2)}) copy-start(f32[1024]{0:T(1024)} %param.29) | copy-start | bytes 12292
  323.8 12.9 %copy-start.15 = (f32[1024]{0:T(1024)S(1)}, f32[1024]{0:T(1024)}, u32[]{:S(2)}) copy-start(f32[1024]{0:T(1024)} %copy-done.14) | copy-start | bytes 12292
  323.8 12.9 %copy-start.19 = (f32[1024]{0:T(1024)S(1)}, f32[1024]{0:T(1024)}, u32[]{:S(2)}) copy-start(f32[1024]{0:T(1024)} %param.33) | copy-start | bytes 12292
  323.8 12.9 %copy-start.20 = (f32[1024]{0:T(1024)S(1)}, f32[1024]{0:T(1024)}, u32[]{:S(2)}) copy-start(f32[1024]{0:T(1024)} %param.30) | copy-start | bytes 12292
  357.8 86.3 %all-to-all-start.3 = ((f32[128,32,128]{2,0,1:T(8,128)}), f32[128,32,128]{2,0,1:T(8,128)}, u32[]{:S(2)}, u32[]{:S(2)}) async-start(f32[128,32,128]{2,0,1:T(8,128)} %copy.79), calls=%async_computation.3 | async-start | bytes 4194304 | tf_op jit(solution)/shard_map/all_to_all | solution.py:117
  365.1 2.5 copy-start.1
  371.1 1.6 copy-start.2
  377.2 1.8 copy-start.22
  384.0 31.5 %collective-permute-start.2 = (f32[1,256,128]{2,1,0:T(8,128)}, f32[1,256,128]{2,1,0:T(8,128)}, u32[]{:S(2)}, u32[]{:S(2)}) collective-permute-start(f32[1,256,128]{2,1,0:T(8,128)} %bitcast.32), channel_id=1, source_target_pairs={{0,4},{4,8},{8,12},{12,16},{16,20},{20,24},{24,28},{1,5},{5,9},{9,... | collective-permute-start | bytes 393224 | tf_op jit(solution)/shard_map/ppermute | solution.py:20
  389.8 42.2 %collective-permute-start.3 = (f32[1,256,128]{2,1,0:T(8,128)}, f32[1,256,128]{2,1,0:T(8,128)S(1)}, u32[]{:S(2)}, u32[]{:S(2)}) collective-permute-start(f32[1,256,128]{2,1,0:T(8,128)} %bitcast.130), channel_id=1, source_target_pairs={{4,0},{8,4},{12,8},{16,12},{20,16},{24,20},{28,24},{5,1},{9,5},{13... | collective-permute-start | bytes 393224 | tf_op jit(solution)/shard_map/ppermute | solution.py:21
where the time goes:
time: 487 us; the launch traced here: 478 us
  other arithmetic  128 us (26%)
  local copies, waits for them, and re-layouts  114 us (23%)
  waiting for transfers between devices  90.6 us (19%)
  matrix products  61.1 us (13%)
  blocking collectives  49.2 us (10%)
  starting transfers between devices  33.9 us (7%)
    unnamed x89, local copies, waits for them, and re-layouts  54.9 us
    all_to_all x1, blocking collectives, per_device(): lax.all_to_all(outgoing, ('mer', 'box'), split_axis=1, concat_axis=1, til...  49.2 us
    unnamed x8, other arithmetic  48.4 us
    ppermute x2, waiting for transfers between devices, padded(): before = lax.ppermute(last, axis, up)  45.6 us
    all_to_all x1, waiting for transfers between devices, per_device(): lax.all_to_all(outgoing, ('mer', 'box'), split_axis=1, concat_axis=1, til...  45 us
    scatter-add x2, other arithmetic, per_device(): force = force.at[upper_node, :, upper_element].add(extended[3])  28.6 us
    scatter-add x2, other arithmetic, per_device(): force = force.at[lower_node, :, lower_element].add(extended[0])  28.6 us
    dot_general x2, matrix products, per_device(): lax.dot_general(slot_hot, weighted, (((0,), (0,)), ((), ())), precision=l...  26.8 us
  transfers between devices with their start and end apart: 7, of which 3 were waited for; matrix products, arithmetic and copies ran while one was open for 21% of the time, Pallas kernels for 0%

commit v1 on v0

v1 whole, which is shorter than its diff:
```python
import functools

import jax
import jax.numpy as jnp
from jax import lax
from jax.experimental import pallas as pl
from jax.experimental.pallas import tpu as pltpu
from jax.sharding import PartitionSpec as P

MODES = 256
STEPS = 2
LANES = 128
WIDE = 256

step_scale = 0.25
f32 = jnp.float32
bf16 = jnp.bfloat16
i32 = jnp.int32


def iota(shape, dim):
    return lax.broadcasted_iota(i32, shape, dim)


def dot(a, b):
    return lax.dot_general(a, b, (((1,), (0,)), ((), ())), preferred_element_type=f32)


def dot_nt(a, b):
    return lax.dot_general(a, b, (((1,), (1,)), ((), ())), preferred_element_type=f32)


def hot(mask):
    return jnp.where(mask, 1.0, 0.0).astype(bf16)


def split(x):
    high = x.astype(bf16)
    return high, (x - high.astype(f32)).astype(bf16)


def stacked(x):
    high, low = split(x)
    return jnp.concatenate([high, low], axis=0)


def folded(x):
    half = x.shape[0] // 2
    return x[:half] + x[half:]


def running(mask):
    rows, width = mask.shape
    below = hot(iota((LANES, LANES), 0) < iota((LANES, LANES), 1))
    total = jnp.zeros((rows, 1), f32)
    counts = []
    for start in range(0, width, LANES):
        block = mask[:, start : start + LANES]
        counts.append(dot(block.astype(bf16), below) + total)
        total = total + jnp.sum(block, axis=1, keepdims=True)
    return jnp.concatenate(counts, axis=1), total


def group_kernel(parts, copies, slot_ref, *refs):
    fields, (out_ref, dest_ref, stack_ref) = refs[:6], refs[6:]
    nodes = slot_ref.shape[1]
    per = nodes // parts
    slot = slot_ref[...].astype(f32)
    place = jnp.floor((slot + 0.5) * (1.0 / parts))
    part = slot - place * parts
    rows = max(16, parts)
    mask = jnp.where(iota((rows, nodes), 0) == part.astype(i32), 1.0, 0.0)
    count, _ = running(mask)
    dest = (part * per + jnp.sum(mask * count, axis=0, keepdims=True)).astype(i32)
    dest_ref[...] = dest
    stack_ref[...] = jnp.zeros_like(stack_ref)
    stack_ref[0:1, :] = place
    for index, field in enumerate(fields):
        stack_ref[index + 1 : index + 2, :] = field[...]
    values = stack_ref[...]
    first = values.astype(bf16).astype(f32)
    second = (values - first).astype(bf16).astype(f32)
    third = values - first - second
    terms = jnp.concatenate([first, second, third, jnp.zeros_like(third)], axis=0).astype(bf16)
    for start in range(0, nodes, WIDE):
        moved = dot_nt(terms, hot(iota((WIDE, nodes), 0) + start == dest))
        moved = moved[0:8] + moved[8:16] + moved[16:24]
        for lane in range(0, WIDE, per):
            for copy in range(copies):
                out_ref[(start + lane) // per * copies + copy] = moved[:, lane : lane + per]


def ungroup_kernel(dest_ref, value_ref, out_ref):
    nodes = dest_ref.shape[1]
    values = value_ref[...]
    first = values.astype(bf16).astype(f32)
    second = (values - first).astype(bf16).astype(f32)
    third = values - first - second
    terms = jnp.concatenate(
        [first, second, third, jnp.zeros((13, nodes), f32)], axis=0
    ).astype(bf16)
    dest = dest_ref[...]
    for start in range(0, nodes, WIDE):
        back = dot(terms, hot(iota((nodes, WIDE), 0) == dest[:, start : start + WIDE]))
        out_ref[:, start : start + WIDE] = back[0:1] + back[1:2] + back[2:3]


def rows_kernel(
    elements, target_ref, rows_ref, lower_ref, upper_ref, key_ref, keycol_ref, off_ref, cnt_ref, win_ref
):
    blocks = off_ref.shape[0]
    count = target_ref.shape[1]
    shared = lower_ref.shape[1]
    mask = jnp.where(iota((blocks, count), 0) == target_ref[...], 1.0, 0.0)
    before, total = running(mask)
    totals = jnp.broadcast_to(total, (blocks, LANES))
    offset = dot(hot(iota((blocks, blocks), 1) < iota((blocks, blocks), 0)), totals.astype(bf16))
    off_ref[...] = offset
    cnt_ref[...] = totals
    window = jnp.floor(offset * (1.0 / LANES)) * LANES
    win_ref[...] = jnp.minimum(window, count - WIDE).astype(i32)
    place = jnp.sum(mask * (before + offset[:, 0:1]), axis=0, keepdims=True).astype(i32)
    row = rows_ref[...].astype(f32)
    node = jnp.floor((row + 0.5) * (1.0 / elements))
    terms = jnp.concatenate(
        [node, row - node * elements, jnp.zeros((14, count), f32)], axis=0
    ).astype(bf16)
    for start in range(0, count, WIDE):
        moved = dot_nt(terms, hot(iota((WIDE, count), 0) + start == place))
        key_ref[:, start : start + WIDE] = (moved[0:1] * elements + moved[1:2]).astype(i32)
    key_ref[:, count : count + shared] = lower_ref[...]
    key_ref[:, count + shared : count + 2 * shared] = upper_ref[...]
    for start in range(0, count + 2 * shared, LANES):
        block = jnp.broadcast_to(key_ref[:, start : start + LANES].astype(f32), (LANES, LANES))
        keycol_ref[start : start + LANES, :] = block.T.astype(i32)


def fill_stack(value_ref, stack_ref):
    nodes, columns, elements = value_ref.shape
    for node in range(nodes):
        high, low = split(value_ref[node])
        lanes = slice(node * elements, (node + 1) * elements)
        stack_ref[0:columns, lanes] = high
        stack_ref[columns:, lanes] = low
    if stack_ref.shape[1] > nodes * elements:
        tail = slice(nodes * elements, stack_ref.shape[1])
        stack_ref[:, tail] = jnp.zeros_like(stack_ref[:, tail])


def picked(stack_ref, hot_ref, key_ref, start):
    depth = stack_ref.shape[1]
    key = key_ref[:, pl.ds(start, WIDE)]
    base = iota((LANES, WIDE), 0)
    for row in range(0, depth, LANES):
        hot_ref[row : row + LANES, :] = hot(base == key - row)
    return dot(stack_ref[...], hot_ref[0:depth, :])


def pick_rows(stack_ref, hot_ref, key_ref, out_ref):
    def body(index, carry):
        start = pl.multiple_of(index * WIDE, WIDE)
        out_ref[:, pl.ds(start, WIDE)] = picked(stack_ref, hot_ref, key_ref, start).astype(bf16)
        return carry

    lax.fori_loop(0, out_ref.shape[1] // WIDE, body, 0)


def pick_boundary(stack_ref, hot_ref, key_ref, low_ref, high_ref):
    shared = low_ref.shape[1]
    first = key_ref.shape[1] - 2 * shared
    for ref, origin in ((low_ref, first), (high_ref, first + shared)):
        for start in range(0, shared, WIDE):
            ref[:, start : start + WIDE] = folded(
                picked(stack_ref, hot_ref, key_ref, origin + start)
            )


def spread(derivative_ref, transposed, rows):
    nodes = derivative_ref.shape[0]
    size = 8 * nodes
    left = jnp.where(iota((rows, nodes), 0) // 8 == iota((rows, nodes), 1), 1.0, 0.0)
    right = jnp.where(iota((nodes, size), 1) // 8 == iota((nodes, size), 0), 1.0, 0.0)
    dims = (((1,), (1,)), ((), ())) if transposed else (((1,), (0,)), ((), ()))
    half = lax.dot_general(
        left, derivative_ref[...], dims, precision=lax.Precision.HIGHEST, preferred_element_type=f32
    )
    full = jnp.dot(half, right, precision=lax.Precision.HIGHEST, preferred_element_type=f32)
    full = jnp.where(iota((rows, size), 0) % 8 == iota((rows, size), 1) % 8, full, 0.0)
    return stacked(full)


def force_into(value_ref, derivative_ref, radial_ref, shear_ref, first_order, force_ref):
    nodes, columns, elements = value_ref.shape
    size = 8 * nodes
    rows = -(-size // 16) * 16
    forward = spread(derivative_ref, False, rows)
    backward = spread(derivative_ref, True, rows)
    radial = jnp.broadcast_to(radial_ref[...][:, None, :], (nodes, 8, elements)).reshape(
        size, elements
    )
    radial = jnp.concatenate([radial, radial], axis=1)
    shear = jnp.broadcast_to(shear_ref[...][:, None, :], (nodes, 8, elements))

    def applied(matrix, x):
        high, low = split(x)
        both = dot(matrix, high)
        return both[:size] + both[rows : rows + size] + dot(matrix[:rows], low)[:size]

    def body(index, carry):
        start = pl.multiple_of(index * 16, 16)
        halves = [value_ref[:, pl.ds(start, 8), :], value_ref[:, pl.ds(start + 8, 8), :]]
        x = jnp.concatenate([half.reshape(size, elements) for half in halves], axis=1)
        back = applied(backward, radial * applied(forward, x))
        for side, half in enumerate(halves):
            order = (first_order + start + 8 * side + iota((8, elements), 0)).astype(f32)
            wave = (2.0 * order / MODES) ** 2
            block = back[:, side * elements : (side + 1) * elements].reshape(nodes, 8, elements)
            force_ref[:, pl.ds(start + 8 * side, 8), :] = -block - shear * wave[None] * half
        return carry

    lax.fori_loop(0, columns // 16, body, 0)


def start_kernel(
    box_ref, value_ref, derivative_ref, radial_ref, shear_ref, key_ref,
    force_ref, low_ref, high_ref, picked_ref, stack_ref, hot_ref,
):
    columns = value_ref.shape[1]
    force_into(
        value_ref, derivative_ref, radial_ref, shear_ref, box_ref[0] * columns % MODES, force_ref
    )
    fill_stack(force_ref, stack_ref)
    pick_boundary(stack_ref, hot_ref, key_ref, low_ref, high_ref)
    fill_stack(value_ref, stack_ref)
    pick_rows(stack_ref, hot_ref, key_ref, picked_ref)


def window_hot(win_ref, place_ref, group, stride):
    window = pl.multiple_of(win_ref[group * stride, 0], LANES)
    place = place_ref[pl.ds(group, 1), :]
    return window, hot(iota((WIDE, LANES), 0) + window == place)


def sample_into(win_ref, place_ref, harmonic_ref, picked_ref, stride, sample_ref):
    def body(group, carry):
        window, chosen = window_hot(win_ref, place_ref, group, stride)
        rows = folded(dot(picked_ref[:, pl.ds(window, WIDE)], chosen))
        sample_ref[pl.ds(group, 1), :] = jnp.sum(
            rows * harmonic_ref[group], axis=0, keepdims=True
        )
        return carry

    lax.fori_loop(0, sample_ref.shape[0], body, 0)


def node_kernel(
    stride, box_ref, win_ref, message_ref, off_ref, cnt_ref, picked_ref,
    harmonic_ref, place_ref, node_ref, sample_ref,
    near_re, near_im, far_re, far_im,
):
    groups, columns, _ = harmonic_ref.shape
    place = message_ref[:, 0, :]
    angle = message_ref[:, 1, :]
    place_ref[...] = jnp.where(place < cnt_ref[...], off_ref[...] + place, -1.0).astype(i32)
    for index in range(5):
        node_ref[index] = message_ref[:, 2 + index, :]

    def power(order):
        return jnp.cos(order * angle), jnp.sin(order * angle)

    def times(x, y):
        return x[0] * y[0] - x[1] * y[1], x[0] * y[1] + x[1] * y[0]

    near = [(jnp.ones_like(angle), jnp.zeros_like(angle))] + [None] * 7
    for bit in (1, 2, 4):
        factor = power(float(bit))
        near[bit] = factor
        for low in range(1, bit):
            near[bit + low] = times(factor, near[low])
    for index, (re, im) in enumerate(near):
        near_re[:, index, :] = re
        near_im[:, index, :] = im
    first = box_ref[0] * columns
    base_re, base_im = power((first % MODES).astype(f32))
    sine = first >= MODES
    far = [
        (jnp.where(sine, base_im, base_re), jnp.where(sine, -base_re, base_im))
    ] + [None] * (columns // 8 - 1)
    bit = 1
    while bit < columns // 8:
        factor = power(float(8 * bit))
        for low in range(min(bit, columns // 8 - bit)):
            far[bit + low] = times(factor, far[low])
        bit *= 2
    for index, (re, im) in enumerate(far):
        far_re[index] = re
        far_im[index] = im

    def body(group, carry):
        re, im = near_re[group], near_im[group]
        for index in range(columns // 8):
            harmonic_ref[group, 8 * index : 8 * index + 8, :] = (
                far_re[index, pl.ds(group, 1), :] * re - far_im[index, pl.ds(group, 1), :] * im
            )
        return carry

    lax.fori_loop(0, groups, body, 0)
    sample_into(win_ref, place_ref, harmonic_ref, picked_ref, stride, sample_ref)


def nodes_step(samples_ref, node_ref, now, before, next_ref, coefficient_ref):
    sample = samples_ref[0]
    for index in range(1, samples_ref.shape[0]):
        sample = sample + samples_ref[index]
    pull = node_ref[0] * (sample - now)
    next_ref[...] = 2.0 * now - before + step_scale * pull / node_ref[1]
    coefficient_ref[...] = -node_ref[2] * pull


def annulus_step(
    stride, first_order, win_ref, place_ref, harmonic_ref, coefficient_ref, keycol_ref,
    below_ref, above_ref, value_ref, previous_ref, force_ref, mass_ref, modes_ref,
    next_ref, reaction_ref, terms_ref, hot_ref, added_ref,
):
    nodes, columns, elements = value_ref.shape
    groups = place_ref.shape[0]
    count = reaction_ref.shape[1]
    shared = below_ref.shape[1]
    reaction_ref[...] = jnp.zeros_like(reaction_ref)

    def react(group, carry):
        window, chosen = window_hot(win_ref, place_ref, group, stride)
        weighted = harmonic_ref[group] * coefficient_ref[pl.ds(group, 1), :]
        rows = folded(dot_nt(stacked(weighted), chosen))
        reaction_ref[:, pl.ds(window, WIDE)] = reaction_ref[:, pl.ds(window, WIDE)] + rows
        return carry

    lax.fori_loop(0, groups, react, 0)
    terms_ref[:, 0:count] = stacked(reaction_ref[...])
    terms_ref[:, count : count + shared] = stacked(below_ref[...])
    terms_ref[:, count + shared : count + 2 * shared] = stacked(above_ref[...])
    depth = count + 2 * shared
    lane = iota((LANES, LANES), 1)

    def place_rows(pair, carry):
        for side in range(2):
            base = lane + (2 * pair + side) * elements
            for row in range(0, depth, LANES):
                hot_ref[row : row + LANES, side * LANES : (side + 1) * LANES] = hot(
                    keycol_ref[row : row + LANES, :] == base
                )
        rows = folded(dot(terms_ref[...], hot_ref[0:depth, :]))
        added_ref[2 * pair] = rows[:, 0:LANES]
        added_ref[2 * pair + 1] = rows[:, LANES:]
        return carry

    lax.fori_loop(0, added_ref.shape[0] // 2, place_rows, 0)
    order = first_order + iota((columns, elements), 0)
    live = jnp.where(order < modes_ref[...], step_scale, 0.0)
    for node in range(nodes):
        gain = live / mass_ref[node : node + 1, :]
        next_ref[node] = (
            2.0 * value_ref[node]
            - previous_ref[node]
            + gain * (force_ref[node] + added_ref[node])
        )


def middle_kernel(
    stride, box_ref, win_ref, samples_ref, node_ref, place_ref, harmonic_ref, keycol_ref, key_ref,
    below_ref, above_ref, value_ref, previous_ref, force_ref, mass_ref, modes_ref,
    derivative_ref, radial_ref, shear_ref,
    next_ref, nextforce_ref, low_ref, high_ref, sample_ref, boxnext_ref,
    coefficient_ref, reaction_ref, terms_ref, hot_ref, added_ref, stack_ref, picked_ref,
):
    columns = value_ref.shape[1]
    first_order = box_ref[0] * columns % MODES
    nodes_step(samples_ref, node_ref, node_ref[3], node_ref[4], boxnext_ref, coefficient_ref)
    annulus_step(
        stride, first_order, win_ref, place_ref, harmonic_ref, coefficient_ref, keycol_ref,
        below_ref, above_ref, value_ref, previous_ref, force_ref, mass_ref, modes_ref,
        next_ref, reaction_ref, terms_ref, hot_ref, added_ref,
    )
    force_into(next_ref, derivative_ref, radial_ref, shear_ref, first_order, nextforce_ref)
    fill_stack(nextforce_ref, stack_ref)
    pick_boundary(stack_ref, hot_ref, key_ref, low_ref, high_ref)
    fill_stack(next_ref, stack_ref)
    pick_rows(stack_ref, hot_ref, key_ref, picked_ref)
    sample_into(win_ref, place_ref, harmonic_ref, picked_ref, stride, sample_ref)


def box_kernel(samples_ref, node_ref, now_ref, boxnext_ref, coefficient_ref):
    nodes_step(samples_ref, node_ref, now_ref[...], node_ref[3], boxnext_ref, coefficient_ref)


def last_kernel(
    stride, box_ref, win_ref, coefficient_ref, place_ref, harmonic_ref, keycol_ref,
    below_ref, above_ref, value_ref, previous_ref, force_ref, mass_ref, modes_ref,
    next_ref, reaction_ref, terms_ref, hot_ref, added_ref,
):
    first_order = box_ref[0] * value_ref.shape[1] % MODES
    annulus_step(
        stride, first_order, win_ref, place_ref, harmonic_ref, coefficient_ref, keycol_ref,
        below_ref, above_ref, value_ref, previous_ref, force_ref, mass_ref, modes_ref,
        next_ref, reaction_ref, terms_ref, hot_ref, added_ref,
    )


def call(kernel, ins, outs, scratch=(), scalars=0, name=None):
    smem = pl.BlockSpec(memory_space=pltpu.SMEM)
    vmem = pl.BlockSpec(memory_space=pltpu.VMEM)
    return pl.pallas_call(
        kernel,
        out_shape=[jax.ShapeDtypeStruct(shape, dtype) for shape, dtype in outs],
        in_specs=[smem] * scalars + [vmem] * (len(ins) - scalars),
        out_specs=[vmem] * len(outs),
        scratch_shapes=[pltpu.VMEM(shape, dtype) for shape, dtype in scratch],
        name=name,
    )(*ins)


def exchanged(low, high):
    size = lax.axis_size("mer")
    up = [(i, i + 1) for i in range(size - 1)]
    down = [(j, i) for i, j in up]
    return lax.ppermute(high, "mer", up), lax.ppermute(low, "mer", down)


def per_device(
    annulus,
    annulus_prev,
    derivative,
    radial_modulus,
    shear_modulus,
    node_mass,
    element_modes,
    upper_rows,
    lower_rows,
    coupling_rows,
    coupling_target,
    box_field,
    box_prev,
    box_angle,
    box_spring,
    box_mass,
    box_weight,
    box_slot,
):
    mer_count = lax.axis_size("mer")
    box_count = lax.axis_size("box")
    blocks = mer_count * box_count
    nodes, columns, elements = annulus.shape
    box_nodes = box_slot.shape[0]
    per = box_nodes // mer_count
    stride = LANES // per
    groups = blocks * per // LANES
    count = coupling_rows.shape[0]
    shared = upper_rows.shape[0]
    depth = count + 2 * shared
    padded_nodes = nodes + nodes % 2
    field = ((nodes, columns, elements), f32)
    side = ((columns, shared), f32)
    grid = ((groups, LANES), f32)
    hot_scratch = ((max(padded_nodes * elements, depth), WIDE), bf16)
    stack_scratch = ((2 * columns, padded_nodes * elements), bf16)
    picked_shape = ((2 * columns, count), bf16)
    box = jnp.full((1,), lax.axis_index("box"), i32)
    modes = element_modes.reshape(1, elements)

    sent = [
        value.reshape(1, box_nodes)
        for value in (box_slot, box_angle, box_spring, box_mass, box_weight, box_field, box_prev)
    ]
    messages, dest = call(
        functools.partial(group_kernel, mer_count, box_count),
        sent,
        [((blocks, 8, per), f32), ((1, box_nodes), i32)],
        [((8, box_nodes), f32)],
        name="group",
    )
    messages = lax.all_to_all(messages, ("mer", "box"), split_axis=0, concat_axis=0, tiled=True)
    if stride > 1:
        messages = messages.reshape(groups, stride, 8, per).swapaxes(1, 2)
        messages = messages.reshape(groups, 8, LANES)

    key, keycol, offset, filled, window = call(
        functools.partial(rows_kernel, elements),
        [
            coupling_target.reshape(1, count),
            coupling_rows.reshape(1, count),
            lower_rows.reshape(1, shared),
            upper_rows.reshape(1, shared),
        ],
        [
            ((1, depth), i32),
            ((depth, LANES), i32),
            ((blocks, LANES), f32),
            ((blocks, LANES), f32),
            ((blocks, LANES), i32),
        ],
        name="rows",
    )
    if stride > 1:
        offset = jnp.repeat(offset[:, 0], per).reshape(groups, LANES)
        filled = jnp.repeat(filled[:, 0], per).reshape(groups, LANES)

    force, low, high, chosen = call(
        start_kernel,
        [box, annulus, derivative, radial_modulus, shear_modulus, key],
        [field, side, side, picked_shape],
        [stack_scratch, hot_scratch],
        scalars=1,
        name="start",
    )
    below, above = exchanged(low, high)

    harmonic, place, node, sample = call(
        functools.partial(node_kernel, stride),
        [box, window, messages, offset, filled, chosen],
        [((groups, columns, LANES), f32), ((groups, LANES), i32), ((5, groups, LANES), f32), grid],
        [((groups, 8, LANES), f32)] * 2 + [((columns // 8, groups, LANES), f32)] * 2,
        scalars=2,
        name="nodes",
    )
    samples = lax.all_gather(sample, "box")

    step_scratch = [
        ((columns, count), f32),
        ((2 * columns, depth), bf16),
        hot_scratch,
        ((padded_nodes, columns, elements), f32),
    ]
    current, force, low, high, sample, box_now = call(
        functools.partial(middle_kernel, stride),
        [
            box, window, samples, node, place, harmonic, keycol, key, below, above, annulus,
            annulus_prev, force, node_mass, modes, derivative, radial_modulus, shear_modulus,
        ],
        [field, field, side, side, grid, grid],
        [grid] + step_scratch + [stack_scratch, picked_shape],
        scalars=2,
        name="middle",
    )
    below, above = exchanged(low, high)
    samples = lax.all_gather(sample, "box")

    box_now, coefficient = call(box_kernel, [samples, node, box_now], [grid, grid], name="box")
    returned = lax.all_to_all(
        box_now.reshape(mer_count, box_count, per), "mer", split_axis=0, concat_axis=0, tiled=True
    )
    returned = lax.dynamic_index_in_dim(
        returned, lax.axis_index("box"), axis=1, keepdims=False
    )
    (box_out,) = call(
        ungroup_kernel, [dest, returned.reshape(1, box_nodes)], [((1, box_nodes), f32)], name="ungroup"
    )
    (current,) = call(
        functools.partial(last_kernel, stride),
        [
            box, window, coefficient, place, harmonic, keycol, below, above, current, annulus,
            force, node_mass, modes,
        ],
        [field],
        step_scratch,
        scalars=2,
        name="last",
    )
    return current, box_out.reshape(box_nodes)


def solution(mesh):
    in_specs = (
        P(None, "box", "mer"),
        P(None, "box", "mer"),
        P(),
        P(None, "mer"),
        P(None, "mer"),
        P(None, "mer"),
        P("mer"),
        P("mer"),
        P("mer"),
        P("mer"),
        P("mer", None),
        P(("mer", "box")),
        P(("mer", "box")),
        P(("mer", "box")),
        P(("mer", "box")),
        P(("mer", "box")),
        P(("mer", "box")),
        P(("mer", "box")),
    )
    out_specs = (P(None, "box", "mer"), P(("mer", "box")))
    return jax.shard_map(
        per_device, mesh=mesh, in_specs=in_specs, out_specs=out_specs, check_vma=False
    )
```

time: 487 us -> 142 us (0.29)
  the two profiles are of different devices: /device:TPU:21 before, /device:TPU:0 now
where the time goes in v1:
time: 142 us; the launch traced here: 141 us
  Pallas kernels  97.2 us (68%)
  starting transfers between devices  24.1 us (17%)
  blocking collectives  12.8 us (9%)
  waiting for transfers between devices  3.44 us (2%)
  local copies, waits for them, and re-layouts  2.59 us (2%)
    pallas_call x8, Pallas kernels, call(): pl.pallas_call(kernel, out_shape=[jax.ShapeDtypeStruct(shape, dtype) for...  97.2 us
    all_gather x2, blocking collectives, per_device(): samples = lax.all_gather(sample, 'box')  12.8 us
    ppermute x4, starting transfers between devices, exchanged(): return (lax.ppermute(high, 'mer', up), lax.ppermute(low, 'mer', down))  10.2 us
    all_to_all x1, starting transfers between devices, per_device(): lax.all_to_all(messages, ('mer', 'box'), split_axis=0, concat_axis=0, til...  7.33 us
    all_to_all x1, starting transfers between devices, per_device(): lax.all_to_all(box_now.reshape(mer_count, box_count, per), 'mer', split_a...  6.61 us
  transfers between devices with their start and end apart: 6, of which 2 were waited for; matrix products, arithmetic and copies ran while one was open for 0% of the time, Pallas kernels for 25%

profile of v1, /device:TPU:0, one launch (start us, length us, event | category | flops | bytes accessed | tf_op | source)
XLA Modules:
  0.0 140.8 jit_solution(18410424842748281951)
XLA Ops:
  0.6 2.4 %group.1 = (f32[32,8,128]{2,1,0:T(8,128)}, s32[1,1024]{1,0:T(1,128)}) custom-call(s32[1,1024]{1,0:T(1,128)} %bitcast.24, f32[1,1024]{1,0:T(1,128)} %bitcast.25, f32[1,1024]{1,0:T(1,128)} %bitcast.26, f32[1,1024]{1,0:T(1,128)} %bitcast.27, f32[1,1024]{1,0:T(1,128)} %bitcast.28, f32[1,1024]{1,0:T(1,128)} %bitcast.29, f32[1,1024]{1,0:T(1,128)} %bitcast.30), custom_call_target="tpu_custom_call" | custom-call | tf_op jit(solution)/shard_map/group/pallas_call | solution.py:412
  3.0 7.3 %all-to-all-start = ((f32[32,8,128]{2,1,0:T(8,128)}), f32[32,8,128]{2,1,0:T(8,128)S(1)}, u32[]{:S(2)}, u32[]{:S(2)}) async-start(f32[32,8,128]{2,1,0:T(8,128)} %get-tuple-element.26), calls=%async_computation | async-start | bytes 262144 | tf_op jit(solution)/shard_map/all_to_all | solution.py:481
  10.4 4.7 %rows.1 = (s32[1,2560]{1,0:T(1,128)}, s32[2560,128]{1,0:T(8,128)}, f32[32,128]{1,0:T(8,128)}, f32[32,128]{1,0:T(8,128)}, s32[32,128]{1,0:T(8,128)}) custom-call(s32[1,2048]{1,0:T(1,128)} %bitcast.22, s32[1,2048]{1,0:T(1,128)} %bitcast.23, s32[1,256]{1,0:T(1,128)} %bitcast.34, s32[1,256]{1,0:T(1,128)} %bitcast.35), custom_call_target="tpu_custom_call" | custom-call | tf_op jit(solution)/shard_map/rows/pallas_call | solution.py:412
  15.0 14.8 %start.1 = (f32[25,128,128]{2,1,0:T(8,128)}, f32[128,256]{1,0:T(8,128)}, f32[128,256]{1,0:T(8,128)}, bf16[256,2048]{1,0:T(8,128)(2,1)}) custom-call(s32[1]{0:T(128)} %bitcast.box_ref, f32[25,128,128]{2,1,0:T(8,128)} %previous_ref.3, f32[25,25]{1,0:T(8,128)} %derivative_ref.3, f32[25,128]{1,0:T(8,128)} %radial_ref.3, f32[25,128]{1,0:T(8,128)} %shear_ref.3, ...), custom_call_target="tpu_custom_call" | custom-call | tf_op jit(solution)/shard_map/start/pallas_call | solution.py:412
  29.8 3.7 %collective-permute-start = (f32[128,256]{1,0:T(8,128)}, f32[128,256]{1,0:T(8,128)S(1)}, u32[]{:S(2)}, u32[]{:S(2)}) collective-permute-start(f32[128,256]{1,0:T(8,128)} %get-tuple-element.36), channel_id=1, source_target_pairs={{0,4},{4,8},{8,12},{12,16},{16,20},{20,24},{24,28},{1,5},{5,9},{9,... | collective-permute-start | bytes 393224 | tf_op jit(solution)/shard_map/ppermute | solution.py:426
  33.5 1.3 collective-permute-start.1
  34.8 0.0 all-to-all-done.message_ref
  34.8 0.0 copy-start
  34.8 0.6 copy-done
  35.4 14.0 %nodes.1 = (f32[32,128,128]{2,1,0:T(8,128)}, s32[32,128]{1,0:T(8,128)}, f32[5,32,128]{2,1,0:T(8,128)}, f32[32,128]{1,0:T(8,128)}) custom-call(s32[1]{0:T(128)} %bitcast.box_ref, s32[32,128]{1,0:T(8,128)} %get-tuple-element.25.win_ref, f32[32,8,128]{2,1,0:T(8,128)} %copy-done, f32[32,128]{1,0:T(8,128)} %get-tuple-element.27.off_ref, ...), custom_call_target="tpu_custom_call" | custom-call | tf_op jit(solution)/shard_map/nodes/pallas_call | solution.py:412
  49.5 6.8 %all-gather = f32[128,128]{1,0:T(8,128)} all-gather(f32[32,128]{1,0:T(8,128)} %get-tuple-element.31), channel_id=2, replica_groups=mesh['mer'=8,'box'=4] {'box'}, dimensions={0}, use_global_device_ids=true | all-gather | bytes 81920 | tf_op jit(solution)/shard_map/all_gather | solution.py:525
  56.3 0.0 collective-permute-done.below_ref
  56.3 0.0 copy-start.2
  56.3 0.0 collective-permute-done.1.above_ref
  56.3 0.0 copy-start.4
  56.3 0.7 copy-done.2
  56.9 0.0 copy-done.4
  57.0 39.0 %middle.1 = (f32[25,128,128]{2,1,0:T(8,128)}, f32[25,128,128]{2,1,0:T(8,128)}, f32[128,256]{1,0:T(8,128)}, f32[128,256]{1,0:T(8,128)}, f32[32,128]{1,0:T(8,128)}, /*index=5*/f32[32,128]{1,0:T(8,128)}) custom-call(s32[1]{0:T(128)} %bitcast.box_ref, s32[32,128]{1,0:T(8,128)} %get-tuple-element.25.win_ref, f32[4,32,128]{2,1,0:T(8,128)} %bitcast.19, ...), custom_call_target="tpu_custom_call" | custom-call | tf_op jit(solution)/shard_map/middle/pallas_call | solution.py:412
  96.0 6.0 %all-gather.1 = f32[128,128]{1,0:T(8,128)} all-gather(f32[32,128]{1,0:T(8,128)} %get-tuple-element.39), channel_id=3, replica_groups=mesh['mer'=8,'box'=4] {'box'}, dimensions={0}, use_global_device_ids=true | all-gather | bytes 81920 | tf_op jit(solution)/shard_map/all_gather | solution.py:545
  102.0 1.5 %box.1 = (f32[32,128]{1,0:T(8,128)}, f32[32,128]{1,0:T(8,128)}) custom-call(f32[4,32,128]{2,1,0:T(8,128)} %bitcast.20, f32[5,32,128]{2,1,0:T(8,128)} %get-tuple-element.32.node_ref, f32[32,128]{1,0:T(8,128)} %get-tuple-element.40.now_ref), custom_call_target="tpu_custom_call" | custom-call | tf_op jit(solution)/shard_map/box/pallas_call | solution.py:412
  103.5 6.6 %all-to-all-start.1 = ((f32[8,4,128]{2,1,0:T(4,128)}), f32[8,4,128]{2,1,0:T(4,128)S(1)}, u32[]{:S(2)}, u32[]{:S(2)}) async-start(f32[8,4,128]{2,1,0:T(4,128)} %bitcast.21), calls=%async_computation.1 | async-start | bytes 32768 | tf_op jit(solution)/shard_map/all_to_all | solution.py:548
  110.1 3.9 %collective-permute-start.2 = (f32[128,256]{1,0:T(8,128)}, f32[128,256]{1,0:T(8,128)S(1)}, u32[]{:S(2)}, u32[]{:S(2)}) collective-permute-start(f32[128,256]{1,0:T(8,128)} %get-tuple-element.42), channel_id=1, source_target_pairs={{0,4},{4,8},{8,12},{12,16},{16,20},{20,24},{24,28},{1,5},{5,9},{9,... | collective-permute-start | bytes 393224 | tf_op jit(solution)/shard_map/ppermute | solution.py:426
  114.0 1.3 collective-permute-start.3
  115.3 1.3 all-to-all-done.1
  116.7 0.6 dynamic-slice_bitcast_fusion.value_ref
  117.3 1.7 %ungroup.1 = f32[1,1024]{1,0:T(1,128)} custom-call(s32[1,1024]{1,0:T(1,128)} %get-tuple-element.46.dest_ref, f32[1,1024]{1,0:T(1,128)} %dynamic-slice_bitcast_fusion.value_ref), custom_call_target="tpu_custom_call" | custom-call | tf_op jit(solution)/shard_map/ungroup/pallas_call | solution.py:412
  119.0 0.0 collective-permute-done.2.below_ref
  119.0 0.0 copy-start.1
  119.0 2.1 %collective-permute-done.3.above_ref = f32[128,256]{1,0:T(8,128)S(1)} collective-permute-done((f32[128,256]{1,0:T(8,128)}, f32[128,256]{1,0:T(8,128)S(1)}, u32[]{:S(2)}, u32[]{:S(2)}) %collective-permute-start.3) | collective-permute-done | bytes 131104 | tf_op jit(solution)/shard_map/ppermute | solution.py:426
  121.1 0.0 copy-start.3
  121.1 0.0 copy-done.1
  121.1 0.6 copy-done.3
  121.7 19.1 %last.1 = f32[25,128,128]{2,1,0:T(8,128)} custom-call(s32[1]{0:T(128)} %bitcast.box_ref, s32[32,128]{1,0:T(8,128)} %get-tuple-element.25.win_ref, f32[32,128]{1,0:T(8,128)} %get-tuple-element.41.coefficient_ref, s32[32,128]{1,0:T(8,128)} %get-tuple-element.33.place_ref, f32[32,128,128]{2,1,0:T(8,128)} %get-tuple-element.34.harmonic_ref, ...), custom_call_target="tpu_custom_call" | custom-call | tf_op jit(solution)/shard_map/last/pallas_call | solution.py:412
Async XLA Ops:
  3.0 31.8 %all-to-all-start = ((f32[32,8,128]{2,1,0:T(8,128)}), f32[32,8,128]{2,1,0:T(8,128)S(1)}, u32[]{:S(2)}, u32[]{:S(2)}) async-start(f32[32,8,128]{2,1,0:T(8,128)} %get-tuple-element.26), calls=%async_computation | async-start | bytes 262144 | tf_op jit(solution)/shard_map/all_to_all | solution.py:481
  29.8 26.5 %collective-permute-start = (f32[128,256]{1,0:T(8,128)}, f32[128,256]{1,0:T(8,128)S(1)}, u32[]{:S(2)}, u32[]{:S(2)}) collective-permute-start(f32[128,256]{1,0:T(8,128)} %get-tuple-element.36), channel_id=1, source_target_pairs={{0,4},{4,8},{8,12},{12,16},{16,20},{20,24},{24,28},{1,5},{5,9},{9,... | collective-permute-start | bytes 393224 | tf_op jit(solution)/shard_map/ppermute | solution.py:426
  33.5 22.8 %collective-permute-start.1 = (f32[128,256]{1,0:T(8,128)}, f32[128,256]{1,0:T(8,128)S(1)}, u32[]{:S(2)}, u32[]{:S(2)}) collective-permute-start(f32[128,256]{1,0:T(8,128)} %get-tuple-element.37), channel_id=1, source_target_pairs={{4,0},{8,4},{12,8},{16,12},{20,16},{24,20},{28,24},{5,1},{9,5},{13... | collective-permute-start | bytes 393224 | tf_op jit(solution)/shard_map/ppermute | solution.py:426
  34.8 0.7 copy-start
  56.3 0.7 copy-start.2
  56.3 0.7 copy-start.4
  103.5 13.2 %all-to-all-start.1 = ((f32[8,4,128]{2,1,0:T(4,128)}), f32[8,4,128]{2,1,0:T(4,128)S(1)}, u32[]{:S(2)}, u32[]{:S(2)}) async-start(f32[8,4,128]{2,1,0:T(4,128)} %bitcast.21), calls=%async_computation.1 | async-start | bytes 32768 | tf_op jit(solution)/shard_map/all_to_all | solution.py:548
  110.1 8.9 %collective-permute-start.2 = (f32[128,256]{1,0:T(8,128)}, f32[128,256]{1,0:T(8,128)S(1)}, u32[]{:S(2)}, u32[]{:S(2)}) collective-permute-start(f32[128,256]{1,0:T(8,128)} %get-tuple-element.42), channel_id=1, source_target_pairs={{0,4},{4,8},{8,12},{12,16},{16,20},{20,24},{24,28},{1,5},{5,9},{9,... | collective-permute-start | bytes 393224 | tf_op jit(solution)/shard_map/ppermute | solution.py:426
  114.0 7.1 %collective-permute-start.3 = (f32[128,256]{1,0:T(8,128)}, f32[128,256]{1,0:T(8,128)S(1)}, u32[]{:S(2)}, u32[]{:S(2)}) collective-permute-start(f32[128,256]{1,0:T(8,128)} %get-tuple-element.43), channel_id=1, source_target_pairs={{4,0},{8,4},{12,8},{16,12},{20,16},{24,20},{28,24},{5,1},{9,5},{13... | collective-permute-start | bytes 393224 | tf_op jit(solution)/shard_map/ppermute | solution.py:426
  119.0 2.1 %copy-start.1 = (f32[128,256]{1,0:T(8,128)}, f32[128,256]{1,0:T(8,128)S(1)}, u32[]{:S(2)}) copy-start(f32[128,256]{1,0:T(8,128)S(1)} %collective-permute-done.2.below_ref) | copy-start | bytes 393220
  121.1 0.6 copy-start.3

commit v2 on v1

v2 whole, which is shorter than its diff:
```python
import functools

import jax
import jax.numpy as jnp
from jax import lax
from jax.experimental import pallas as pl
from jax.experimental.pallas import tpu as pltpu
from jax.sharding import PartitionSpec as P

MODES = 256
STEPS = 2
LANES = 128
WIDE = 256
BATCH = 8

step_scale = 0.25
f32 = jnp.float32
bf16 = jnp.bfloat16
i32 = jnp.int32


def iota(shape, dim):
    return lax.broadcasted_iota(i32, shape, dim)


def dot(a, b):
    return lax.dot_general(a, b, (((1,), (0,)), ((), ())), preferred_element_type=f32)


def dot_nt(a, b):
    return lax.dot_general(a, b, (((1,), (1,)), ((), ())), preferred_element_type=f32)


def hot(mask):
    return jnp.where(mask, 1.0, 0.0).astype(bf16)


def split(x):
    high = x.astype(bf16)
    return high, (x - high.astype(f32)).astype(bf16)


def stacked(x):
    high, low = split(x)
    return jnp.concatenate([high, low], axis=0)


def folded(x):
    half = x.shape[0] // 2
    return x[:half] + x[half:]


def thirds(x):
    first = x.astype(bf16).astype(f32)
    second = (x - first).astype(bf16).astype(f32)
    return jnp.concatenate([first, second, x - first - second], axis=0)


def cos_sin(x):
    turns = jnp.floor(x * 0.6366197723675814 + 0.5)
    r = x - turns * 1.5703125 - turns * 4.837512969970703125e-4 - turns * 7.54978995489188216e-8
    z = r * r
    sine = ((-1.9515295891e-4 * z + 8.3321608736e-3) * z - 1.6666654611e-1) * z * r + r
    cosine = ((2.443315711809948e-5 * z - 1.388731625493765e-3) * z + 4.166664568298827e-2) * z * z
    cosine = cosine - 0.5 * z + 1.0
    quarter = turns.astype(i32)
    odd = (quarter & 1) == 1
    cosine, sine = jnp.where(odd, sine, cosine), jnp.where(odd, cosine, sine)
    return (
        jnp.where(((quarter + 1) & 2) == 2, -cosine, cosine),
        jnp.where((quarter & 2) == 2, -sine, sine),
    )


def running(mask):
    rows, width = mask.shape
    below = hot(iota((LANES, LANES), 0) < iota((LANES, LANES), 1))
    total = jnp.zeros((rows, 1), f32)
    counts = []
    for start in range(0, width, LANES):
        block = mask[:, start : start + LANES]
        counts.append(dot(block.astype(bf16), below) + total)
        total = total + jnp.sum(block, axis=1, keepdims=True)
    return jnp.concatenate(counts, axis=1), total


def group_kernel(parts, copies, slot_hbm, *refs):
    fields, refs = refs[:6], refs[6:]
    out_ref, part_hbm, rank_hbm, part_ref, rank_ref, slot_ref, stack_ref, done = refs
    nodes = slot_ref.shape[1]
    per = nodes // parts
    stack_ref[...] = jnp.zeros_like(stack_ref)
    moves = [pltpu.make_async_copy(slot_hbm, slot_ref, done.at[0])]
    for index, field in enumerate(fields):
        moves.append(
            pltpu.make_async_copy(field, stack_ref.at[index + 1 : index + 2, :], done.at[index + 1])
        )
    for move in moves:
        move.start()
    moves[0].wait()
    slot = slot_ref[...].astype(f32)
    place = jnp.floor((slot + 0.5) * (1.0 / parts))
    part = (slot - place * parts).astype(i32)
    rows = max(16, parts)
    mask = jnp.where(iota((rows, nodes), 0) == part, 1.0, 0.0)
    count, _ = running(mask)
    rank = jnp.sum(mask * count, axis=0, keepdims=True).astype(i32)
    part_ref[...] = part
    rank_ref[...] = rank
    kept = [
        pltpu.make_async_copy(part_ref, part_hbm, done.at[7]),
        pltpu.make_async_copy(rank_ref, rank_hbm, done.at[8]),
    ]
    for move in kept:
        move.start()
    for move in moves[1:]:
        move.wait()
    stack_ref[0:1, :] = place
    terms = thirds(stack_ref[...])
    blocks = [jnp.where(part == index, terms, 0.0) for index in range(parts)]
    chosen = hot(iota((per, nodes), 0) == rank)
    moved = dot_nt(jnp.concatenate(blocks, axis=0).astype(bf16), chosen)
    for index in range(parts):
        block = moved[24 * index : 24 * index + 24]
        block = block[0:8] + block[8:16] + block[16:24]
        for copy in range(copies):
            out_ref[index * copies + copy] = block
    for move in kept:
        move.wait()


def ungroup_kernel(part_ref, rank_ref, value_ref, out_ref):
    parts, per = value_ref.shape
    nodes = part_ref.shape[1]
    chosen = hot(iota((per, nodes), 0) == rank_ref[...])
    back = dot(thirds(value_ref[...]).astype(bf16), chosen)
    back = back[0:parts] + back[parts : 2 * parts] + back[2 * parts :]
    mask = iota((parts, nodes), 0) == part_ref[...]
    out_ref[...] = jnp.sum(jnp.where(mask, back, 0.0), axis=0, keepdims=True)


def order_rows(
    elements, target_ref, rows_ref, lower_ref, upper_ref, key_ref, keycol_ref, off_ref, cnt_ref, win_ref
):
    blocks = off_ref.shape[0]
    count = target_ref.shape[1]
    shared = lower_ref.shape[1]
    mask = jnp.where(iota((blocks, count), 0) == target_ref[...], 1.0, 0.0)
    before, total = running(mask)
    totals = jnp.broadcast_to(total, (blocks, LANES))
    offset = dot(hot(iota((blocks, blocks), 1) < iota((blocks, blocks), 0)), totals.astype(bf16))
    off_ref[...] = offset
    cnt_ref[...] = totals
    window = jnp.floor(offset * (1.0 / LANES)) * LANES
    win_ref[...] = jnp.minimum(window, count - WIDE).astype(i32)
    place = jnp.sum(mask * (before + offset[:, 0:1]), axis=0, keepdims=True)
    strip = jnp.floor((place + 0.5) * (1.0 / LANES))
    lane = (place - strip * LANES).astype(i32)
    row = rows_ref[...].astype(f32)
    node = jnp.floor((row + 0.5) * (1.0 / elements))
    strips = count // LANES
    chosen = iota((strips, count), 0) == strip.astype(i32)
    terms = jnp.concatenate(
        [jnp.where(chosen, node, 0.0), jnp.where(chosen, row - node * elements, 0.0)], axis=0
    )
    moved = dot_nt(terms.astype(bf16), hot(iota((LANES, count), 0) == lane))
    moved = (moved[:strips] * elements + moved[strips:]).astype(i32)
    for index in range(strips):
        key_ref[:, index * LANES : (index + 1) * LANES] = moved[index : index + 1]
    key_ref[:, count : count + shared] = lower_ref[...]
    key_ref[:, count + shared : count + 2 * shared] = upper_ref[...]
    for start in range(0, count + 2 * shared, LANES):
        block = jnp.broadcast_to(key_ref[:, start : start + LANES].astype(f32), (LANES, LANES))
        keycol_ref[start : start + LANES, :] = block.T.astype(i32)


def fill_stack(value_ref, stack_ref):
    nodes, columns, elements = value_ref.shape
    for node in range(nodes):
        high, low = split(value_ref[node])
        lanes = slice(node * elements, (node + 1) * elements)
        stack_ref[0:columns, lanes] = high
        stack_ref[columns:, lanes] = low
    if stack_ref.shape[1] > nodes * elements:
        tail = slice(nodes * elements, stack_ref.shape[1])
        stack_ref[:, tail] = jnp.zeros_like(stack_ref[:, tail])


def picked(stack_ref, hot_ref, key_ref, start):
    depth = stack_ref.shape[1]
    key = key_ref[:, pl.ds(start, WIDE)]
    base = iota((LANES, WIDE), 0)
    for row in range(0, depth, LANES):
        hot_ref[row : row + LANES, :] = hot(base == key - row)
    return dot(stack_ref[...], hot_ref[0:depth, :])


def pick_rows(stack_ref, hot_ref, key_ref, out_ref):
    def body(index, carry):
        start = pl.multiple_of(index * WIDE, WIDE)
        out_ref[:, pl.ds(start, WIDE)] = picked(stack_ref, hot_ref, key_ref, start).astype(bf16)
        return carry

    lax.fori_loop(0, out_ref.shape[1] // WIDE, body, 0)


def pick_boundary(stack_ref, hot_ref, key_ref, low_ref, high_ref):
    shared = low_ref.shape[1]
    first = key_ref.shape[1] - 2 * shared
    for ref, origin in ((low_ref, first), (high_ref, first + shared)):
        for start in range(0, shared, WIDE):
            ref[:, start : start + WIDE] = folded(
                picked(stack_ref, hot_ref, key_ref, origin + start)
            )


def spread(derivative_ref, transposed, rows):
    nodes = derivative_ref.shape[0]
    size = 8 * nodes
    left = jnp.where(iota((rows, nodes), 0) // 8 == iota((rows, nodes), 1), 1.0, 0.0)
    right = jnp.where(iota((nodes, size), 1) // 8 == iota((nodes, size), 0), 1.0, 0.0)
    dims = (((1,), (1,)), ((), ())) if transposed else (((1,), (0,)), ((), ()))
    half = lax.dot_general(
        left, derivative_ref[...], dims, precision=lax.Precision.HIGHEST, preferred_element_type=f32
    )
    full = jnp.dot(half, right, precision=lax.Precision.HIGHEST, preferred_element_type=f32)
    full = jnp.where(iota((rows, size), 0) % 8 == iota((rows, size), 1) % 8, full, 0.0)
    return stacked(full)


def force_into(value_ref, forward, backward, radial_ref, shear_ref, first_order, force_ref):
    nodes, columns, elements = value_ref.shape
    size = 8 * nodes
    rows = forward.shape[0] // 2
    radial = jnp.broadcast_to(radial_ref[...][:, None, :], (nodes, 8, elements)).reshape(
        size, elements
    )
    radial = jnp.concatenate([radial, radial], axis=1)
    shear = jnp.broadcast_to(shear_ref[...][:, None, :], (nodes, 8, elements))

    def applied(matrix, x):
        high, low = split(x)
        both = dot(matrix[...], high)
        return both[:size] + both[rows : rows + size] + dot(matrix[0:rows, :], low)[:size]

    def body(index, carry):
        first = pl.multiple_of(index * 32, 32)
        starts = [first, first + 16]
        halves = [
            [value_ref[:, pl.ds(start, 8), :], value_ref[:, pl.ds(start + 8, 8), :]]
            for start in starts
        ]
        fields = [
            jnp.concatenate([half.reshape(size, elements) for half in pair], axis=1)
            for pair in halves
        ]
        fluxes = [radial * applied(forward, x) for x in fields]
        backs = [applied(backward, flux) for flux in fluxes]
        for start, pair, back in zip(starts, halves, backs):
            for side, half in enumerate(pair):
                order = (first_order + start + 8 * side + iota((8, elements), 0)).astype(f32)
                wave = (2.0 * order / MODES) ** 2
                block = back[:, side * elements : (side + 1) * elements]
                force_ref[:, pl.ds(start + 8 * side, 8), :] = (
                    -block.reshape(nodes, 8, elements) - shear * wave[None] * half
                )
        return carry

    lax.fori_loop(0, columns // 32, body, 0)


def transfers(pairs, done):
    return [
        pltpu.make_async_copy(source, target, done.at[index])
        for index, (source, target) in enumerate(pairs)
    ]


def begin(moves):
    for move in moves:
        move.start()


def finish(moves):
    for move in moves:
        move.wait()


def start_kernel(
    elements, box_ref, target_hbm, rows_hbm, lower_hbm, upper_hbm, derivative_hbm,
    value_hbm, radial_hbm, shear_hbm,
    off_ref, cnt_ref, win_ref, picked_ref,
    key_hbm, keycol_hbm, forward_hbm, backward_hbm, force_hbm, low_hbm, high_hbm,
    target_ref, rows_ref, lower_ref, upper_ref, derivative_ref, value_ref, radial_ref, shear_ref,
    key_ref, keycol_ref, forward_ref, backward_ref, force_ref, low_ref, high_ref,
    stack_ref, hot_ref, done, kept,
):
    moves = transfers(
        [
            (target_hbm, target_ref), (rows_hbm, rows_ref), (lower_hbm, lower_ref),
            (upper_hbm, upper_ref), (derivative_hbm, derivative_ref), (value_hbm, value_ref),
            (radial_hbm, radial_ref), (shear_hbm, shear_ref),
        ],
        done,
    )
    saves = transfers(
        [
            (key_ref, key_hbm), (keycol_ref, keycol_hbm), (forward_ref, forward_hbm),
            (backward_ref, backward_hbm), (force_ref, force_hbm), (low_ref, low_hbm),
            (high_ref, high_hbm),
        ],
        kept,
    )
    begin(moves)
    finish(moves[:5])
    order_rows(
        elements, target_ref, rows_ref, lower_ref, upper_ref, key_ref, keycol_ref, off_ref,
        cnt_ref, win_ref,
    )
    columns = value_ref.shape[1]
    rows = forward_ref.shape[0] // 2
    forward_ref[...] = spread(derivative_ref, False, rows)
    backward_ref[...] = spread(derivative_ref, True, rows)
    begin(saves[:4])
    finish(moves[5:])
    force_into(
        value_ref, forward_ref, backward_ref, radial_ref, shear_ref,
        box_ref[0] * columns % MODES, force_ref,
    )
    begin(saves[4:5])
    fill_stack(force_ref, stack_ref)
    pick_boundary(stack_ref, hot_ref, key_ref, low_ref, high_ref)
    begin(saves[5:])
    fill_stack(value_ref, stack_ref)
    pick_rows(stack_ref, hot_ref, key_ref, picked_ref)
    finish(saves)


def window_hot(win_ref, place_ref, group, stride):
    window = pl.multiple_of(win_ref[group * stride, 0], LANES)
    place = place_ref[pl.ds(group, 1), :]
    return window, hot(iota((WIDE, LANES), 0) + window == place)


def sample_into(win_ref, place_ref, harmonic_ref, picked_ref, stride, sample_ref):
    def body(index, carry):
        for group in [BATCH * index + part for part in range(BATCH)]:
            window, chosen = window_hot(win_ref, place_ref, group, stride)
            rows = folded(dot(picked_ref[:, pl.ds(window, WIDE)], chosen))
            sample_ref[pl.ds(group, 1), :] = jnp.sum(
                rows * harmonic_ref[group], axis=0, keepdims=True
            )
        return carry

    lax.fori_loop(0, sample_ref.shape[0] // BATCH, body, 0)


def node_kernel(
    stride, box_ref, win_ref, message_ref, off_ref, cnt_ref, picked_ref,
    harmonic_ref, place_ref, node_ref, sample_ref,
    near_re, near_im, far_re, far_im,
):
    groups, columns, _ = harmonic_ref.shape
    place = message_ref[:, 0, :]
    angle = message_ref[:, 1, :]
    place_ref[...] = jnp.where(place < cnt_ref[...], off_ref[...] + place, -1.0).astype(i32)
    for index in range(5):
        node_ref[index] = message_ref[:, 2 + index, :]

    def power(order):
        return cos_sin(order * angle)

    def times(x, y):
        return x[0] * y[0] - x[1] * y[1], x[0] * y[1] + x[1] * y[0]

    near = [(jnp.ones_like(angle), jnp.zeros_like(angle))] + [None] * 7
    for bit in (1, 2, 4):
        factor = power(float(bit))
        near[bit] = factor
        for low in range(1, bit):
            near[bit + low] = times(factor, near[low])
    for index, (re, im) in enumerate(near):
        near_re[:, index, :] = re
        near_im[:, index, :] = im
    first = box_ref[0] * columns
    base_re, base_im = power((first % MODES).astype(f32))
    sine = first >= MODES
    far = [
        (jnp.where(sine, base_im, base_re), jnp.where(sine, -base_re, base_im))
    ] + [None] * (columns // 8 - 1)
    bit = 1
    while bit < columns // 8:
        factor = power(float(8 * bit))
        for low in range(min(bit, columns // 8 - bit)):
            far[bit + low] = times(factor, far[low])
        bit *= 2
    for index, (re, im) in enumerate(far):
        far_re[index] = re
        far_im[index] = im

    def body(group, carry):
        re, im = near_re[group], near_im[group]
        for index in range(columns // 8):
            harmonic_ref[group, 8 * index : 8 * index + 8, :] = (
                far_re[index, pl.ds(group, 1), :] * re - far_im[index, pl.ds(group, 1), :] * im
            )
        return carry

    lax.fori_loop(0, groups, body, 0)
    sample_into(win_ref, place_ref, harmonic_ref, picked_ref, stride, sample_ref)


def nodes_step(samples_ref, node_ref, now, before, next_ref, coefficient_ref):
    sample = samples_ref[0]
    for index in range(1, samples_ref.shape[0]):
        sample = sample + samples_ref[index]
    pull = node_ref[0] * (sample - now)
    next_ref[...] = 2.0 * now - before + step_scale * pull / node_ref[1]
    coefficient_ref[...] = -node_ref[2] * pull


def annulus_step(
    early, late, emit, stride, first_order, win_ref, place_ref, harmonic_ref, coefficient_ref, keycol_ref,
    below_ref, above_ref, value_ref, previous_ref, force_ref, mass_ref, modes_ref,
    next_ref, reaction_ref, terms_ref, hot_ref, hot2_ref, added_ref,
):
    nodes, columns, elements = value_ref.shape
    groups = place_ref.shape[0]
    count = reaction_ref.shape[1]
    shared = below_ref.shape[1]
    reaction_ref[...] = jnp.zeros_like(reaction_ref)

    def react(index, carry):
        found = []
        for group in [BATCH * index + part for part in range(BATCH)]:
            window, chosen = window_hot(win_ref, place_ref, group, stride)
            weighted = harmonic_ref[group] * coefficient_ref[pl.ds(group, 1), :]
            found.append((window, folded(dot_nt(stacked(weighted), chosen))))
        for window, rows in found:
            reaction_ref[:, pl.ds(window, WIDE)] = reaction_ref[:, pl.ds(window, WIDE)] + rows
        return carry

    lax.fori_loop(0, groups // BATCH, react, 0)
    finish(early)
    terms_ref[:, 0:count] = stacked(reaction_ref[...])
    terms_ref[:, count : count + shared] = stacked(below_ref[...])
    terms_ref[:, count + shared : count + 2 * shared] = stacked(above_ref[...])
    depth = count + 2 * shared
    lane = iota((LANES, LANES), 1)

    def place_rows(first, width, buffer):
        for side in range(width):
            base = lane + (first + side) * elements
            for row in range(0, depth, LANES):
                buffer[row : row + LANES, side * LANES : (side + 1) * LANES] = hot(
                    keycol_ref[row : row + LANES, :] == base
                )
        rows = folded(dot(terms_ref[...], buffer[0:depth, 0 : width * LANES]))
        for side in range(width):
            added_ref[first + side] = rows[:, side * LANES : (side + 1) * LANES]

    def place_four(index, carry):
        place_rows(4 * index, 2, hot_ref)
        place_rows(4 * index + 2, 2, hot2_ref)
        return carry

    lax.fori_loop(0, nodes // 4, place_four, 0)
    for first in range(nodes // 4 * 4, nodes, 2):
        place_rows(first, min(2, nodes - first), hot_ref)
    order = first_order + iota((columns, elements), 0)
    finish(late)
    live = order < modes_ref[...]
    for node in range(nodes):
        gain = jnp.where(live, step_scale / mass_ref[node : node + 1, :], 0.0)
        next_ref[node] = (
            2.0 * value_ref[node]
            - previous_ref[node]
            + gain * (force_ref[node] + added_ref[node])
        )
        emit(node)


def middle_kernel(
    stride, box_ref, win_ref, samples_ref, node_ref, place_ref, harmonic_ref,
    keycol_hbm, below_hbm, above_hbm, value_hbm, previous_hbm, force_hbm, mass_hbm, modes_hbm,
    key_hbm, forward_hbm, backward_hbm, radial_hbm, shear_hbm,
    sample_ref, boxnext_ref, next_hbm, nextforce_hbm, low_hbm, high_hbm,
    keycol_ref, below_ref, above_ref, value_ref, previous_ref, force_ref, mass_ref, modes_ref,
    key_ref, forward_ref, backward_ref, radial_ref, shear_ref,
    next_ref, low_ref, high_ref,
    coefficient_ref, reaction_ref, terms_ref, hot_ref, hot2_ref, added_ref, stack_ref, picked_ref,
    done, kept,
):
    moves = transfers(
        [
            (keycol_hbm, keycol_ref), (below_hbm, below_ref), (above_hbm, above_ref),
            (value_hbm, value_ref), (previous_hbm, previous_ref), (force_hbm, force_ref),
            (mass_hbm, mass_ref), (modes_hbm, modes_ref), (key_hbm, key_ref),
            (forward_hbm, forward_ref), (backward_hbm, backward_ref), (radial_hbm, radial_ref),
            (shear_hbm, shear_ref),
        ],
        done,
    )
    saves = transfers(
        [
            (next_ref, next_hbm), (added_ref, nextforce_hbm), (low_ref, low_hbm),
            (high_ref, high_hbm),
        ],
        kept,
    )
    begin(moves)
    columns = value_ref.shape[1]
    first_order = box_ref[0] * columns % MODES
    nodes_step(samples_ref, node_ref, node_ref[3], node_ref[4], boxnext_ref, coefficient_ref)
    annulus_step(
        moves[:3], moves[3:], lambda node: None,
        stride, first_order, win_ref, place_ref, harmonic_ref, coefficient_ref, keycol_ref,
        below_ref, above_ref, value_ref, previous_ref, force_ref, mass_ref, modes_ref,
        next_ref, reaction_ref, terms_ref, hot_ref, hot2_ref, added_ref,
    )
    begin(saves[:1])
    force_into(
        next_ref, forward_ref, backward_ref, radial_ref, shear_ref, first_order, added_ref
    )
    begin(saves[1:2])
    fill_stack(added_ref, stack_ref)
    pick_boundary(stack_ref, hot_ref, key_ref, low_ref, high_ref)
    begin(saves[2:])
    fill_stack(next_ref, stack_ref)
    pick_rows(stack_ref, hot_ref, key_ref, picked_ref)
    sample_into(win_ref, place_ref, harmonic_ref, picked_ref, stride, sample_ref)
    finish(saves)


def box_kernel(samples_ref, node_ref, now_ref, boxnext_ref, coefficient_ref):
    nodes_step(samples_ref, node_ref, now_ref[...], node_ref[3], boxnext_ref, coefficient_ref)


def last_kernel(
    stride, box_ref, win_ref, coefficient_ref, place_ref, harmonic_ref,
    keycol_hbm, below_hbm, above_hbm, value_hbm, previous_hbm, force_hbm, mass_hbm, modes_hbm,
    next_hbm,
    keycol_ref, below_ref, above_ref, value_ref, previous_ref, force_ref, mass_ref, modes_ref,
    next_ref, reaction_ref, terms_ref, hot_ref, hot2_ref, added_ref, done, kept,
):
    moves = transfers(
        [
            (keycol_hbm, keycol_ref), (below_hbm, below_ref), (above_hbm, above_ref),
            (value_hbm, value_ref), (previous_hbm, previous_ref), (force_hbm, force_ref),
            (mass_hbm, mass_ref), (modes_hbm, modes_ref),
        ],
        done,
    )
    begin(moves)
    first_order = box_ref[0] * value_ref.shape[1] % MODES
    saves = transfers(
        [(next_ref.at[node], next_hbm.at[node]) for node in range(value_ref.shape[0])], kept
    )
    annulus_step(
        moves[:3], moves[3:], lambda node: saves[node].start(),
        stride, first_order, win_ref, place_ref, harmonic_ref, coefficient_ref, keycol_ref,
        below_ref, above_ref, value_ref, previous_ref, force_ref, mass_ref, modes_ref,
        next_ref, reaction_ref, terms_ref, hot_ref, hot2_ref, added_ref,
    )
    finish(saves)


def exchanged(low, high):
    size = lax.axis_size("mer")
    up = [(i, i + 1) for i in range(size - 1)]
    down = [(j, i) for i, j in up]
    return lax.ppermute(high, "mer", up), lax.ppermute(low, "mer", down)


SMEM, VMEM, HBM = pltpu.SMEM, pltpu.VMEM, pltpu.HBM


def call(kernel, ins, outs, scratch=(), copies=(), name=None, limit=40):
    arrays = [
        pltpu.with_memory_space_constraint(array, memory) if pinned else array
        for array, memory, pinned in ins
    ]
    return pl.pallas_call(
        kernel,
        out_shape=[
            memory(shape, dtype) if memory else jax.ShapeDtypeStruct(shape, dtype)
            for shape, dtype, memory in outs
        ],
        in_specs=[pl.BlockSpec(memory_space=memory) for _, memory, _ in ins],
        out_specs=[pl.BlockSpec(memory_space=memory or VMEM) for _, _, memory in outs],
        scratch_shapes=[VMEM(shape, dtype) for shape, dtype in scratch]
        + [pltpu.SemaphoreType.DMA((number,)) for number in copies],
        compiler_params=pltpu.CompilerParams(vmem_limit_bytes=limit << 20),
        name=name,
    )(*arrays)


def per_device(
    annulus,
    annulus_prev,
    derivative,
    radial_modulus,
    shear_modulus,
    node_mass,
    element_modes,
    upper_rows,
    lower_rows,
    coupling_rows,
    coupling_target,
    box_field,
    box_prev,
    box_angle,
    box_spring,
    box_mass,
    box_weight,
    box_slot,
):
    mer_count = lax.axis_size("mer")
    box_count = lax.axis_size("box")
    blocks = mer_count * box_count
    nodes, columns, elements = annulus.shape
    box_nodes = box_slot.shape[0]
    per = box_nodes // mer_count
    stride = LANES // per
    groups = blocks * per // LANES
    count = coupling_rows.shape[0]
    shared = upper_rows.shape[0]
    depth = count + 2 * shared
    padded_nodes = nodes + nodes % 2
    rows = -(-8 * nodes // 16) * 16
    volume = (nodes, columns, elements)
    grid = (groups, LANES)
    flat = (nodes, elements)
    hot_scratch = ((max(padded_nodes * elements, depth), WIDE), bf16)
    stack_scratch = ((2 * columns, padded_nodes * elements), bf16)

    def far(value):
        return value, HBM, True

    def near(value):
        return value, VMEM, True

    def landed(value):
        return value, VMEM, False

    def anywhere(value):
        return value, pl.ANY, False

    def scalar(value):
        return value, SMEM, False

    box = scalar(jnp.full((1,), lax.axis_index("box"), i32))

    sent = [
        far(value.reshape(1, box_nodes))
        for value in (box_slot, box_angle, box_spring, box_mass, box_weight, box_field, box_prev)
    ]
    line = ((1, box_nodes), i32)
    messages, part, rank = call(
        functools.partial(group_kernel, mer_count, box_count),
        sent,
        [((blocks, 8, per), f32, None), line + (HBM,), line + (HBM,)],
        [line, line, line, ((8, box_nodes), f32)],
        copies=(9,),
        name="group",
    )
    messages = lax.all_to_all(messages, ("mer", "box"), split_axis=0, concat_axis=0, tiled=True)
    if stride > 1:
        messages = messages.reshape(groups, stride, 8, per).swapaxes(1, 2)
        messages = messages.reshape(groups, 8, LANES)

    expanded = VMEM if stride == 1 else None
    field = (volume, f32)
    table = (flat, f32)
    limits = ((1, elements), i32)
    side = ((columns, shared), f32)
    keys = [((1, depth), i32), ((depth, LANES), i32)]
    matrices = [((2 * rows, 8 * nodes), bf16)] * 2
    picked = ((2 * columns, count), bf16)
    kept = keys + matrices + [field, side, side]
    (
        offset, filled, window, chosen, key, keycol, forward, backward, force, low, high,
    ) = call(
        functools.partial(start_kernel, elements),
        [
            box,
            far(coupling_target.reshape(1, count)),
            far(coupling_rows.reshape(1, count)),
            far(lower_rows.reshape(1, shared)),
            far(upper_rows.reshape(1, shared)),
            far(derivative),
            far(annulus),
            far(radial_modulus),
            far(shear_modulus),
        ],
        [
            ((blocks, LANES), f32, expanded),
            ((blocks, LANES), f32, expanded),
            ((blocks, LANES), i32, None),
            picked + (VMEM,),
        ]
        + [shape + (HBM,) for shape in kept],
        [((1, count), i32)] * 2
        + [((1, shared), i32)] * 2
        + [((nodes, nodes), f32), field, table, table]
        + kept
        + [stack_scratch, hot_scratch],
        copies=(8, 7),
        name="start",
    )
    if stride > 1:
        offset = landed(jnp.repeat(offset[:, 0], per).reshape(groups, LANES))
        filled = landed(jnp.repeat(filled[:, 0], per).reshape(groups, LANES))
    else:
        offset, filled = near(offset), near(filled)
    window = scalar(window)
    below, above = exchanged(low, high)

    harmonic, place, node, sample = call(
        functools.partial(node_kernel, stride),
        [box, window, landed(messages), offset, filled, near(chosen)],
        [
            ((groups, columns, LANES), f32, VMEM),
            (grid, i32, VMEM),
            ((5, groups, LANES), f32, VMEM),
            (grid, f32, None),
        ],
        [((groups, 8, LANES), f32)] * 2 + [((columns // 8, groups, LANES), f32)] * 2,
        name="nodes",
    )
    samples = lax.all_gather(sample, "box")

    modes = element_modes.reshape(1, elements)
    fetched = keys[1:] + [side, side, field, field, field, table, limits]
    step_scratch = [
        ((columns, count), f32),
        ((2 * columns, depth), bf16),
        hot_scratch,
        hot_scratch,
        field,
    ]
    sample, box_now, current, force, low, high = call(
        functools.partial(middle_kernel, stride),
        [
            box, window, landed(samples), near(node), near(place), near(harmonic),
            far(keycol), anywhere(below), anywhere(above), far(annulus), far(annulus_prev), far(force),
            far(node_mass), far(modes), far(key), far(forward), far(backward),
            far(radial_modulus), far(shear_modulus),
        ],
        [(grid, f32, None), (grid, f32, VMEM)]
        + [shape + (HBM,) for shape in (field, field, side, side)],
        fetched
        + keys[:1]
        + matrices
        + [table, table, field, side, side]
        + [(grid, f32)]
        + step_scratch
        + [stack_scratch, picked],
        copies=(13, 4),
        name="middle",
    )
    below, above = exchanged(low, high)
    samples = lax.all_gather(sample, "box")

    box_now, coefficient = call(
        box_kernel,
        [landed(samples), near(node), near(box_now)],
        [(grid, f32, None), (grid, f32, VMEM)],
        name="box",
    )
    returned = lax.all_to_all(
        box_now.reshape(mer_count, box_count, per), "mer", split_axis=0, concat_axis=0, tiled=True
    )
    returned = lax.dynamic_index_in_dim(
        returned, lax.axis_index("box"), axis=1, keepdims=False
    )
    (box_out,) = call(
        ungroup_kernel,
        [landed(part), landed(rank), landed(returned)],
        [((1, box_nodes), f32, None)],
        name="ungroup",
    )
    (current,) = call(
        functools.partial(last_kernel, stride),
        [
            box, window, near(coefficient), near(place), near(harmonic), far(keycol),
            anywhere(below), anywhere(above), far(current), far(annulus), far(force), far(node_mass), far(modes),
        ],
        [field + (HBM,)],
        fetched + [field] + step_scratch,
        copies=(8, nodes),
        name="last",
    )
    return current, box_out.reshape(box_nodes)


def solution(mesh):
    in_specs = (
        P(None, "box", "mer"),
        P(None, "box", "mer"),
        P(),
        P(None, "mer"),
        P(None, "mer"),
        P(None, "mer"),
        P("mer"),
        P("mer"),
        P("mer"),
        P("mer"),
        P("mer", None),
        P(("mer", "box")),
        P(("mer", "box")),
        P(("mer", "box")),
        P(("mer", "box")),
        P(("mer", "box")),
        P(("mer", "box")),
        P(("mer", "box")),
    )
    out_specs = (P(None, "box", "mer"), P(("mer", "box")))
    return jax.shard_map(
        per_device, mesh=mesh, in_specs=in_specs, out_specs=out_specs, check_vma=False
    )
```

time: 142 us -> 98.1 us (0.69)
  Pallas kernels: 97.2 us -> 53.4 us
  blocking collectives: 12.8 us -> 10.7 us
  waiting for transfers between devices: 3.44 us -> 4.97 us
    pallas_call x8 -> x7, Pallas kernels: 97.2 us -> 53.4 us  [call(): pl.pallas_call(kernel, out_shape=[memory(shape, dtype) if memory else jax...]
    all_gather x2, blocking collectives: 12.8 us -> 10.7 us  [per_device(): samples = lax.all_gather(sample, 'box')]
    ppermute x4, waiting for transfers between devices: 2.09 us -> 3.62 us  [exchanged(): return (lax.ppermute(high, 'mer', up), lax.ppermute(low, 'mer', down))]
    unnamed x10 -> x16, local copies, waits for them, and re-layouts: 1.99 us -> 3.34 us
  transfers between devices with their start and end apart: 6 -> 6, of which waited for: 2 -> 2; matrix products, arithmetic and copies ran while one was open for 0% -> 0% of each run, Pallas kernels for 25% -> 18%
where the time goes in v2:
time: 98.1 us; the launch traced here: 97.5 us
  Pallas kernels  53.4 us (54%)
  starting transfers between devices  24.2 us (25%)
  blocking collectives  10.7 us (11%)
  waiting for transfers between devices  4.97 us (5%)
  local copies, waits for them, and re-layouts  3.35 us (3%)
    pallas_call x7, Pallas kernels, call(): pl.pallas_call(kernel, out_shape=[memory(shape, dtype) if memory else jax...  53.4 us
    all_gather x2, blocking collectives, per_device(): samples = lax.all_gather(sample, 'box')  10.7 us
    ppermute x4, starting transfers between devices, exchanged(): return (lax.ppermute(high, 'mer', up), lax.ppermute(low, 'mer', down))  10.2 us
    all_to_all x1, starting transfers between devices, per_device(): lax.all_to_all(messages, ('mer', 'box'), split_axis=0, concat_axis=0, til...  7.33 us
    all_to_all x1, starting transfers between devices, per_device(): lax.all_to_all(box_now.reshape(mer_count, box_count, per), 'mer', split_a...  6.69 us
    ppermute x4, waiting for transfers between devices, exchanged(): return (lax.ppermute(high, 'mer', up), lax.ppermute(low, 'mer', down))  3.62 us
    unnamed x16, local copies, waits for them, and re-layouts  3.34 us
  transfers between devices with their start and end apart: 6, of which 2 were waited for; matrix products, arithmetic and copies ran while one was open for 0% of the time, Pallas kernels for 18%

profile of v2, /device:TPU:0, one launch (start us, length us, event | category | flops | bytes accessed | tf_op | source)
XLA Modules:
  0.0 97.5 jit_solution(17475765216036768997)
XLA Ops:
  0.6 2.2 %group.1 = (f32[32,8,128]{2,1,0:T(8,128)}, s32[1,1024]{1,0:T(1,128)}, s32[1,1024]{1,0:T(1,128)}) custom-call(s32[1,1024]{1,0:T(1,128)} %bitcast.23, f32[1,1024]{1,0:T(1,128)} %bitcast.24, f32[1,1024]{1,0:T(1,128)} %bitcast.25, f32[1,1024]{1,0:T(1,128)} %bitcast.26, f32[1,1024]{1,0:T(1,128)} %bitcast.27, f32[1,1024]{1,0:T(1,128)} %bitcast.28, f32[1,1024]{1,0:T(1,128)} %bitcast.29), custom_call_target="tpu_custom_call" | custom-call | tf_op jit(solution)/shard_map/group/pallas_call | solution.py:583
  2.8 7.3 %all-to-all-start = ((f32[32,8,128]{2,1,0:T(8,128)}), f32[32,8,128]{2,1,0:T(8,128)S(1)}, u32[]{:S(2)}, u32[]{:S(2)}) async-start(f32[32,8,128]{2,1,0:T(8,128)} %get-tuple-element.29), calls=%async_computation | async-start | bytes 262144 | tf_op jit(solution)/shard_map/all_to_all | solution.py:667
  10.2 11.5 %start.1 = (f32[32,128]{1,0:T(8,128)S(1)}, f32[32,128]{1,0:T(8,128)S(1)}, s32[32,128]{1,0:T(8,128)S(1)}, bf16[256,2048]{1,0:T(8,128)(2,1)S(1)}, s32[1,2560]{1,0:...) custom-call(s32[1]{0:T(128)} %bitcast.box_ref, ...), custom_call_target="tpu_custom_call" | custom-call | tf_op jit(solution)/shard_map/start/pallas_call | solution.py:583
  21.7 0.0 copy-start.2
  21.7 0.6 copy-done.2
  22.3 0.0 copy-start.4
  22.3 0.6 copy-done.4
  22.9 3.7 %collective-permute-start = (f32[128,256]{1,0:T(8,128)}, f32[128,256]{1,0:T(8,128)S(1)}, u32[]{:S(2)}, u32[]{:S(2)}) collective-permute-start(f32[128,256]{1,0:T(8,128)} %get-tuple-element.38), channel_id=1, source_target_pairs={{0,4},{4,8},{8,12},{12,16},{16,20},{20,24},{24,28},{1,5},{5,9},{9,... | collective-permute-start | bytes 393224 | tf_op jit(solution)/shard_map/ppermute | solution.py:572
  26.6 1.3 %collective-permute-start.1 = (f32[128,256]{1,0:T(8,128)}, f32[128,256]{1,0:T(8,128)S(1)}, u32[]{:S(2)}, u32[]{:S(2)}) collective-permute-start(f32[128,256]{1,0:T(8,128)} %get-tuple-element.39), channel_id=1, source_target_pairs={{4,0},{8,4},{12,8},{16,12},{20,16},{24,20},{28,24},{5,1},{9,5},{13... | collective-permute-start | bytes 393224 | tf_op jit(solution)/shard_map/ppermute | solution.py:572
  27.9 0.0 all-to-all-done.message_ref
  27.9 0.0 copy-start.3
  27.9 0.7 copy-done.3
  28.6 0.0 copy-start.5
  28.6 0.7 copy-done.5
  29.3 5.7 %nodes.1 = (f32[32,128,128]{2,1,0:T(8,128)S(1)}, s32[32,128]{1,0:T(8,128)S(1)}, f32[5,32,128]{2,1,0:T(8,128)S(1)}, f32[32,128]{1,0:T(8,128)S(1)}) custom-call(s32[1]{0:T(128)} %bitcast.box_ref, s32[32,128]{1,0:T(8,128)S(1)} %get-tuple-element.28.win_ref, f32[32,8,128]{2,1,0:T(8,128)S(1)} %all-to-all-done.message_ref, f32[32,128]{1,0:T(8,128)S(1)} %copy-done.3, ...), custom_call_target="tpu_custom_call" | custom-call | tf_op jit(solution)/shard_map/nodes/pallas_call | solution.py:583
  35.0 0.0 copy-start
  35.0 5.4 %all-gather = f32[128,128]{1,0:T(8,128)S(1)} all-gather(f32[32,128]{1,0:T(8,128)S(1)} %get-tuple-element.33), channel_id=2, replica_groups=mesh['mer'=8,'box'=4] {'box'}, dimensions={0}, use_global_device_ids=true | all-gather | bytes 81920 | tf_op jit(solution)/shard_map/all_gather | solution.py:731
  40.4 0.0 collective-permute-done.below_hbm
  40.4 0.0 collective-permute-done.1.above_hbm
  40.4 0.0 copy-start.6
  40.4 0.0 copy-start.7
  40.5 21.8 %middle.1 = (f32[32,128]{1,0:T(8,128)S(1)}, f32[32,128]{1,0:T(8,128)S(1)}, f32[25,128,128]{2,1,0:T(8,128)}, f32[25,128,128]{2,1,0:T(8,128)}, f32[128,256]{1,0:T(8,128)}, /*index=5*/f32[128,256]{1,0:T(8,128)}) custom-call(s32[1]{0:T(128)} %bitcast.box_ref, s32[32,128]{1,0:T(8,128)S(1)} %get-tuple-element.28.win_ref, f32[4,32,128]{2,1,0:T(8,128)S(1)} %bitcast.18, ...), custom_call_target="tpu_custom_call" | custom-call | tf_op jit(solution)/shard_map/middle/pallas_call | solution.py:583
  62.3 0.0 copy-done
  62.3 5.2 %all-gather.1 = f32[128,128]{1,0:T(8,128)S(1)} all-gather(f32[32,128]{1,0:T(8,128)S(1)} %get-tuple-element.44), channel_id=3, replica_groups=mesh['mer'=8,'box'=4] {'box'}, dimensions={0}, use_global_device_ids=true | all-gather | bytes 81920 | tf_op jit(solution)/shard_map/all_gather | solution.py:763
  67.5 0.6 box.1
  68.2 6.7 %all-to-all-start.1 = ((f32[8,4,128]{2,1,0:T(4,128)}), f32[8,4,128]{2,1,0:T(4,128)S(1)}, u32[]{:S(2)}, u32[]{:S(2)}) async-start(f32[8,4,128]{2,1,0:T(4,128)} %bitcast.15), calls=%async_computation.1 | async-start | bytes 32768 | tf_op jit(solution)/shard_map/all_to_all | solution.py:771
  74.8 3.9 %collective-permute-start.2 = (f32[128,256]{1,0:T(8,128)}, f32[128,256]{1,0:T(8,128)S(1)}, u32[]{:S(2)}, u32[]{:S(2)}) collective-permute-start(f32[128,256]{1,0:T(8,128)} %get-tuple-element.47), channel_id=1, source_target_pairs={{0,4},{4,8},{8,12},{12,16},{16,20},{20,24},{24,28},{1,5},{5,9},{9,... | collective-permute-start | bytes 393224 | tf_op jit(solution)/shard_map/ppermute | solution.py:572
  78.8 1.3 %collective-permute-start.3 = (f32[128,256]{1,0:T(8,128)}, f32[128,256]{1,0:T(8,128)S(1)}, u32[]{:S(2)}, u32[]{:S(2)}) collective-permute-start(f32[128,256]{1,0:T(8,128)} %get-tuple-element.48), channel_id=1, source_target_pairs={{4,0},{8,4},{12,8},{16,12},{20,16},{24,20},{28,24},{5,1},{9,5},{13... | collective-permute-start | bytes 393224 | tf_op jit(solution)/shard_map/ppermute | solution.py:572
  80.1 1.3 %all-to-all-done.1 = f32[8,4,128]{2,1,0:T(4,128)S(1)} async-done(((f32[8,4,128]{2,1,0:T(4,128)}), f32[8,4,128]{2,1,0:T(4,128)S(1)}, u32[]{:S(2)}, u32[]{:S(2)}) %all-to-all-start.1) | async-done | bytes 16416 | tf_op jit(solution)/shard_map/all_to_all | solution.py:771
  81.4 0.0 copy-done.6
  81.4 0.0 copy-done.7
  81.5 0.8 ungroup.1
  82.2 0.0 collective-permute-done.2.below_hbm
  82.2 3.6 %collective-permute-done.3.above_hbm = f32[128,256]{1,0:T(8,128)S(1)} collective-permute-done((f32[128,256]{1,0:T(8,128)}, f32[128,256]{1,0:T(8,128)S(1)}, u32[]{:S(2)}, u32[]{:S(2)}) %collective-permute-start.3) | collective-permute-done | bytes 131104 | tf_op jit(solution)/shard_map/ppermute | solution.py:572
  85.8 0.0 copy-start.1
  85.8 0.7 copy-done.1
  86.6 10.7 %last.1 = f32[25,128,128]{2,1,0:T(8,128)} custom-call(s32[1]{0:T(128)} %bitcast.box_ref, s32[32,128]{1,0:T(8,128)S(1)} %get-tuple-element.28.win_ref, f32[32,128]{1,0:T(8,128)S(1)} %get-tuple-element.46.coefficient_ref, s32[32,128]{1,0:T(8,128)S(1)} %copy-done.1, f32[32,128,128]{2,1,0:T(8,128)S(1)} %get-tuple-element.36.harmonic_ref, ...), custom_call_target="tpu_custom_call" | custom-call | tf_op jit(solution)/shard_map/last/pallas_call | solution.py:583
  (1 shorter events, 0.0 us)
Async XLA Ops:
  2.8 25.0 %all-to-all-start = ((f32[32,8,128]{2,1,0:T(8,128)}), f32[32,8,128]{2,1,0:T(8,128)S(1)}, u32[]{:S(2)}, u32[]{:S(2)}) async-start(f32[32,8,128]{2,1,0:T(8,128)} %get-tuple-element.29), calls=%async_computation | async-start | bytes 262144 | tf_op jit(solution)/shard_map/all_to_all | solution.py:667
  21.7 0.6 copy-start.2
  22.3 0.6 copy-start.4
  22.9 17.6 %collective-permute-start = (f32[128,256]{1,0:T(8,128)}, f32[128,256]{1,0:T(8,128)S(1)}, u32[]{:S(2)}, u32[]{:S(2)}) collective-permute-start(f32[128,256]{1,0:T(8,128)} %get-tuple-element.38), channel_id=1, source_target_pairs={{0,4},{4,8},{8,12},{12,16},{16,20},{20,24},{24,28},{1,5},{5,9},{9,... | collective-permute-start | bytes 393224 | tf_op jit(solution)/shard_map/ppermute | solution.py:572
  26.6 13.9 %collective-permute-start.1 = (f32[128,256]{1,0:T(8,128)}, f32[128,256]{1,0:T(8,128)S(1)}, u32[]{:S(2)}, u32[]{:S(2)}) collective-permute-start(f32[128,256]{1,0:T(8,128)} %get-tuple-element.39), channel_id=1, source_target_pairs={{4,0},{8,4},{12,8},{16,12},{20,16},{24,20},{28,24},{5,1},{9,5},{13... | collective-permute-start | bytes 393224 | tf_op jit(solution)/shard_map/ppermute | solution.py:572
  27.9 0.7 copy-start.3
  28.6 0.7 copy-start.5
  35.0 27.3 %copy-start = (s32[32,128]{1,0:T(8,128)}, s32[32,128]{1,0:T(8,128)S(1)}, u32[]{:S(2)}) copy-start(s32[32,128]{1,0:T(8,128)S(1)} %get-tuple-element.35.place_ref) | copy-start | bytes 49156
  40.4 41.0 %copy-start.6 = (s32[1,1024]{1,0:T(1,128)S(1)}, s32[1,1024]{1,0:T(1,128)}, u32[]{:S(2)}) copy-start(s32[1,1024]{1,0:T(1,128)} %get-tuple-element.51.part_ref) | copy-start | bytes 12292
  40.4 41.0 %copy-start.7 = (s32[1,1024]{1,0:T(1,128)S(1)}, s32[1,1024]{1,0:T(1,128)}, u32[]{:S(2)}) copy-start(s32[1,1024]{1,0:T(1,128)} %get-tuple-element.52.rank_ref) | copy-start | bytes 12292
  68.2 13.3 %all-to-all-start.1 = ((f32[8,4,128]{2,1,0:T(4,128)}), f32[8,4,128]{2,1,0:T(4,128)S(1)}, u32[]{:S(2)}, u32[]{:S(2)}) async-start(f32[8,4,128]{2,1,0:T(4,128)} %bitcast.15), calls=%async_computation.1 | async-start | bytes 32768 | tf_op jit(solution)/shard_map/all_to_all | solution.py:771
  74.8 7.4 %collective-permute-start.2 = (f32[128,256]{1,0:T(8,128)}, f32[128,256]{1,0:T(8,128)S(1)}, u32[]{:S(2)}, u32[]{:S(2)}) collective-permute-start(f32[128,256]{1,0:T(8,128)} %get-tuple-element.47), channel_id=1, source_target_pairs={{0,4},{4,8},{8,12},{12,16},{16,20},{20,24},{24,28},{1,5},{5,9},{9,... | collective-permute-start | bytes 393224 | tf_op jit(solution)/shard_map/ppermute | solution.py:572
  78.8 7.1 %collective-permute-start.3 = (f32[128,256]{1,0:T(8,128)}, f32[128,256]{1,0:T(8,128)S(1)}, u32[]{:S(2)}, u32[]{:S(2)}) collective-permute-start(f32[128,256]{1,0:T(8,128)} %get-tuple-element.48), channel_id=1, source_target_pairs={{4,0},{8,4},{12,8},{16,12},{20,16},{24,20},{28,24},{5,1},{9,5},{13... | collective-permute-start | bytes 393224 | tf_op jit(solution)/shard_map/ppermute | solution.py:572
  85.8 0.7 copy-start.1

commit v3 on v2

--- a/solution.py
+++ b/solution.py
@@ -11,7 +11,9 @@
 STEPS = 2
 LANES = 128
 WIDE = 256
-BATCH = 8
+BATCH = 16
+PAIRS = 6
+CHAINS = 4
 
 step_scale = 0.25
 f32 = jnp.float32
@@ -152,7 +154,7 @@
     off_ref[...] = offset
     cnt_ref[...] = totals
     window = jnp.floor(offset * (1.0 / LANES)) * LANES
-    win_ref[...] = jnp.minimum(window, count - WIDE).astype(i32)
+    win_ref[...] = jnp.minimum(window, count - WIDE).T[0:1, :].astype(i32)
     place = jnp.sum(mask * (before + offset[:, 0:1]), axis=0, keepdims=True)
     strip = jnp.floor((place + 0.5) * (1.0 / LANES))
     lane = (place - strip * LANES).astype(i32)
@@ -186,46 +188,42 @@
         stack_ref[:, tail] = jnp.zeros_like(stack_ref[:, tail])
 
 
-def picked(stack_ref, hot_ref, key_ref, start):
-    depth = stack_ref.shape[1]
+def picked(stack_ref, key_ref, start):
     key = key_ref[:, pl.ds(start, WIDE)]
     base = iota((LANES, WIDE), 0)
-    for row in range(0, depth, LANES):
-        hot_ref[row : row + LANES, :] = hot(base == key - row)
-    return dot(stack_ref[...], hot_ref[0:depth, :])
-
-
-def pick_rows(stack_ref, hot_ref, key_ref, out_ref):
+    chosen = [hot(base == key - row) for row in range(0, stack_ref.shape[1], LANES)]
+    return dot(stack_ref[...], jnp.concatenate(chosen, axis=0))
+
+
+def pick_rows(stack_ref, key_ref, out_ref):
     def body(index, carry):
-        start = pl.multiple_of(index * WIDE, WIDE)
-        out_ref[:, pl.ds(start, WIDE)] = picked(stack_ref, hot_ref, key_ref, start).astype(bf16)
+        for part in range(4):
+            start = pl.multiple_of((4 * index + part) * WIDE, WIDE)
+            out_ref[:, pl.ds(start, WIDE)] = picked(stack_ref, key_ref, start).astype(bf16)
         return carry
 
-    lax.fori_loop(0, out_ref.shape[1] // WIDE, body, 0)
-
-
-def pick_boundary(stack_ref, hot_ref, key_ref, low_ref, high_ref):
+    lax.fori_loop(0, out_ref.shape[1] // (4 * WIDE), body, 0)
+
+
+def pick_boundary(stack_ref, key_ref, low_ref, high_ref):
     shared = low_ref.shape[1]
     first = key_ref.shape[1] - 2 * shared
     for ref, origin in ((low_ref, first), (high_ref, first + shared)):
         for start in range(0, shared, WIDE):
-            ref[:, start : start + WIDE] = folded(
-                picked(stack_ref, hot_ref, key_ref, origin + start)
-            )
+            ref[:, start : start + WIDE] = folded(picked(stack_ref, key_ref, origin + start))
 
 
 def spread(derivative_ref, transposed, rows):
     nodes = derivative_ref.shape[0]
     size = 8 * nodes
-    left = jnp.where(iota((rows, nodes), 0) // 8 == iota((rows, nodes), 1), 1.0, 0.0)
-    right = jnp.where(iota((nodes, size), 1) // 8 == iota((nodes, size), 0), 1.0, 0.0)
-    dims = (((1,), (1,)), ((), ())) if transposed else (((1,), (0,)), ((), ()))
-    half = lax.dot_general(
-        left, derivative_ref[...], dims, precision=lax.Precision.HIGHEST, preferred_element_type=f32
-    )
-    full = jnp.dot(half, right, precision=lax.Precision.HIGHEST, preferred_element_type=f32)
-    full = jnp.where(iota((rows, size), 0) % 8 == iota((rows, size), 1) % 8, full, 0.0)
-    return stacked(full)
+    left = hot(iota((rows, nodes), 0) // 8 == iota((rows, nodes), 1))
+    right = hot(iota((nodes, size), 1) // 8 == iota((nodes, size), 0))
+    same = iota((rows, size), 0) % 8 == iota((rows, size), 1) % 8
+    parts = []
+    for term in split(derivative_ref[...]):
+        half = (dot_nt if transposed else dot)(left, term)
+        parts.append(jnp.where(same, dot(half.astype(bf16), right), 0.0))
+    return jnp.concatenate(parts, axis=0).astype(bf16)
 
 
 def force_into(value_ref, forward, backward, radial_ref, shear_ref, first_order, force_ref):
@@ -244,8 +242,8 @@
         return both[:size] + both[rows : rows + size] + dot(matrix[0:rows, :], low)[:size]
 
     def body(index, carry):
-        first = pl.multiple_of(index * 32, 32)
-        starts = [first, first + 16]
+        first = pl.multiple_of(index * 16 * CHAINS, 16 * CHAINS)
+        starts = [first + 16 * chain for chain in range(CHAINS)]
         halves = [
             [value_ref[:, pl.ds(start, 8), :], value_ref[:, pl.ds(start + 8, 8), :]]
             for start in starts
@@ -266,7 +264,7 @@
                 )
         return carry
 
-    lax.fori_loop(0, columns // 32, body, 0)
+    lax.fori_loop(0, columns // (16 * CHAINS), body, 0)
 
 
 def transfers(pairs, done):
@@ -289,11 +287,10 @@
 def start_kernel(
     elements, box_ref, target_hbm, rows_hbm, lower_hbm, upper_hbm, derivative_hbm,
     value_hbm, radial_hbm, shear_hbm,
-    off_ref, cnt_ref, win_ref, picked_ref,
-    key_hbm, keycol_hbm, forward_hbm, backward_hbm, force_hbm, low_hbm, high_hbm,
+    win_ref, off_hbm, cnt_hbm, picked_hbm, key_hbm, keycol_hbm, forward_hbm, backward_hbm, force_hbm, low_hbm, high_hbm,
     target_ref, rows_ref, lower_ref, upper_ref, derivative_ref, value_ref, radial_ref, shear_ref,
-    key_ref, keycol_ref, forward_ref, backward_ref, force_ref, low_ref, high_ref,
-    stack_ref, hot_ref, done, kept,
+    off_ref, cnt_ref, picked_ref, key_ref, keycol_ref, forward_ref, backward_ref, force_ref, low_ref,
+    high_ref, stack_ref, done, kept,
 ):
     moves = transfers(
         [
@@ -305,6 +302,7 @@
     )
     saves = transfers(
         [
+            (off_ref, off_hbm), (cnt_ref, cnt_hbm), (picked_ref, picked_hbm),
             (key_ref, key_hbm), (keycol_ref, keycol_hbm), (forward_ref, forward_hbm),
             (backward_ref, backward_hbm), (force_ref, force_hbm), (low_ref, low_hbm),
             (high_ref, high_hbm),
@@ -321,93 +319,108 @@
     rows = forward_ref.shape[0] // 2
     forward_ref[...] = spread(derivative_ref, False, rows)
     backward_ref[...] = spread(derivative_ref, True, rows)
-    begin(saves[:4])
+    begin(saves[:2] + saves[3:7])
     finish(moves[5:])
+    fill_stack(value_ref, stack_ref)
+    pick_rows(stack_ref, key_ref, picked_ref)
+    begin(saves[2:3])
     force_into(
         value_ref, forward_ref, backward_ref, radial_ref, shear_ref,
         box_ref[0] * columns % MODES, force_ref,
     )
-    begin(saves[4:5])
+    begin(saves[7:8])
     fill_stack(force_ref, stack_ref)
-    pick_boundary(stack_ref, hot_ref, key_ref, low_ref, high_ref)
-    begin(saves[5:])
-    fill_stack(value_ref, stack_ref)
-    pick_rows(stack_ref, hot_ref, key_ref, picked_ref)
+    pick_boundary(stack_ref, key_ref, low_ref, high_ref)
+    begin(saves[8:])
     finish(saves)
 
 
-def window_hot(win_ref, place_ref, group, stride):
-    window = pl.multiple_of(win_ref[group * stride, 0], LANES)
-    place = place_ref[pl.ds(group, 1), :]
+def window_hot(win_ref, harmonic_ref, group, stride):
+    window = pl.multiple_of(win_ref[0, group * stride], LANES)
+    columns = harmonic_ref.shape[1] - 8
+    place = harmonic_ref[group, columns : columns + 1, :].astype(i32)
     return window, hot(iota((WIDE, LANES), 0) + window == place)
 
 
-def sample_into(win_ref, place_ref, harmonic_ref, picked_ref, stride, sample_ref):
+def sample_into(win_ref, harmonic_ref, picked_ref, stride, sample_ref):
+    columns = harmonic_ref.shape[1] - 8
+
     def body(index, carry):
         for group in [BATCH * index + part for part in range(BATCH)]:
-            window, chosen = window_hot(win_ref, place_ref, group, stride)
+            window, chosen = window_hot(win_ref, harmonic_ref, group, stride)
             rows = folded(dot(picked_ref[:, pl.ds(window, WIDE)], chosen))
             sample_ref[pl.ds(group, 1), :] = jnp.sum(
-                rows * harmonic_ref[group], axis=0, keepdims=True
+                rows * harmonic_ref[group, 0:columns, :], axis=0, keepdims=True
             )
         return carry
 
     lax.fori_loop(0, sample_ref.shape[0] // BATCH, body, 0)
 
 
+def times(x, y):
+    return x[0] * y[0] - x[1] * y[1], x[0] * y[1] + x[1] * y[0]
+
+
 def node_kernel(
-    stride, box_ref, win_ref, message_ref, off_ref, cnt_ref, picked_ref,
-    harmonic_ref, place_ref, node_ref, sample_ref,
-    near_re, near_im, far_re, far_im,
+    stride, box_ref, win_ref, message_ref, off_hbm, cnt_hbm, picked_hbm,
+    harmonic_ref, node_ref, sample_ref,
+    off_ref, cnt_ref, picked_ref, place_ref, near_ref, far_re, far_im, done,
 ):
-    groups, columns, _ = harmonic_ref.shape
+    moves = transfers(
+        [(off_hbm, off_ref), (cnt_hbm, cnt_ref), (picked_hbm, picked_ref)], done
+    )
+    begin(moves)
+    groups, columns = harmonic_ref.shape[0], harmonic_ref.shape[1] - 8
     place = message_ref[:, 0, :]
     angle = message_ref[:, 1, :]
-    place_ref[...] = jnp.where(place < cnt_ref[...], off_ref[...] + place, -1.0).astype(i32)
     for index in range(5):
         node_ref[index] = message_ref[:, 2 + index, :]
-
-    def power(order):
-        return cos_sin(order * angle)
-
-    def times(x, y):
-        return x[0] * y[0] - x[1] * y[1], x[0] * y[1] + x[1] * y[0]
-
-    near = [(jnp.ones_like(angle), jnp.zeros_like(angle))] + [None] * 7
-    for bit in (1, 2, 4):
-        factor = power(float(bit))
-        near[bit] = factor
-        for low in range(1, bit):
-            near[bit + low] = times(factor, near[low])
-    for index, (re, im) in enumerate(near):
-        near_re[:, index, :] = re
-        near_im[:, index, :] = im
+    for bit in range(3):
+        re, im = cos_sin(float(1 << bit) * angle)
+        near_ref[2 * bit] = re
+        near_ref[2 * bit + 1] = im
     first = box_ref[0] * columns
-    base_re, base_im = power((first % MODES).astype(f32))
+    base_re, base_im = cos_sin((first % MODES).astype(f32) * angle)
     sine = first >= MODES
     far = [
         (jnp.where(sine, base_im, base_re), jnp.where(sine, -base_re, base_im))
     ] + [None] * (columns // 8 - 1)
     bit = 1
     while bit < columns // 8:
-        factor = power(float(8 * bit))
+        factor = cos_sin(float(8 * bit) * angle)
         for low in range(min(bit, columns // 8 - bit)):
             far[bit + low] = times(factor, far[low])
         bit *= 2
     for index, (re, im) in enumerate(far):
         far_re[index] = re
         far_im[index] = im
-
-    def body(group, carry):
-        re, im = near_re[group], near_im[group]
-        for index in range(columns // 8):
-            harmonic_ref[group, 8 * index : 8 * index + 8, :] = (
-                far_re[index, pl.ds(group, 1), :] * re - far_im[index, pl.ds(group, 1), :] * im
+    finish(moves[:2])
+    place_ref[...] = jnp.where(place < cnt_ref[...], off_ref[...] + place, -1.0)
+    order = iota((8, LANES), 0)
+
+    def body(index, carry):
+        for group in [4 * index + part for part in range(4)]:
+            row = pl.ds(group, 1)
+            powers = [
+                (
+                    jnp.where((order >> bit) & 1 == 1, near_ref[2 * bit, row, :], 1.0),
+                    jnp.where((order >> bit) & 1 == 1, near_ref[2 * bit + 1, row, :], 0.0),
+                )
+                for bit in range(3)
+            ]
+            re, im = times(times(powers[0], powers[1]), powers[2])
+            for step in range(columns // 8):
+                harmonic_ref[group, 8 * step : 8 * step + 8, :] = (
+                    far_re[step, row, :] * re - far_im[step, row, :] * im
+                )
+            harmonic_ref[group, columns : columns + 8, :] = jnp.broadcast_to(
+                place_ref[row, :], (8, LANES)
             )
         return carry
 
-    lax.fori_loop(0, groups, body, 0)
-    sample_into(win_ref, place_ref, harmonic_ref, picked_ref, stride, sample_ref)
+    lax.fori_loop(0, groups // 4, body, 0)
+    finish(moves[2:])
+    sample_into(win_ref, harmonic_ref, picked_ref, stride, sample_ref)
 
 
 def nodes_step(samples_ref, node_ref, now, before, next_ref, coefficient_ref):
@@ -419,54 +432,64 @@
     coefficient_ref[...] = -node_ref[2] * pull
 
 
-def annulus_step(
-    early, late, emit, stride, first_order, win_ref, place_ref, harmonic_ref, coefficient_ref, keycol_ref,
-    below_ref, above_ref, value_ref, previous_ref, force_ref, mass_ref, modes_ref,
-    next_ref, reaction_ref, terms_ref, hot_ref, hot2_ref, added_ref,
-):
-    nodes, columns, elements = value_ref.shape
-    groups = place_ref.shape[0]
-    count = reaction_ref.shape[1]
-    shared = below_ref.shape[1]
+def react_into(win_ref, harmonic_ref, coefficient_ref, stride, reaction_ref):
     reaction_ref[...] = jnp.zeros_like(reaction_ref)
+    columns = reaction_ref.shape[0]
 
     def react(index, carry):
         found = []
         for group in [BATCH * index + part for part in range(BATCH)]:
-            window, chosen = window_hot(win_ref, place_ref, group, stride)
-            weighted = harmonic_ref[group] * coefficient_ref[pl.ds(group, 1), :]
+            window, chosen = window_hot(win_ref, harmonic_ref, group, stride)
+            weighted = harmonic_ref[group, 0:columns, :] * coefficient_ref[pl.ds(group, 1), :]
             found.append((window, folded(dot_nt(stacked(weighted), chosen))))
         for window, rows in found:
             reaction_ref[:, pl.ds(window, WIDE)] = reaction_ref[:, pl.ds(window, WIDE)] + rows
         return carry
 
-    lax.fori_loop(0, groups // BATCH, react, 0)
+    lax.fori_loop(0, harmonic_ref.shape[0] // BATCH, react, 0)
+
+
+def place_into(terms_ref, keycol_ref, elements, nodes, added_ref):
+    depth = terms_ref.shape[1]
+    lane = iota((LANES, LANES), 1)
+
+    def place_rows(first, width):
+        sides = []
+        for side in range(width):
+            base = lane + (first + side) * elements
+            chosen = [
+                hot(keycol_ref[row : row + LANES, :] == base) for row in range(0, depth, LANES)
+            ]
+            sides.append(jnp.concatenate(chosen, axis=0))
+        rows = folded(dot(terms_ref[...], jnp.concatenate(sides, axis=1)))
+        for side in range(width):
+            added_ref[first + side] = rows[:, side * LANES : (side + 1) * LANES]
+
+    def place_many(index, carry):
+        for part in range(PAIRS):
+            place_rows(2 * (PAIRS * index + part), 2)
+        return carry
+
+    steps = nodes // (2 * PAIRS)
+    lax.fori_loop(0, steps, place_many, 0)
+    for first in range(2 * PAIRS * steps, nodes, 2):
+        place_rows(first, min(2, nodes - first))
+
+
+def annulus_step(
+    early, late, emit, stride, first_order, win_ref, harmonic_ref, coefficient_ref,
+    keycol_ref, below_ref, above_ref, value_ref, previous_ref, force_ref, mass_ref, modes_ref,
+    next_ref, reaction_ref, terms_ref, added_ref,
+):
+    nodes, columns, elements = value_ref.shape
+    count = reaction_ref.shape[1]
+    shared = below_ref.shape[1]
+    react_into(win_ref, harmonic_ref, coefficient_ref, stride, reaction_ref)
     finish(early)
     terms_ref[:, 0:count] = stacked(reaction_ref[...])
     terms_ref[:, count : count + shared] = stacked(below_ref[...])
     terms_ref[:, count + shared : count + 2 * shared] = stacked(above_ref[...])
-    depth = count + 2 * shared
-    lane = iota((LANES, LANES), 1)
-
-    def place_rows(first, width, buffer):
-        for side in range(width):
-            base = lane + (first + side) * elements
-            for row in range(0, depth, LANES):
-                buffer[row : row + LANES, side * LANES : (side + 1) * LANES] = hot(
-                    keycol_ref[row : row + LANES, :] == base
-                )
-        rows = folded(dot(terms_ref[...], buffer[0:depth, 0 : width * LANES]))
-        for side in range(width):
-            added_ref[first + side] = rows[:, side * LANES : (side + 1) * LANES]
-
-    def place_four(index, carry):
-        place_rows(4 * index, 2, hot_ref)
-        place_rows(4 * index + 2, 2, hot2_ref)
-        return carry
-
-    lax.fori_loop(0, nodes // 4, place_four, 0)
-    for first in range(nodes // 4 * 4, nodes, 2):
-        place_rows(first, min(2, nodes - first), hot_ref)
+    place_into(terms_ref, keycol_ref, elements, nodes, added_ref)
     order = first_order + iota((columns, elements), 0)
     finish(late)
     live = order < modes_ref[...]
@@ -481,14 +504,14 @@
 
 
 def middle_kernel(
-    stride, box_ref, win_ref, samples_ref, node_ref, place_ref, harmonic_ref,
+    stride, box_ref, win_ref, samples_ref, node_ref, harmonic_ref,
     keycol_hbm, below_hbm, above_hbm, value_hbm, previous_hbm, force_hbm, mass_hbm, modes_hbm,
     key_hbm, forward_hbm, backward_hbm, radial_hbm, shear_hbm,
     sample_ref, boxnext_ref, next_hbm, nextforce_hbm, low_hbm, high_hbm,
     keycol_ref, below_ref, above_ref, value_ref, previous_ref, force_ref, mass_ref, modes_ref,
     key_ref, forward_ref, backward_ref, radial_ref, shear_ref,
     next_ref, low_ref, high_ref,
-    coefficient_ref, reaction_ref, terms_ref, hot_ref, hot2_ref, added_ref, stack_ref, picked_ref,
+    coefficient_ref, reaction_ref, terms_ref, added_ref, stack_ref, picked_ref,
     done, kept,
 ):
     moves = transfers(
@@ -514,9 +537,9 @@
     nodes_step(samples_ref, node_ref, node_ref[3], node_ref[4], boxnext_ref, coefficient_ref)
     annulus_step(
         moves[:3], moves[3:], lambda node: None,
-        stride, first_order, win_ref, place_ref, harmonic_ref, coefficient_ref, keycol_ref,
+        stride, first_order, win_ref, harmonic_ref, coefficient_ref, keycol_ref,
         below_ref, above_ref, value_ref, previous_ref, force_ref, mass_ref, modes_ref,
-        next_ref, reaction_ref, terms_ref, hot_ref, hot2_ref, added_ref,
+        next_ref, reaction_ref, terms_ref, added_ref,
     )
     begin(saves[:1])
     force_into(
@@ -524,24 +547,28 @@
     )
     begin(saves[1:2])
     fill_stack(added_ref, stack_ref)
-    pick_boundary(stack_ref, hot_ref, key_ref, low_ref, high_ref)
+    pick_boundary(stack_ref, key_ref, low_ref, high_ref)
     begin(saves[2:])
     fill_stack(next_ref, stack_ref)
-    pick_rows(stack_ref, hot_ref, key_ref, picked_ref)
-    sample_into(win_ref, place_ref, harmonic_ref, picked_ref, stride, sample_ref)
+    pick_rows(stack_ref, key_ref, picked_ref)
+    sample_into(win_ref, harmonic_ref, picked_ref, stride, sample_ref)
     finish(saves)
 
 
-def box_kernel(samples_ref, node_ref, now_ref, boxnext_ref, coefficient_ref):
+def box_kernel(copies, box_ref, samples_ref, node_ref, now_ref, own_ref, coefficient_ref, *scratch):
+    boxnext_ref = scratch[0] if scratch else own_ref
     nodes_step(samples_ref, node_ref, now_ref[...], node_ref[3], boxnext_ref, coefficient_ref)
+    if scratch:
+        for index in range(own_ref.shape[0]):
+            own_ref[index : index + 1, :] = boxnext_ref[pl.ds(index * copies + box_ref[0], 1), :]
 
 
 def last_kernel(
-    stride, box_ref, win_ref, coefficient_ref, place_ref, harmonic_ref,
+    stride, box_ref, win_ref, coefficient_ref, harmonic_ref,
     keycol_hbm, below_hbm, above_hbm, value_hbm, previous_hbm, force_hbm, mass_hbm, modes_hbm,
     next_hbm,
     keycol_ref, below_ref, above_ref, value_ref, previous_ref, force_ref, mass_ref, modes_ref,
-    next_ref, reaction_ref, terms_ref, hot_ref, hot2_ref, added_ref, done, kept,
+    next_ref, reaction_ref, terms_ref, added_ref, done, kept,
 ):
     moves = transfers(
         [
@@ -558,9 +585,9 @@
     )
     annulus_step(
         moves[:3], moves[3:], lambda node: saves[node].start(),
-        stride, first_order, win_ref, place_ref, harmonic_ref, coefficient_ref, keycol_ref,
+        stride, first_order, win_ref, harmonic_ref, coefficient_ref, keycol_ref,
         below_ref, above_ref, value_ref, previous_ref, force_ref, mass_ref, modes_ref,
-        next_ref, reaction_ref, terms_ref, hot_ref, hot2_ref, added_ref,
+        next_ref, reaction_ref, terms_ref, added_ref,
     )
     finish(saves)
 
@@ -575,7 +602,7 @@
 SMEM, VMEM, HBM = pltpu.SMEM, pltpu.VMEM, pltpu.HBM
 
 
-def call(kernel, ins, outs, scratch=(), copies=(), name=None, limit=40):
+def call(kernel, ins, outs, scratch=(), copies=(), name=None, limit=40, flops=0):
     arrays = [
         pltpu.with_memory_space_constraint(array, memory) if pinned else array
         for array, memory, pinned in ins
@@ -591,6 +618,9 @@
         scratch_shapes=[VMEM(shape, dtype) for shape, dtype in scratch]
         + [pltpu.SemaphoreType.DMA((number,)) for number in copies],
         compiler_params=pltpu.CompilerParams(vmem_limit_bytes=limit << 20),
+        cost_estimate=pl.CostEstimate(flops=flops, transcendentals=0, bytes_accessed=0)
+        if flops
+        else None,
         name=name,
     )(*arrays)
 
@@ -631,7 +661,6 @@
     volume = (nodes, columns, elements)
     grid = (groups, LANES)
     flat = (nodes, elements)
-    hot_scratch = ((max(padded_nodes * elements, depth), WIDE), bf16)
     stack_scratch = ((2 * columns, padded_nodes * elements), bf16)
 
     def far(value):
@@ -669,7 +698,6 @@
         messages = messages.reshape(groups, stride, 8, per).swapaxes(1, 2)
         messages = messages.reshape(groups, 8, LANES)
 
-    expanded = VMEM if stride == 1 else None
     field = (volume, f32)
     table = (flat, f32)
     limits = ((1, elements), i32)
@@ -677,9 +705,10 @@
     keys = [((1, depth), i32), ((depth, LANES), i32)]
     matrices = [((2 * rows, 8 * nodes), bf16)] * 2
     picked = ((2 * columns, count), bf16)
-    kept = keys + matrices + [field, side, side]
+    counts = ((blocks, LANES), f32)
+    kept = [counts, counts, picked] + keys + matrices + [field, side, side]
     (
-        offset, filled, window, chosen, key, keycol, forward, backward, force, low, high,
+        window, offset, filled, chosen, key, keycol, forward, backward, force, low, high,
     ) = call(
         functools.partial(start_kernel, elements),
         [
@@ -694,39 +723,38 @@
             far(shear_modulus),
         ],
         [
-            ((blocks, LANES), f32, expanded),
-            ((blocks, LANES), f32, expanded),
-            ((blocks, LANES), i32, None),
-            picked + (VMEM,),
+            ((1, blocks), i32, None),
         ]
         + [shape + (HBM,) for shape in kept],
         [((1, count), i32)] * 2
         + [((1, shared), i32)] * 2
         + [((nodes, nodes), f32), field, table, table]
         + kept
-        + [stack_scratch, hot_scratch],
-        copies=(8, 7),
+        + [stack_scratch],
+        copies=(8, 10),
         name="start",
+        flops=4 * columns * nodes * elements * (count + 2 * shared),
     )
     if stride > 1:
-        offset = landed(jnp.repeat(offset[:, 0], per).reshape(groups, LANES))
-        filled = landed(jnp.repeat(filled[:, 0], per).reshape(groups, LANES))
-    else:
-        offset, filled = near(offset), near(filled)
+        offset = jnp.repeat(offset[:, 0], per).reshape(groups, LANES)
+        filled = jnp.repeat(filled[:, 0], per).reshape(groups, LANES)
     window = scalar(window)
     below, above = exchanged(low, high)
 
-    harmonic, place, node, sample = call(
+    harmonic, node, sample = call(
         functools.partial(node_kernel, stride),
-        [box, window, landed(messages), offset, filled, near(chosen)],
-        [
-            ((groups, columns, LANES), f32, VMEM),
-            (grid, i32, VMEM),
+        [box, window, landed(messages), far(offset), far(filled), far(chosen)],
+        [
+            ((groups, columns + 8, LANES), f32, VMEM),
             ((5, groups, LANES), f32, VMEM),
             (grid, f32, None),
         ],
-        [((groups, 8, LANES), f32)] * 2 + [((columns // 8, groups, LANES), f32)] * 2,
+        [(grid, f32), (grid, f32), picked, (grid, f32)]
+        + [((6, groups, LANES), f32)]
+        + [((columns // 8, groups, LANES), f32)] * 2,
+        copies=(3,),
         name="nodes",
+        flops=4 * columns * groups * LANES * WIDE,
     )
     samples = lax.all_gather(sample, "box")
 
@@ -735,14 +763,12 @@
     step_scratch = [
         ((columns, count), f32),
         ((2 * columns, depth), bf16),
-        hot_scratch,
-        hot_scratch,
         field,
     ]
     sample, box_now, current, force, low, high = call(
         functools.partial(middle_kernel, stride),
         [
-            box, window, landed(samples), near(node), near(place), near(harmonic),
+            box, window, landed(samples), near(node), near(harmonic),
             far(keycol), anywhere(below), anywhere(above), far(annulus), far(annulus_prev), far(force),
             far(node_mass), far(modes), far(key), far(forward), far(backward),
             far(radial_modulus), far(shear_modulus),
@@ -758,38 +784,42 @@
         + [stack_scratch, picked],
         copies=(13, 4),
         name="middle",
+        flops=8 * columns * nodes * elements * (count + 2 * shared),
     )
     below, above = exchanged(low, high)
     samples = lax.all_gather(sample, "box")
 
-    box_now, coefficient = call(
-        box_kernel,
-        [landed(samples), near(node), near(box_now)],
-        [(grid, f32, None), (grid, f32, VMEM)],
+    direct = stride == 1
+    returned, coefficient = call(
+        functools.partial(box_kernel, box_count),
+        [box, landed(samples), near(node), near(box_now)],
+        [((mer_count, per) if direct else grid, f32, None), (grid, f32, VMEM)],
+        [(grid, f32)] * direct,
         name="box",
     )
-    returned = lax.all_to_all(
-        box_now.reshape(mer_count, box_count, per), "mer", split_axis=0, concat_axis=0, tiled=True
-    )
-    returned = lax.dynamic_index_in_dim(
-        returned, lax.axis_index("box"), axis=1, keepdims=False
-    )
+    if not direct:
+        returned = lax.dynamic_index_in_dim(
+            returned.reshape(mer_count, box_count, per), lax.axis_index("box"), axis=1, keepdims=False
+        )
+    returned = lax.all_to_all(returned, "mer", split_axis=0, concat_axis=0, tiled=True)
+    (current,) = call(
+        functools.partial(last_kernel, stride),
+        [
+            box, window, near(coefficient), near(harmonic), far(keycol),
+            anywhere(below), anywhere(above), far(current), far(annulus), far(force), far(node_mass), far(modes),
+        ],
+        [field + (HBM,)],
+        fetched + [field] + step_scratch,
+        copies=(8, nodes),
+        name="last",
+        flops=4 * columns * nodes * elements * (count + 2 * shared),
+    )
+    current, returned = lax.optimization_barrier((current, returned))
     (box_out,) = call(
         ungroup_kernel,
         [landed(part), landed(rank), landed(returned)],
         [((1, box_nodes), f32, None)],
         name="ungroup",
-    )
-    (current,) = call(
-        functools.partial(last_kernel, stride),
-        [
-            box, window, near(coefficient), near(place), near(harmonic), far(keycol),
-            anywhere(below), anywhere(above), far(current), far(annulus), far(force), far(node_mass), far(modes),
-        ],
-        [field + (HBM,)],
-        fetched + [field] + step_scratch,
-        copies=(8, nodes),
-        name="last",
     )
     return current, box_out.reshape(box_nodes)
 

time: 98.1 us -> 82.9 us (0.85)
  Pallas kernels: 53.4 us -> 45.3 us
  waiting for transfers between devices: 4.97 us -> 0.02 us
  local copies, waits for them, and re-layouts: 3.35 us -> 0.01 us
  starting transfers between devices: 24.2 us -> 25.7 us
    pallas_call x7, Pallas kernels: 53.4 us -> 45.3 us  [call(): pl.pallas_call(kernel, out_shape=[memory(shape, dtype) if memory else jax...]
    ppermute x4, waiting for transfers between devices: 3.62 us -> 0.01 us  [exchanged(): return (lax.ppermute(high, 'mer', up), lax.ppermute(low, 'mer', down))]
    unnamed x16 -> x4, local copies, waits for them, and re-layouts: 3.34 us -> 0.01 us
    all_to_all x1, waiting for transfers between devices: 1.35 us -> 0.01 us  [per_device(): lax.all_to_all(returned, 'mer', split_axis=0, concat_axis=0, tiled=True)]
  transfers between devices with their start and end apart: 6 -> 6, of which waited for: 2 -> 0; matrix products, arithmetic and copies ran while one was open for 0% -> 0% of each run, Pallas kernels for 18% -> 30%
where the time goes in v3:
time: 82.9 us; the launch traced here: 82.5 us
  Pallas kernels  45.3 us (55%)
  starting transfers between devices  25.7 us (31%)
  blocking collectives  10.7 us (13%)
    pallas_call x7, Pallas kernels, call(): pl.pallas_call(kernel, out_shape=[memory(shape, dtype) if memory else jax...  45.3 us
    ppermute x4, starting transfers between devices, exchanged(): return (lax.ppermute(high, 'mer', up), lax.ppermute(low, 'mer', down))  10.8 us
    all_gather x2, blocking collectives, per_device(): samples = lax.all_gather(sample, 'box')  10.7 us
    all_to_all x1, starting transfers between devices, per_device(): lax.all_to_all(returned, 'mer', split_axis=0, concat_axis=0, tiled=True)  7.54 us
    all_to_all x1, starting transfers between devices, per_device(): lax.all_to_all(messages, ('mer', 'box'), split_axis=0, concat_axis=0, til...  7.33 us
  transfers between devices with their start and end apart: 6, of which 0 were waited for; matrix products, arithmetic and copies ran while one was open for 0% of the time, Pallas kernels for 30%

profile of v3, /device:TPU:0, one launch (start us, length us, event | category | flops | bytes accessed | tf_op | source)
XLA Modules:
  0.0 82.5 jit_solution(14385149444137617670)
XLA Ops:
  0.6 2.2 %group.1 = (f32[32,8,128]{2,1,0:T(8,128)}, s32[1,1024]{1,0:T(1,128)}, s32[1,1024]{1,0:T(1,128)}) custom-call(s32[1,1024]{1,0:T(1,128)} %bitcast.23, f32[1,1024]{1,0:T(1,128)} %bitcast.24, f32[1,1024]{1,0:T(1,128)} %bitcast.25, f32[1,1024]{1,0:T(1,128)} %bitcast.26, f32[1,1024]{1,0:T(1,128)} %bitcast.27, f32[1,1024]{1,0:T(1,128)} %bitcast.28, f32[1,1024]{1,0:T(1,128)} %bitcast.29), custom_call_target="tpu_custom_call" | custom-call | tf_op jit(solution)/shard_map/group/pallas_call | solution.py:610
  2.8 7.3 %all-to-all-start = ((f32[32,8,128]{2,1,0:T(8,128)}), f32[32,8,128]{2,1,0:T(8,128)S(1)}, u32[]{:S(2)}, u32[]{:S(2)}) async-start(f32[32,8,128]{2,1,0:T(8,128)} %get-tuple-element.30), calls=%async_computation | async-start | bytes 262144 | tf_op jit(solution)/shard_map/all_to_all | solution.py:696
  10.2 10.3 %start.1 = (s32[1,32]{1,0:T(1,128)S(1)}, f32[32,128]{1,0:T(8,128)}, f32[32,128]{1,0:T(8,128)}, bf16[256,2048]{1,0:T(8,128)(2,1)}, s32[1,2560]{1,0:T(1,128)}, /*i...) custom-call(s32[1]{0:T(128)} %bitcast.box_ref, ...), custom_call_target="tpu_custom_call" | custom-call | flops 4194304000 | tf_op jit(solution)/shard_map/start/pallas_call | solution.py:610
  20.5 3.7 %collective-permute-start = (f32[128,256]{1,0:T(8,128)}, f32[128,256]{1,0:T(8,128)S(1)}, u32[]{:S(2)}, u32[]{:S(2)}) collective-permute-start(f32[128,256]{1,0:T(8,128)} %get-tuple-element.38), channel_id=1, source_target_pairs={{0,4},{4,8},{8,12},{12,16},{16,20},{20,24},{24,28},{1,5},{5,9},{9,... | collective-permute-start | bytes 393224 | tf_op jit(solution)/shard_map/ppermute | solution.py:599
  24.2 1.3 %collective-permute-start.1 = (f32[128,256]{1,0:T(8,128)}, f32[128,256]{1,0:T(8,128)S(1)}, u32[]{:S(2)}, u32[]{:S(2)}) collective-permute-start(f32[128,256]{1,0:T(8,128)} %get-tuple-element.39), channel_id=1, source_target_pairs={{4,0},{8,4},{12,8},{16,12},{20,16},{24,20},{28,24},{5,1},{9,5},{13... | collective-permute-start | bytes 393224 | tf_op jit(solution)/shard_map/ppermute | solution.py:599
  25.5 0.0 all-to-all-done.message_ref
  25.5 4.9 %nodes.1 = (f32[32,136,128]{2,1,0:T(8,128)S(1)}, f32[5,32,128]{2,1,0:T(8,128)S(1)}, f32[32,128]{1,0:T(8,128)S(1)}) custom-call(s32[1]{0:T(128)} %bitcast.box_ref, s32[1,32]{1,0:T(1,128)S(1)} %get-tuple-element.29.win_ref, f32[32,8,128]{2,1,0:T(8,128)S(1)} %all-to-all-done.message_ref, f32[32,128]{1,0:T(8,128)} %get-tuple-element.31.off_hbm, ...), custom_call_target="tpu_custom_call" | custom-call | flops 536870912 | tf_op jit(solution)/shard_map/nodes/pallas_call | solution.py:610
  30.4 5.4 %all-gather = f32[128,128]{1,0:T(8,128)S(1)} all-gather(f32[32,128]{1,0:T(8,128)S(1)} %get-tuple-element.34), channel_id=2, replica_groups=mesh['mer'=8,'box'=4] {'box'}, dimensions={0}, use_global_device_ids=true | all-gather | bytes 81920 | tf_op jit(solution)/shard_map/all_gather | solution.py:759
  35.8 0.0 collective-permute-done.below_hbm
  35.8 0.0 collective-permute-done.1.above_hbm
  35.8 17.5 %middle.1 = (f32[32,128]{1,0:T(8,128)S(1)}, f32[32,128]{1,0:T(8,128)S(1)}, f32[25,128,128]{2,1,0:T(8,128)}, f32[25,128,128]{2,1,0:T(8,128)}, f32[128,256]{1,0:T(8,128)}, /*index=5*/f32[128,256]{1,0:T(8,128)}) custom-call(s32[1]{0:T(128)} %bitcast.box_ref, s32[1,32]{1,0:T(1,128)S(1)} %get-tuple-element.29.win_ref, f32[4,32,128]{2,1,0:T(8,128)S(1)} %bitcast.21, ...), custom_call_target="tpu_custom_call" | custom-call | flops 8388608000 | tf_op jit(solution)/shard_map/middle/pallas_call | solution.py:610
  53.3 4.6 %collective-permute-start.2 = (f32[128,256]{1,0:T(8,128)}, f32[128,256]{1,0:T(8,128)S(1)}, u32[]{:S(2)}, u32[]{:S(2)}) collective-permute-start(f32[128,256]{1,0:T(8,128)} %get-tuple-element.47), channel_id=1, source_target_pairs={{0,4},{4,8},{8,12},{12,16},{16,20},{20,24},{24,28},{1,5},{5,9},{9,... | collective-permute-start | bytes 393224 | tf_op jit(solution)/shard_map/ppermute | solution.py:599
  57.9 1.3 %collective-permute-start.3 = (f32[128,256]{1,0:T(8,128)}, f32[128,256]{1,0:T(8,128)S(1)}, u32[]{:S(2)}, u32[]{:S(2)}) collective-permute-start(f32[128,256]{1,0:T(8,128)} %get-tuple-element.48), channel_id=1, source_target_pairs={{4,0},{8,4},{12,8},{16,12},{20,16},{24,20},{28,24},{5,1},{9,5},{13... | collective-permute-start | bytes 393224 | tf_op jit(solution)/shard_map/ppermute | solution.py:599
  59.2 5.2 %all-gather.1 = f32[128,128]{1,0:T(8,128)S(1)} all-gather(f32[32,128]{1,0:T(8,128)S(1)} %get-tuple-element.44), channel_id=3, replica_groups=mesh['mer'=8,'box'=4] {'box'}, dimensions={0}, use_global_device_ids=true | all-gather | bytes 81920 | tf_op jit(solution)/shard_map/all_gather | solution.py:790
  64.4 0.6 box.1
  65.0 7.5 %all-to-all-start.1 = ((f32[8,1,128]{2,1,0:T(1,128)}), f32[8,1,128]{2,1,0:T(1,128)S(1)}, u32[]{:S(2)}, u32[]{:S(2)}) async-start(f32[8,1,128]{2,1,0:T(1,128)} %bitcast.16), calls=%async_computation.1 | async-start | bytes 8192 | tf_op jit(solution)/shard_map/all_to_all | solution.py:804
  72.6 0.0 collective-permute-done.2.below_hbm
  72.6 0.0 collective-permute-done.3.above_hbm
  72.6 0.0 copy-start
  72.6 0.0 copy-start.1
  72.6 9.1 %last.1 = f32[25,128,128]{2,1,0:T(8,128)} custom-call(s32[1]{0:T(128)} %bitcast.box_ref, s32[1,32]{1,0:T(1,128)S(1)} %get-tuple-element.29.win_ref, f32[32,128]{1,0:T(8,128)S(1)} %get-tuple-element.46.coefficient_ref, f32[32,136,128]{2,1,0:T(8,128)S(1)} %get-tuple-element.36.harmonic_ref, s32[2560,128]{1,0:T(8,128)} %get-tuple-element.37.keycol_hbm, ...), custom_call_target="tpu_custom_call" | custom-call | flops 4194304000 | tf_op jit(solution)/shard_map/last/pallas_call | solution.py:610
  81.7 0.0 all-to-all-done.1
  81.7 0.0 copy-done
  81.7 0.0 copy-done.1
  81.7 0.8 ungroup.1
Async XLA Ops:
  2.8 22.6 %all-to-all-start = ((f32[32,8,128]{2,1,0:T(8,128)}), f32[32,8,128]{2,1,0:T(8,128)S(1)}, u32[]{:S(2)}, u32[]{:S(2)}) async-start(f32[32,8,128]{2,1,0:T(8,128)} %get-tuple-element.30), calls=%async_computation | async-start | bytes 262144 | tf_op jit(solution)/shard_map/all_to_all | solution.py:696
  20.5 15.3 %collective-permute-start = (f32[128,256]{1,0:T(8,128)}, f32[128,256]{1,0:T(8,128)S(1)}, u32[]{:S(2)}, u32[]{:S(2)}) collective-permute-start(f32[128,256]{1,0:T(8,128)} %get-tuple-element.38), channel_id=1, source_target_pairs={{0,4},{4,8},{8,12},{12,16},{16,20},{20,24},{24,28},{1,5},{5,9},{9,... | collective-permute-start | bytes 393224 | tf_op jit(solution)/shard_map/ppermute | solution.py:599
  24.2 11.7 %collective-permute-start.1 = (f32[128,256]{1,0:T(8,128)}, f32[128,256]{1,0:T(8,128)S(1)}, u32[]{:S(2)}, u32[]{:S(2)}) collective-permute-start(f32[128,256]{1,0:T(8,128)} %get-tuple-element.39), channel_id=1, source_target_pairs={{4,0},{8,4},{12,8},{16,12},{20,16},{24,20},{28,24},{5,1},{9,5},{13... | collective-permute-start | bytes 393224 | tf_op jit(solution)/shard_map/ppermute | solution.py:599
  53.3 19.2 %collective-permute-start.2 = (f32[128,256]{1,0:T(8,128)}, f32[128,256]{1,0:T(8,128)S(1)}, u32[]{:S(2)}, u32[]{:S(2)}) collective-permute-start(f32[128,256]{1,0:T(8,128)} %get-tuple-element.47), channel_id=1, source_target_pairs={{0,4},{4,8},{8,12},{12,16},{16,20},{20,24},{24,28},{1,5},{5,9},{9,... | collective-permute-start | bytes 393224 | tf_op jit(solution)/shard_map/ppermute | solution.py:599
  57.9 14.7 %collective-permute-start.3 = (f32[128,256]{1,0:T(8,128)}, f32[128,256]{1,0:T(8,128)S(1)}, u32[]{:S(2)}, u32[]{:S(2)}) collective-permute-start(f32[128,256]{1,0:T(8,128)} %get-tuple-element.48), channel_id=1, source_target_pairs={{4,0},{8,4},{12,8},{16,12},{20,16},{24,20},{28,24},{5,1},{9,5},{13... | collective-permute-start | bytes 393224 | tf_op jit(solution)/shard_map/ppermute | solution.py:599
  65.0 16.7 %all-to-all-start.1 = ((f32[8,1,128]{2,1,0:T(1,128)}), f32[8,1,128]{2,1,0:T(1,128)S(1)}, u32[]{:S(2)}, u32[]{:S(2)}) async-start(f32[8,1,128]{2,1,0:T(1,128)} %bitcast.16), calls=%async_computation.1 | async-start | bytes 8192 | tf_op jit(solution)/shard_map/all_to_all | solution.py:804
  72.6 9.1 %copy-start = (s32[1,1024]{1,0:T(1,128)S(1)}, s32[1,1024]{1,0:T(1,128)}, u32[]{:S(2)}) copy-start(s32[1,1024]{1,0:T(1,128)} %get-tuple-element.53.part_ref) | copy-start | bytes 12292
  72.6 9.1 %copy-start.1 = (s32[1,1024]{1,0:T(1,128)S(1)}, s32[1,1024]{1,0:T(1,128)}, u32[]{:S(2)}) copy-start(s32[1,1024]{1,0:T(1,128)} %get-tuple-element.54.rank_ref) | copy-start | bytes 12292

commit v4 on v3

--- a/solution.py
+++ b/solution.py
@@ -12,6 +12,7 @@
 LANES = 128
 WIDE = 256
 BATCH = 16
+SAMPLES = 32
 PAIRS = 6
 CHAINS = 4
 
@@ -226,7 +227,10 @@
     return jnp.concatenate(parts, axis=0).astype(bf16)
 
 
-def force_into(value_ref, forward, backward, radial_ref, shear_ref, first_order, force_ref):
+def force_into(
+    value_ref, previous_ref, forward, backward, radial_ref, shear_ref, mass_ref, modes_ref,
+    first_order, force_ref, drift_ref,
+):
     nodes, columns, elements = value_ref.shape
     size = 8 * nodes
     rows = forward.shape[0] // 2
@@ -235,6 +239,7 @@
     )
     radial = jnp.concatenate([radial, radial], axis=1)
     shear = jnp.broadcast_to(shear_ref[...][:, None, :], (nodes, 8, elements))
+    scale = jnp.broadcast_to((step_scale / mass_ref[...])[:, None, :], (nodes, 8, elements))
 
     def applied(matrix, x):
         high, low = split(x)
@@ -256,12 +261,14 @@
         backs = [applied(backward, flux) for flux in fluxes]
         for start, pair, back in zip(starts, halves, backs):
             for side, half in enumerate(pair):
-                order = (first_order + start + 8 * side + iota((8, elements), 0)).astype(f32)
-                wave = (2.0 * order / MODES) ** 2
+                part = pl.ds(start + 8 * side, 8)
+                order = first_order + start + 8 * side + iota((8, elements), 0)
+                wave = (2.0 * order.astype(f32) / MODES) ** 2
                 block = back[:, side * elements : (side + 1) * elements]
-                force_ref[:, pl.ds(start + 8 * side, 8), :] = (
-                    -block.reshape(nodes, 8, elements) - shear * wave[None] * half
-                )
+                force = -block.reshape(nodes, 8, elements) - shear * wave[None] * half
+                gain = jnp.where((order < modes_ref[...])[None], scale, 0.0)
+                force_ref[:, part, :] = force
+                drift_ref[:, part, :] = 2.0 * half - previous_ref[:, part, :] + gain * force
         return carry
 
     lax.fori_loop(0, columns // (16 * CHAINS), body, 0)
@@ -286,17 +293,19 @@
 
 def start_kernel(
     elements, box_ref, target_hbm, rows_hbm, lower_hbm, upper_hbm, derivative_hbm,
-    value_hbm, radial_hbm, shear_hbm,
-    win_ref, off_hbm, cnt_hbm, picked_hbm, key_hbm, keycol_hbm, forward_hbm, backward_hbm, force_hbm, low_hbm, high_hbm,
+    value_hbm, radial_hbm, shear_hbm, mass_hbm, modes_hbm, previous_hbm,
+    win_ref, off_hbm, cnt_hbm, picked_hbm, key_hbm, keycol_hbm, forward_hbm, backward_hbm, drift_hbm, low_hbm, high_hbm,
     target_ref, rows_ref, lower_ref, upper_ref, derivative_ref, value_ref, radial_ref, shear_ref,
-    off_ref, cnt_ref, picked_ref, key_ref, keycol_ref, forward_ref, backward_ref, force_ref, low_ref,
-    high_ref, stack_ref, done, kept,
+    mass_ref, modes_ref, previous_ref,
+    off_ref, cnt_ref, picked_ref, key_ref, keycol_ref, forward_ref, backward_ref, drift_ref, low_ref,
+    high_ref, force_ref, stack_ref, done, kept,
 ):
     moves = transfers(
         [
             (target_hbm, target_ref), (rows_hbm, rows_ref), (lower_hbm, lower_ref),
             (upper_hbm, upper_ref), (derivative_hbm, derivative_ref), (value_hbm, value_ref),
-            (radial_hbm, radial_ref), (shear_hbm, shear_ref),
+            (radial_hbm, radial_ref), (shear_hbm, shear_ref), (mass_hbm, mass_ref),
+            (modes_hbm, modes_ref), (previous_hbm, previous_ref),
         ],
         done,
     )
@@ -304,7 +313,7 @@
         [
             (off_ref, off_hbm), (cnt_ref, cnt_hbm), (picked_ref, picked_hbm),
             (key_ref, key_hbm), (keycol_ref, keycol_hbm), (forward_ref, forward_hbm),
-            (backward_ref, backward_hbm), (force_ref, force_hbm), (low_ref, low_hbm),
+            (backward_ref, backward_hbm), (drift_ref, drift_hbm), (low_ref, low_hbm),
             (high_ref, high_hbm),
         ],
         kept,
@@ -320,13 +329,14 @@
     forward_ref[...] = spread(derivative_ref, False, rows)
     backward_ref[...] = spread(derivative_ref, True, rows)
     begin(saves[:2] + saves[3:7])
-    finish(moves[5:])
+    finish(moves[5:6])
     fill_stack(value_ref, stack_ref)
     pick_rows(stack_ref, key_ref, picked_ref)
     begin(saves[2:3])
+    finish(moves[6:])
     force_into(
-        value_ref, forward_ref, backward_ref, radial_ref, shear_ref,
-        box_ref[0] * columns % MODES, force_ref,
+        value_ref, previous_ref, forward_ref, backward_ref, radial_ref, shear_ref, mass_ref,
+        modes_ref, box_ref[0] * columns % MODES, force_ref, drift_ref,
     )
     begin(saves[7:8])
     fill_stack(force_ref, stack_ref)
@@ -346,7 +356,7 @@
     columns = harmonic_ref.shape[1] - 8
 
     def body(index, carry):
-        for group in [BATCH * index + part for part in range(BATCH)]:
+        for group in [SAMPLES * index + part for part in range(SAMPLES)]:
             window, chosen = window_hot(win_ref, harmonic_ref, group, stride)
             rows = folded(dot(picked_ref[:, pl.ds(window, WIDE)], chosen))
             sample_ref[pl.ds(group, 1), :] = jnp.sum(
@@ -354,7 +364,7 @@
             )
         return carry
 
-    lax.fori_loop(0, sample_ref.shape[0] // BATCH, body, 0)
+    lax.fori_loop(0, sample_ref.shape[0] // SAMPLES, body, 0)
 
 
 def times(x, y):
@@ -449,7 +459,7 @@
     lax.fori_loop(0, harmonic_ref.shape[0] // BATCH, react, 0)
 
 
-def place_into(terms_ref, keycol_ref, elements, nodes, added_ref):
+def place_into(terms_ref, keycol_ref, elements, nodes, emit, flush):
     depth = terms_ref.shape[1]
     lane = iota((LANES, LANES), 1)
 
@@ -463,25 +473,28 @@
             sides.append(jnp.concatenate(chosen, axis=0))
         rows = folded(dot(terms_ref[...], jnp.concatenate(sides, axis=1)))
         for side in range(width):
-            added_ref[first + side] = rows[:, side * LANES : (side + 1) * LANES]
+            emit(first + side, rows[:, side * LANES : (side + 1) * LANES])
 
     def place_many(index, carry):
         for part in range(PAIRS):
             place_rows(2 * (PAIRS * index + part), 2)
+        flush(2 * PAIRS * index, 2 * PAIRS, index)
         return carry
 
     steps = nodes // (2 * PAIRS)
     lax.fori_loop(0, steps, place_many, 0)
     for first in range(2 * PAIRS * steps, nodes, 2):
         place_rows(first, min(2, nodes - first))
+    if nodes > 2 * PAIRS * steps:
+        flush(2 * PAIRS * steps, nodes - 2 * PAIRS * steps, steps)
 
 
 def annulus_step(
-    early, late, emit, stride, first_order, win_ref, harmonic_ref, coefficient_ref,
-    keycol_ref, below_ref, above_ref, value_ref, previous_ref, force_ref, mass_ref, modes_ref,
-    next_ref, reaction_ref, terms_ref, added_ref,
+    early, late, after, flush, stride, first_order, win_ref, harmonic_ref, coefficient_ref,
+    keycol_ref, below_ref, above_ref, drift_ref, mass_ref, modes_ref,
+    next_ref, reaction_ref, terms_ref,
 ):
-    nodes, columns, elements = value_ref.shape
+    nodes, columns, elements = drift_ref.shape
     count = reaction_ref.shape[1]
     shared = below_ref.shape[1]
     react_into(win_ref, harmonic_ref, coefficient_ref, stride, reaction_ref)
@@ -489,36 +502,34 @@
     terms_ref[:, 0:count] = stacked(reaction_ref[...])
     terms_ref[:, count : count + shared] = stacked(below_ref[...])
     terms_ref[:, count + shared : count + 2 * shared] = stacked(above_ref[...])
-    place_into(terms_ref, keycol_ref, elements, nodes, added_ref)
-    order = first_order + iota((columns, elements), 0)
     finish(late)
-    live = order < modes_ref[...]
-    for node in range(nodes):
-        gain = jnp.where(live, step_scale / mass_ref[node : node + 1, :], 0.0)
-        next_ref[node] = (
-            2.0 * value_ref[node]
-            - previous_ref[node]
-            + gain * (force_ref[node] + added_ref[node])
-        )
-        emit(node)
+    live = first_order + iota((columns, elements), 0) < modes_ref[...]
+
+    def emit(node, added):
+        gain = jnp.where(live, step_scale / mass_ref[pl.ds(node, 1), :], 0.0)
+        value = drift_ref[node] + gain * added
+        next_ref[node] = value
+        after(node, value)
+
+    place_into(terms_ref, keycol_ref, elements, nodes, emit, flush)
 
 
 def middle_kernel(
     stride, box_ref, win_ref, samples_ref, node_ref, harmonic_ref,
-    keycol_hbm, below_hbm, above_hbm, value_hbm, previous_hbm, force_hbm, mass_hbm, modes_hbm,
-    key_hbm, forward_hbm, backward_hbm, radial_hbm, shear_hbm,
-    sample_ref, boxnext_ref, next_hbm, nextforce_hbm, low_hbm, high_hbm,
-    keycol_ref, below_ref, above_ref, value_ref, previous_ref, force_ref, mass_ref, modes_ref,
-    key_ref, forward_ref, backward_ref, radial_ref, shear_ref,
+    keycol_hbm, below_hbm, above_hbm, drift_hbm, mass_hbm, modes_hbm,
+    value_hbm, key_hbm, forward_hbm, backward_hbm, radial_hbm, shear_hbm,
+    sample_ref, boxnext_ref, nextdrift_hbm, low_hbm, high_hbm,
+    keycol_ref, below_ref, above_ref, drift_ref, mass_ref, modes_ref,
+    value_ref, key_ref, forward_ref, backward_ref, radial_ref, shear_ref,
     next_ref, low_ref, high_ref,
-    coefficient_ref, reaction_ref, terms_ref, added_ref, stack_ref, picked_ref,
+    coefficient_ref, reaction_ref, terms_ref, force_ref, stack_ref, picked_ref,
     done, kept,
 ):
     moves = transfers(
         [
             (keycol_hbm, keycol_ref), (below_hbm, below_ref), (above_hbm, above_ref),
-            (value_hbm, value_ref), (previous_hbm, previous_ref), (force_hbm, force_ref),
-            (mass_hbm, mass_ref), (modes_hbm, modes_ref), (key_hbm, key_ref),
+            (drift_hbm, drift_ref), (mass_hbm, mass_ref), (modes_hbm, modes_ref),
+            (value_hbm, value_ref), (key_hbm, key_ref),
             (forward_hbm, forward_ref), (backward_hbm, backward_ref), (radial_hbm, radial_ref),
             (shear_hbm, shear_ref),
         ],
@@ -526,8 +537,7 @@
     )
     saves = transfers(
         [
-            (next_ref, next_hbm), (added_ref, nextforce_hbm), (low_ref, low_hbm),
-            (high_ref, high_hbm),
+            (drift_ref, nextdrift_hbm), (low_ref, low_hbm), (high_ref, high_hbm),
         ],
         kept,
     )
@@ -535,22 +545,33 @@
     columns = value_ref.shape[1]
     first_order = box_ref[0] * columns % MODES
     nodes_step(samples_ref, node_ref, node_ref[3], node_ref[4], boxnext_ref, coefficient_ref)
+    elements = value_ref.shape[2]
+    if stack_ref.shape[1] > value_ref.shape[0] * elements:
+        tail = slice(value_ref.shape[0] * elements, stack_ref.shape[1])
+        stack_ref[:, tail] = jnp.zeros_like(stack_ref[:, tail])
+
+    def after(node, value):
+        lanes = pl.ds(pl.multiple_of(node * elements, elements), elements)
+        high, low = split(value)
+        stack_ref[0:columns, lanes] = high
+        stack_ref[columns:, lanes] = low
+
     annulus_step(
-        moves[:3], moves[3:], lambda node: None,
+        moves[:3], moves[3:6], after, lambda first, size, index: None,
         stride, first_order, win_ref, harmonic_ref, coefficient_ref, keycol_ref,
-        below_ref, above_ref, value_ref, previous_ref, force_ref, mass_ref, modes_ref,
-        next_ref, reaction_ref, terms_ref, added_ref,
+        below_ref, above_ref, drift_ref, mass_ref, modes_ref,
+        next_ref, reaction_ref, terms_ref,
+    )
+    finish(moves[6:])
+    pick_rows(stack_ref, key_ref, picked_ref)
+    force_into(
+        next_ref, value_ref, forward_ref, backward_ref, radial_ref, shear_ref, mass_ref,
+        modes_ref, first_order, force_ref, drift_ref,
     )
     begin(saves[:1])
-    force_into(
-        next_ref, forward_ref, backward_ref, radial_ref, shear_ref, first_order, added_ref
-    )
-    begin(saves[1:2])
-    fill_stack(added_ref, stack_ref)
+    fill_stack(force_ref, stack_ref)
     pick_boundary(stack_ref, key_ref, low_ref, high_ref)
-    begin(saves[2:])
-    fill_stack(next_ref, stack_ref)
-    pick_rows(stack_ref, key_ref, picked_ref)
+    begin(saves[1:])
     sample_into(win_ref, harmonic_ref, picked_ref, stride, sample_ref)
     finish(saves)
 
@@ -565,31 +586,40 @@
 
 def last_kernel(
     stride, box_ref, win_ref, coefficient_ref, harmonic_ref,
-    keycol_hbm, below_hbm, above_hbm, value_hbm, previous_hbm, force_hbm, mass_hbm, modes_hbm,
+    keycol_hbm, below_hbm, above_hbm, drift_hbm, mass_hbm, modes_hbm,
     next_hbm,
-    keycol_ref, below_ref, above_ref, value_ref, previous_ref, force_ref, mass_ref, modes_ref,
-    next_ref, reaction_ref, terms_ref, added_ref, done, kept,
+    keycol_ref, below_ref, above_ref, drift_ref, mass_ref, modes_ref,
+    next_ref, reaction_ref, terms_ref, done, kept,
 ):
     moves = transfers(
         [
             (keycol_hbm, keycol_ref), (below_hbm, below_ref), (above_hbm, above_ref),
-            (value_hbm, value_ref), (previous_hbm, previous_ref), (force_hbm, force_ref),
-            (mass_hbm, mass_ref), (modes_hbm, modes_ref),
+            (drift_hbm, drift_ref), (mass_hbm, mass_ref), (modes_hbm, modes_ref),
         ],
         done,
     )
     begin(moves)
-    first_order = box_ref[0] * value_ref.shape[1] % MODES
-    saves = transfers(
-        [(next_ref.at[node], next_hbm.at[node]) for node in range(value_ref.shape[0])], kept
-    )
+    first_order = box_ref[0] * drift_ref.shape[1] % MODES
+
+    def save(first, size, index):
+        part = pl.ds(first, size)
+        return pltpu.make_async_copy(next_ref.at[part], next_hbm.at[part], kept.at[index])
+
     annulus_step(
-        moves[:3], moves[3:], lambda node: saves[node].start(),
+        moves[:3], moves[3:], lambda node, value: None,
+        lambda first, size, index: save(first, size, index).start(),
         stride, first_order, win_ref, harmonic_ref, coefficient_ref, keycol_ref,
-        below_ref, above_ref, value_ref, previous_ref, force_ref, mass_ref, modes_ref,
-        next_ref, reaction_ref, terms_ref, added_ref,
-    )
-    finish(saves)
+        below_ref, above_ref, drift_ref, mass_ref, modes_ref,
+        next_ref, reaction_ref, terms_ref,
+    )
+    nodes = drift_ref.shape[0]
+    steps = -(-nodes // (2 * PAIRS))
+    finish(
+        [
+            save(2 * PAIRS * index, min(2 * PAIRS, nodes - 2 * PAIRS * index), index)
+            for index in range(steps)
+        ]
+    )
 
 
 def exchanged(low, high):
@@ -688,7 +718,7 @@
     messages, part, rank = call(
         functools.partial(group_kernel, mer_count, box_count),
         sent,
-        [((blocks, 8, per), f32, None), line + (HBM,), line + (HBM,)],
+        [((blocks, 8, per), f32, VMEM), line + (HBM,), line + (HBM,)],
         [line, line, line, ((8, box_nodes), f32)],
         copies=(9,),
         name="group",
@@ -701,6 +731,7 @@
     field = (volume, f32)
     table = (flat, f32)
     limits = ((1, elements), i32)
+    modes = element_modes.reshape(1, elements)
     side = ((columns, shared), f32)
     keys = [((1, depth), i32), ((depth, LANES), i32)]
     matrices = [((2 * rows, 8 * nodes), bf16)] * 2
@@ -708,7 +739,7 @@
     counts = ((blocks, LANES), f32)
     kept = [counts, counts, picked] + keys + matrices + [field, side, side]
     (
-        window, offset, filled, chosen, key, keycol, forward, backward, force, low, high,
+        window, offset, filled, chosen, key, keycol, forward, backward, drift, low, high,
     ) = call(
         functools.partial(start_kernel, elements),
         [
@@ -721,6 +752,9 @@
             far(annulus),
             far(radial_modulus),
             far(shear_modulus),
+            far(node_mass),
+            far(modes),
+            far(annulus_prev),
         ],
         [
             ((1, blocks), i32, None),
@@ -728,10 +762,10 @@
         + [shape + (HBM,) for shape in kept],
         [((1, count), i32)] * 2
         + [((1, shared), i32)] * 2
-        + [((nodes, nodes), f32), field, table, table]
+        + [((nodes, nodes), f32), field, table, table, table, limits, field]
         + kept
-        + [stack_scratch],
-        copies=(8, 10),
+        + [field, stack_scratch],
+        copies=(11, 10),
         name="start",
         flops=4 * columns * nodes * elements * (count + 2 * shared),
     )
@@ -758,31 +792,30 @@
     )
     samples = lax.all_gather(sample, "box")
 
-    modes = element_modes.reshape(1, elements)
-    fetched = keys[1:] + [side, side, field, field, field, table, limits]
+    fetched = keys[1:] + [side, side, field, table, limits]
     step_scratch = [
         ((columns, count), f32),
         ((2 * columns, depth), bf16),
-        field,
     ]
-    sample, box_now, current, force, low, high = call(
+    sample, box_now, drift, low, high = call(
         functools.partial(middle_kernel, stride),
         [
             box, window, landed(samples), near(node), near(harmonic),
-            far(keycol), anywhere(below), anywhere(above), far(annulus), far(annulus_prev), far(force),
-            far(node_mass), far(modes), far(key), far(forward), far(backward),
-            far(radial_modulus), far(shear_modulus),
+            far(keycol), anywhere(below), anywhere(above), far(drift), far(node_mass), far(modes),
+            far(annulus), far(key), far(forward), far(backward), far(radial_modulus),
+            far(shear_modulus),
         ],
         [(grid, f32, None), (grid, f32, VMEM)]
-        + [shape + (HBM,) for shape in (field, field, side, side)],
+        + [shape + (HBM,) for shape in (field, side, side)],
         fetched
+        + [field]
         + keys[:1]
         + matrices
         + [table, table, field, side, side]
         + [(grid, f32)]
         + step_scratch
-        + [stack_scratch, picked],
-        copies=(13, 4),
+        + [field, stack_scratch, picked],
+        copies=(12, 3),
         name="middle",
         flops=8 * columns * nodes * elements * (count + 2 * shared),
     )
@@ -793,7 +826,7 @@
     returned, coefficient = call(
         functools.partial(box_kernel, box_count),
         [box, landed(samples), near(node), near(box_now)],
-        [((mer_count, per) if direct else grid, f32, None), (grid, f32, VMEM)],
+        [((mer_count, per) if direct else grid, f32, VMEM), (grid, f32, VMEM)],
         [(grid, f32)] * direct,
         name="box",
     )
@@ -805,12 +838,12 @@
     (current,) = call(
         functools.partial(last_kernel, stride),
         [
-            box, window, near(coefficient), near(harmonic), far(keycol),
-            anywhere(below), anywhere(above), far(current), far(annulus), far(force), far(node_mass), far(modes),
+            box, window, near(coefficient), near(harmonic), far(keycol), anywhere(below),
+            anywhere(above), far(drift), far(node_mass), far(modes),
         ],
         [field + (HBM,)],
         fetched + [field] + step_scratch,
-        copies=(8, nodes),
+        copies=(6, -(-nodes // (2 * PAIRS))),
         name="last",
         flops=4 * columns * nodes * elements * (count + 2 * shared),
     )

time: 82.9 us -> 82.2 us (level)
  no operation moved by 1% of the time
where the time goes in v4:
time: 82.2 us; the launch traced here: 81.9 us
  Pallas kernels  44.7 us (54%)
  starting transfers between devices  25.7 us (31%)
  blocking collectives  10.7 us (13%)
    pallas_call x7, Pallas kernels, call(): pl.pallas_call(kernel, out_shape=[memory(shape, dtype) if memory else jax...  44.7 us
    ppermute x4, starting transfers between devices, exchanged(): return (lax.ppermute(high, 'mer', up), lax.ppermute(low, 'mer', down))  10.8 us
    all_gather x2, blocking collectives, per_device(): samples = lax.all_gather(sample, 'box')  10.7 us
    all_to_all x1, starting transfers between devices, per_device(): lax.all_to_all(returned, 'mer', split_axis=0, concat_axis=0, tiled=True)  7.63 us
    all_to_all x1, starting transfers between devices, per_device(): lax.all_to_all(messages, ('mer', 'box'), split_axis=0, concat_axis=0, til...  7.33 us
  transfers between devices with their start and end apart: 6, of which 0 were waited for; matrix products, arithmetic and copies ran while one was open for 0% of the time, Pallas kernels for 30%

profile of v4, /device:TPU:0, one launch (start us, length us, event | category | flops | bytes accessed | tf_op | source)
XLA Modules:
  0.0 81.9 jit_solution(12993918331199483415)
XLA Ops:
  0.6 2.2 %group.1 = (f32[32,8,128]{2,1,0:T(8,128)}, s32[1,1024]{1,0:T(1,128)}, s32[1,1024]{1,0:T(1,128)}) custom-call(s32[1,1024]{1,0:T(1,128)} %bitcast.23, f32[1,1024]{1,0:T(1,128)} %bitcast.24, f32[1,1024]{1,0:T(1,128)} %bitcast.25, f32[1,1024]{1,0:T(1,128)} %bitcast.26, f32[1,1024]{1,0:T(1,128)} %bitcast.27, f32[1,1024]{1,0:T(1,128)} %bitcast.28, f32[1,1024]{1,0:T(1,128)} %bitcast.29), custom_call_target="tpu_custom_call" | custom-call | tf_op jit(solution)/shard_map/group/pallas_call | solution.py:640
  2.9 7.3 %all-to-all-start = ((f32[32,8,128]{2,1,0:T(8,128)}), f32[32,8,128]{2,1,0:T(8,128)S(1)}, u32[]{:S(2)}, u32[]{:S(2)}) async-start(f32[32,8,128]{2,1,0:T(8,128)} %get-tuple-element.29), calls=%async_computation | async-start | bytes 262144 | tf_op jit(solution)/shard_map/all_to_all | solution.py:726
  10.2 10.5 %start.1 = (s32[1,32]{1,0:T(1,128)S(1)}, f32[32,128]{1,0:T(8,128)}, f32[32,128]{1,0:T(8,128)}, bf16[256,2048]{1,0:T(8,128)(2,1)}, s32[1,2560]{1,0:T(1,128)}, /*i...) custom-call(s32[1]{0:T(128)} %bitcast.box_ref, ...), custom_call_target="tpu_custom_call" | custom-call | flops 4194304000 | tf_op jit(solution)/shard_map/start/pallas_call | solution.py:640
  20.7 3.7 %collective-permute-start = (f32[128,256]{1,0:T(8,128)}, f32[128,256]{1,0:T(8,128)S(1)}, u32[]{:S(2)}, u32[]{:S(2)}) collective-permute-start(f32[128,256]{1,0:T(8,128)} %get-tuple-element.37), channel_id=1, source_target_pairs={{0,4},{4,8},{8,12},{12,16},{16,20},{20,24},{24,28},{1,5},{5,9},{9,... | collective-permute-start | bytes 393224 | tf_op jit(solution)/shard_map/ppermute | solution.py:629
  24.4 1.3 %collective-permute-start.1 = (f32[128,256]{1,0:T(8,128)}, f32[128,256]{1,0:T(8,128)S(1)}, u32[]{:S(2)}, u32[]{:S(2)}) collective-permute-start(f32[128,256]{1,0:T(8,128)} %get-tuple-element.38), channel_id=1, source_target_pairs={{4,0},{8,4},{12,8},{16,12},{20,16},{24,20},{28,24},{5,1},{9,5},{13... | collective-permute-start | bytes 393224 | tf_op jit(solution)/shard_map/ppermute | solution.py:629
  25.7 0.0 all-to-all-done.message_ref
  25.7 4.8 %nodes.1 = (f32[32,136,128]{2,1,0:T(8,128)S(1)}, f32[5,32,128]{2,1,0:T(8,128)S(1)}, f32[32,128]{1,0:T(8,128)S(1)}) custom-call(s32[1]{0:T(128)} %bitcast.box_ref, s32[1,32]{1,0:T(1,128)S(1)} %get-tuple-element.28.win_ref, f32[32,8,128]{2,1,0:T(8,128)S(1)} %all-to-all-done.message_ref, f32[32,128]{1,0:T(8,128)} %get-tuple-element.30.off_hbm, ...), custom_call_target="tpu_custom_call" | custom-call | flops 536870912 | tf_op jit(solution)/shard_map/nodes/pallas_call | solution.py:640
  30.5 5.4 %all-gather = f32[128,128]{1,0:T(8,128)S(1)} all-gather(f32[32,128]{1,0:T(8,128)S(1)} %get-tuple-element.33), channel_id=2, replica_groups=mesh['mer'=8,'box'=4] {'box'}, dimensions={0}, use_global_device_ids=true | all-gather | bytes 81920 | tf_op jit(solution)/shard_map/all_gather | solution.py:793
  35.9 0.0 collective-permute-done.below_hbm
  35.9 0.0 collective-permute-done.1.above_hbm
  35.9 17.3 %middle.1 = (f32[32,128]{1,0:T(8,128)S(1)}, f32[32,128]{1,0:T(8,128)S(1)}, f32[25,128,128]{2,1,0:T(8,128)}, f32[128,256]{1,0:T(8,128)}, f32[128,256]{1,0:T(8,128)}) custom-call(s32[1]{0:T(128)} %bitcast.box_ref, s32[1,32]{1,0:T(1,128)S(1)} %get-tuple-element.28.win_ref, f32[4,32,128]{2,1,0:T(8,128)S(1)} %bitcast.21, ...), custom_call_target="tpu_custom_call" | custom-call | flops 8388608000 | tf_op jit(solution)/shard_map/middle/pallas_call | solution.py:640
  53.2 4.5 %collective-permute-start.2 = (f32[128,256]{1,0:T(8,128)}, f32[128,256]{1,0:T(8,128)S(1)}, u32[]{:S(2)}, u32[]{:S(2)}) collective-permute-start(f32[128,256]{1,0:T(8,128)} %get-tuple-element.46), channel_id=1, source_target_pairs={{0,4},{4,8},{8,12},{12,16},{16,20},{20,24},{24,28},{1,5},{5,9},{9,... | collective-permute-start | bytes 393224 | tf_op jit(solution)/shard_map/ppermute | solution.py:629
  57.7 1.3 %collective-permute-start.3 = (f32[128,256]{1,0:T(8,128)}, f32[128,256]{1,0:T(8,128)S(1)}, u32[]{:S(2)}, u32[]{:S(2)}) collective-permute-start(f32[128,256]{1,0:T(8,128)} %get-tuple-element.47), channel_id=1, source_target_pairs={{4,0},{8,4},{12,8},{16,12},{20,16},{24,20},{28,24},{5,1},{9,5},{13... | collective-permute-start | bytes 393224 | tf_op jit(solution)/shard_map/ppermute | solution.py:629
  59.0 5.2 %all-gather.1 = f32[128,128]{1,0:T(8,128)S(1)} all-gather(f32[32,128]{1,0:T(8,128)S(1)} %get-tuple-element.43), channel_id=3, replica_groups=mesh['mer'=8,'box'=4] {'box'}, dimensions={0}, use_global_device_ids=true | all-gather | bytes 81920 | tf_op jit(solution)/shard_map/all_gather | solution.py:823
  64.3 0.6 box.1
  64.9 7.6 %all-to-all-start.1 = ((f32[8,1,128]{2,1,0:T(1,128)}), f32[8,1,128]{2,1,0:T(1,128)S(1)}, u32[]{:S(2)}, u32[]{:S(2)}) async-start(f32[8,1,128]{2,1,0:T(1,128)} %bitcast.16), calls=%async_computation.1 | async-start | bytes 8192 | tf_op jit(solution)/shard_map/all_to_all | solution.py:837
  72.5 0.0 collective-permute-done.2.below_hbm
  72.5 0.0 collective-permute-done.3.above_hbm
  72.5 0.0 copy-start
  72.5 0.0 copy-start.1
  72.5 8.5 %last.1 = f32[25,128,128]{2,1,0:T(8,128)} custom-call(s32[1]{0:T(128)} %bitcast.box_ref, s32[1,32]{1,0:T(1,128)S(1)} %get-tuple-element.28.win_ref, f32[32,128]{1,0:T(8,128)S(1)} %get-tuple-element.45.coefficient_ref, f32[32,136,128]{2,1,0:T(8,128)S(1)} %get-tuple-element.35.harmonic_ref, s32[2560,128]{1,0:T(8,128)} %get-tuple-element.36.keycol_hbm, ...), custom_call_target="tpu_custom_call" | custom-call | flops 4194304000 | tf_op jit(solution)/shard_map/last/pallas_call | solution.py:640
  81.1 0.0 all-to-all-done.1
  81.1 0.0 copy-done
  81.1 0.0 copy-done.1
  81.1 0.8 ungroup.1
Async XLA Ops:
  2.9 22.8 %all-to-all-start = ((f32[32,8,128]{2,1,0:T(8,128)}), f32[32,8,128]{2,1,0:T(8,128)S(1)}, u32[]{:S(2)}, u32[]{:S(2)}) async-start(f32[32,8,128]{2,1,0:T(8,128)} %get-tuple-element.29), calls=%async_computation | async-start | bytes 262144 | tf_op jit(solution)/shard_map/all_to_all | solution.py:726
  20.7 15.2 %collective-permute-start = (f32[128,256]{1,0:T(8,128)}, f32[128,256]{1,0:T(8,128)S(1)}, u32[]{:S(2)}, u32[]{:S(2)}) collective-permute-start(f32[128,256]{1,0:T(8,128)} %get-tuple-element.37), channel_id=1, source_target_pairs={{0,4},{4,8},{8,12},{12,16},{16,20},{20,24},{24,28},{1,5},{5,9},{9,... | collective-permute-start | bytes 393224 | tf_op jit(solution)/shard_map/ppermute | solution.py:629
  24.4 11.5 %collective-permute-start.1 = (f32[128,256]{1,0:T(8,128)}, f32[128,256]{1,0:T(8,128)S(1)}, u32[]{:S(2)}, u32[]{:S(2)}) collective-permute-start(f32[128,256]{1,0:T(8,128)} %get-tuple-element.38), channel_id=1, source_target_pairs={{4,0},{8,4},{12,8},{16,12},{20,16},{24,20},{28,24},{5,1},{9,5},{13... | collective-permute-start | bytes 393224 | tf_op jit(solution)/shard_map/ppermute | solution.py:629
  53.2 19.3 %collective-permute-start.2 = (f32[128,256]{1,0:T(8,128)}, f32[128,256]{1,0:T(8,128)S(1)}, u32[]{:S(2)}, u32[]{:S(2)}) collective-permute-start(f32[128,256]{1,0:T(8,128)} %get-tuple-element.46), channel_id=1, source_target_pairs={{0,4},{4,8},{8,12},{12,16},{16,20},{20,24},{24,28},{1,5},{5,9},{9,... | collective-permute-start | bytes 393224 | tf_op jit(solution)/shard_map/ppermute | solution.py:629
  57.7 14.8 %collective-permute-start.3 = (f32[128,256]{1,0:T(8,128)}, f32[128,256]{1,0:T(8,128)S(1)}, u32[]{:S(2)}, u32[]{:S(2)}) collective-permute-start(f32[128,256]{1,0:T(8,128)} %get-tuple-element.47), channel_id=1, source_target_pairs={{4,0},{8,4},{12,8},{16,12},{20,16},{24,20},{28,24},{5,1},{9,5},{13... | collective-permute-start | bytes 393224 | tf_op jit(solution)/shard_map/ppermute | solution.py:629
  64.9 16.2 %all-to-all-start.1 = ((f32[8,1,128]{2,1,0:T(1,128)}), f32[8,1,128]{2,1,0:T(1,128)S(1)}, u32[]{:S(2)}, u32[]{:S(2)}) async-start(f32[8,1,128]{2,1,0:T(1,128)} %bitcast.16), calls=%async_computation.1 | async-start | bytes 8192 | tf_op jit(solution)/shard_map/all_to_all | solution.py:837
  72.5 8.6 %copy-start = (s32[1,1024]{1,0:T(1,128)S(1)}, s32[1,1024]{1,0:T(1,128)}, u32[]{:S(2)}) copy-start(s32[1,1024]{1,0:T(1,128)} %get-tuple-element.51.part_ref) | copy-start | bytes 12292
  72.5 8.6 %copy-start.1 = (s32[1,1024]{1,0:T(1,128)S(1)}, s32[1,1024]{1,0:T(1,128)}, u32[]{:S(2)}) copy-start(s32[1,1024]{1,0:T(1,128)} %get-tuple-element.52.rank_ref) | copy-start | bytes 12292

commit v5 on v4

--- a/solution.py
+++ b/solution.py
@@ -198,20 +198,21 @@
 
 def pick_rows(stack_ref, key_ref, out_ref):
     def body(index, carry):
-        for part in range(4):
-            start = pl.multiple_of((4 * index + part) * WIDE, WIDE)
+        for part in range(8):
+            start = pl.multiple_of((8 * index + part) * WIDE, WIDE)
             out_ref[:, pl.ds(start, WIDE)] = picked(stack_ref, key_ref, start).astype(bf16)
         return carry
 
-    lax.fori_loop(0, out_ref.shape[1] // (4 * WIDE), body, 0)
-
-
-def pick_boundary(stack_ref, key_ref, low_ref, high_ref):
+    lax.fori_loop(0, out_ref.shape[1] // (8 * WIDE), body, 0)
+
+
+def pick_boundary(stack_ref, key_ref, low_ref, high_ref, saves):
     shared = low_ref.shape[1]
     first = key_ref.shape[1] - 2 * shared
-    for ref, origin in ((low_ref, first), (high_ref, first + shared)):
+    for ref, origin, save in ((low_ref, first, saves[0]), (high_ref, first + shared, saves[1])):
         for start in range(0, shared, WIDE):
             ref[:, start : start + WIDE] = folded(picked(stack_ref, key_ref, origin + start))
+        save.start()
 
 
 def spread(derivative_ref, transposed, rows):
@@ -340,8 +341,7 @@
     )
     begin(saves[7:8])
     fill_stack(force_ref, stack_ref)
-    pick_boundary(stack_ref, key_ref, low_ref, high_ref)
-    begin(saves[8:])
+    pick_boundary(stack_ref, key_ref, low_ref, high_ref, saves[8:])
     finish(saves)
 
 
@@ -570,8 +570,7 @@
     )
     begin(saves[:1])
     fill_stack(force_ref, stack_ref)
-    pick_boundary(stack_ref, key_ref, low_ref, high_ref)
-    begin(saves[1:])
+    pick_boundary(stack_ref, key_ref, low_ref, high_ref, saves[1:])
     sample_into(win_ref, harmonic_ref, picked_ref, stride, sample_ref)
     finish(saves)
 

time: 82.2 us -> 82 us (level)
  no operation moved by 1% of the time
where the time goes in v5:
time: 82 us; the launch traced here: 81.6 us
  Pallas kernels  44.4 us (54%)
  starting transfers between devices  25.7 us (31%)
  blocking collectives  10.7 us (13%)
    pallas_call x7, Pallas kernels, call(): pl.pallas_call(kernel, out_shape=[memory(shape, dtype) if memory else jax...  44.4 us
    ppermute x4, starting transfers between devices, exchanged(): return (lax.ppermute(high, 'mer', up), lax.ppermute(low, 'mer', down))  10.8 us
    all_gather x2, blocking collectives, per_device(): samples = lax.all_gather(sample, 'box')  10.7 us
    all_to_all x1, starting transfers between devices, per_device(): lax.all_to_all(returned, 'mer', split_axis=0, concat_axis=0, tiled=True)  7.6 us
    all_to_all x1, starting transfers between devices, per_device(): lax.all_to_all(messages, ('mer', 'box'), split_axis=0, concat_axis=0, til...  7.33 us
  transfers between devices with their start and end apart: 6, of which 0 were waited for; matrix products, arithmetic and copies ran while one was open for 0% of the time, Pallas kernels for 30%

profile of v5, /device:TPU:0, one launch (start us, length us, event | category | flops | bytes accessed | tf_op | source)
XLA Modules:
  0.0 81.6 jit_solution(8405975568767101822)
XLA Ops:
  0.6 2.2 %group.1 = (f32[32,8,128]{2,1,0:T(8,128)}, s32[1,1024]{1,0:T(1,128)}, s32[1,1024]{1,0:T(1,128)}) custom-call(s32[1,1024]{1,0:T(1,128)} %bitcast.23, f32[1,1024]{1,0:T(1,128)} %bitcast.24, f32[1,1024]{1,0:T(1,128)} %bitcast.25, f32[1,1024]{1,0:T(1,128)} %bitcast.26, f32[1,1024]{1,0:T(1,128)} %bitcast.27, f32[1,1024]{1,0:T(1,128)} %bitcast.28, f32[1,1024]{1,0:T(1,128)} %bitcast.29), custom_call_target="tpu_custom_call" | custom-call | tf_op jit(solution)/shard_map/group/pallas_call | solution.py:639
  2.9 7.3 %all-to-all-start = ((f32[32,8,128]{2,1,0:T(8,128)}), f32[32,8,128]{2,1,0:T(8,128)S(1)}, u32[]{:S(2)}, u32[]{:S(2)}) async-start(f32[32,8,128]{2,1,0:T(8,128)} %get-tuple-element.29), calls=%async_computation | async-start | bytes 262144 | tf_op jit(solution)/shard_map/all_to_all | solution.py:725
  10.2 10.4 %start.1 = (s32[1,32]{1,0:T(1,128)S(1)}, f32[32,128]{1,0:T(8,128)}, f32[32,128]{1,0:T(8,128)}, bf16[256,2048]{1,0:T(8,128)(2,1)}, s32[1,2560]{1,0:T(1,128)}, /*i...) custom-call(s32[1]{0:T(128)} %bitcast.box_ref, ...), custom_call_target="tpu_custom_call" | custom-call | flops 4194304000 | tf_op jit(solution)/shard_map/start/pallas_call | solution.py:639
  20.6 3.7 %collective-permute-start = (f32[128,256]{1,0:T(8,128)}, f32[128,256]{1,0:T(8,128)S(1)}, u32[]{:S(2)}, u32[]{:S(2)}) collective-permute-start(f32[128,256]{1,0:T(8,128)} %get-tuple-element.37), channel_id=1, source_target_pairs={{0,4},{4,8},{8,12},{12,16},{16,20},{20,24},{24,28},{1,5},{5,9},{9,... | collective-permute-start | bytes 393224 | tf_op jit(solution)/shard_map/ppermute | solution.py:628
  24.3 1.3 %collective-permute-start.1 = (f32[128,256]{1,0:T(8,128)}, f32[128,256]{1,0:T(8,128)S(1)}, u32[]{:S(2)}, u32[]{:S(2)}) collective-permute-start(f32[128,256]{1,0:T(8,128)} %get-tuple-element.38), channel_id=1, source_target_pairs={{4,0},{8,4},{12,8},{16,12},{20,16},{24,20},{28,24},{5,1},{9,5},{13... | collective-permute-start | bytes 393224 | tf_op jit(solution)/shard_map/ppermute | solution.py:628
  25.6 0.0 all-to-all-done.message_ref
  25.6 4.8 %nodes.1 = (f32[32,136,128]{2,1,0:T(8,128)S(1)}, f32[5,32,128]{2,1,0:T(8,128)S(1)}, f32[32,128]{1,0:T(8,128)S(1)}) custom-call(s32[1]{0:T(128)} %bitcast.box_ref, s32[1,32]{1,0:T(1,128)S(1)} %get-tuple-element.28.win_ref, f32[32,8,128]{2,1,0:T(8,128)S(1)} %all-to-all-done.message_ref, f32[32,128]{1,0:T(8,128)} %get-tuple-element.30.off_hbm, ...), custom_call_target="tpu_custom_call" | custom-call | flops 536870912 | tf_op jit(solution)/shard_map/nodes/pallas_call | solution.py:639
  30.4 5.4 %all-gather = f32[128,128]{1,0:T(8,128)S(1)} all-gather(f32[32,128]{1,0:T(8,128)S(1)} %get-tuple-element.33), channel_id=2, replica_groups=mesh['mer'=8,'box'=4] {'box'}, dimensions={0}, use_global_device_ids=true | all-gather | bytes 81920 | tf_op jit(solution)/shard_map/all_gather | solution.py:792
  35.8 0.0 collective-permute-done.below_hbm
  35.8 0.0 collective-permute-done.1.above_hbm
  35.8 17.2 %middle.1 = (f32[32,128]{1,0:T(8,128)S(1)}, f32[32,128]{1,0:T(8,128)S(1)}, f32[25,128,128]{2,1,0:T(8,128)}, f32[128,256]{1,0:T(8,128)}, f32[128,256]{1,0:T(8,128)}) custom-call(s32[1]{0:T(128)} %bitcast.box_ref, s32[1,32]{1,0:T(1,128)S(1)} %get-tuple-element.28.win_ref, f32[4,32,128]{2,1,0:T(8,128)S(1)} %bitcast.21, ...), custom_call_target="tpu_custom_call" | custom-call | flops 8388608000 | tf_op jit(solution)/shard_map/middle/pallas_call | solution.py:639
  52.9 4.5 %collective-permute-start.2 = (f32[128,256]{1,0:T(8,128)}, f32[128,256]{1,0:T(8,128)S(1)}, u32[]{:S(2)}, u32[]{:S(2)}) collective-permute-start(f32[128,256]{1,0:T(8,128)} %get-tuple-element.46), channel_id=1, source_target_pairs={{0,4},{4,8},{8,12},{12,16},{16,20},{20,24},{24,28},{1,5},{5,9},{9,... | collective-permute-start | bytes 393224 | tf_op jit(solution)/shard_map/ppermute | solution.py:628
  57.5 1.3 %collective-permute-start.3 = (f32[128,256]{1,0:T(8,128)}, f32[128,256]{1,0:T(8,128)S(1)}, u32[]{:S(2)}, u32[]{:S(2)}) collective-permute-start(f32[128,256]{1,0:T(8,128)} %get-tuple-element.47), channel_id=1, source_target_pairs={{4,0},{8,4},{12,8},{16,12},{20,16},{24,20},{28,24},{5,1},{9,5},{13... | collective-permute-start | bytes 393224 | tf_op jit(solution)/shard_map/ppermute | solution.py:628
  58.8 5.2 %all-gather.1 = f32[128,128]{1,0:T(8,128)S(1)} all-gather(f32[32,128]{1,0:T(8,128)S(1)} %get-tuple-element.43), channel_id=3, replica_groups=mesh['mer'=8,'box'=4] {'box'}, dimensions={0}, use_global_device_ids=true | all-gather | bytes 81920 | tf_op jit(solution)/shard_map/all_gather | solution.py:822
  64.0 0.6 box.1
  64.6 7.6 %all-to-all-start.1 = ((f32[8,1,128]{2,1,0:T(1,128)}), f32[8,1,128]{2,1,0:T(1,128)S(1)}, u32[]{:S(2)}, u32[]{:S(2)}) async-start(f32[8,1,128]{2,1,0:T(1,128)} %bitcast.16), calls=%async_computation.1 | async-start | bytes 8192 | tf_op jit(solution)/shard_map/all_to_all | solution.py:836
  72.2 0.0 collective-permute-done.2.below_hbm
  72.2 0.0 collective-permute-done.3.above_hbm
  72.2 0.0 copy-start
  72.3 0.0 copy-start.1
  72.3 8.5 %last.1 = f32[25,128,128]{2,1,0:T(8,128)} custom-call(s32[1]{0:T(128)} %bitcast.box_ref, s32[1,32]{1,0:T(1,128)S(1)} %get-tuple-element.28.win_ref, f32[32,128]{1,0:T(8,128)S(1)} %get-tuple-element.45.coefficient_ref, f32[32,136,128]{2,1,0:T(8,128)S(1)} %get-tuple-element.35.harmonic_ref, s32[2560,128]{1,0:T(8,128)} %get-tuple-element.36.keycol_hbm, ...), custom_call_target="tpu_custom_call" | custom-call | flops 4194304000 | tf_op jit(solution)/shard_map/last/pallas_call | solution.py:639
  80.8 0.0 all-to-all-done.1
  80.8 0.0 copy-done
  80.8 0.0 copy-done.1
  80.8 0.8 ungroup.1
Async XLA Ops:
  2.9 22.7 %all-to-all-start = ((f32[32,8,128]{2,1,0:T(8,128)}), f32[32,8,128]{2,1,0:T(8,128)S(1)}, u32[]{:S(2)}, u32[]{:S(2)}) async-start(f32[32,8,128]{2,1,0:T(8,128)} %get-tuple-element.29), calls=%async_computation | async-start | bytes 262144 | tf_op jit(solution)/shard_map/all_to_all | solution.py:725
  20.6 15.2 %collective-permute-start = (f32[128,256]{1,0:T(8,128)}, f32[128,256]{1,0:T(8,128)S(1)}, u32[]{:S(2)}, u32[]{:S(2)}) collective-permute-start(f32[128,256]{1,0:T(8,128)} %get-tuple-element.37), channel_id=1, source_target_pairs={{0,4},{4,8},{8,12},{12,16},{16,20},{20,24},{24,28},{1,5},{5,9},{9,... | collective-permute-start | bytes 393224 | tf_op jit(solution)/shard_map/ppermute | solution.py:628
  24.3 11.5 %collective-permute-start.1 = (f32[128,256]{1,0:T(8,128)}, f32[128,256]{1,0:T(8,128)S(1)}, u32[]{:S(2)}, u32[]{:S(2)}) collective-permute-start(f32[128,256]{1,0:T(8,128)} %get-tuple-element.38), channel_id=1, source_target_pairs={{4,0},{8,4},{12,8},{16,12},{20,16},{24,20},{28,24},{5,1},{9,5},{13... | collective-permute-start | bytes 393224 | tf_op jit(solution)/shard_map/ppermute | solution.py:628
  52.9 19.3 %collective-permute-start.2 = (f32[128,256]{1,0:T(8,128)}, f32[128,256]{1,0:T(8,128)S(1)}, u32[]{:S(2)}, u32[]{:S(2)}) collective-permute-start(f32[128,256]{1,0:T(8,128)} %get-tuple-element.46), channel_id=1, source_target_pairs={{0,4},{4,8},{8,12},{12,16},{16,20},{20,24},{24,28},{1,5},{5,9},{9,... | collective-permute-start | bytes 393224 | tf_op jit(solution)/shard_map/ppermute | solution.py:628
  57.5 14.8 %collective-permute-start.3 = (f32[128,256]{1,0:T(8,128)}, f32[128,256]{1,0:T(8,128)S(1)}, u32[]{:S(2)}, u32[]{:S(2)}) collective-permute-start(f32[128,256]{1,0:T(8,128)} %get-tuple-element.47), channel_id=1, source_target_pairs={{4,0},{8,4},{12,8},{16,12},{20,16},{24,20},{28,24},{5,1},{9,5},{13... | collective-permute-start | bytes 393224 | tf_op jit(solution)/shard_map/ppermute | solution.py:628
  64.6 16.2 %all-to-all-start.1 = ((f32[8,1,128]{2,1,0:T(1,128)}), f32[8,1,128]{2,1,0:T(1,128)S(1)}, u32[]{:S(2)}, u32[]{:S(2)}) async-start(f32[8,1,128]{2,1,0:T(1,128)} %bitcast.16), calls=%async_computation.1 | async-start | bytes 8192 | tf_op jit(solution)/shard_map/all_to_all | solution.py:836
  72.2 8.5 %copy-start = (s32[1,1024]{1,0:T(1,128)S(1)}, s32[1,1024]{1,0:T(1,128)}, u32[]{:S(2)}) copy-start(s32[1,1024]{1,0:T(1,128)} %get-tuple-element.51.part_ref) | copy-start | bytes 12292
  72.3 8.5 %copy-start.1 = (s32[1,1024]{1,0:T(1,128)S(1)}, s32[1,1024]{1,0:T(1,128)}, u32[]{:S(2)}) copy-start(s32[1,1024]{1,0:T(1,128)} %get-tuple-element.52.rank_ref) | copy-start | bytes 12292
